TPU v7x, 32 devices: a whole 2x2x4 slice. The times are simulated.
32 devices in a mesh: dp: 2 (over x), ctx: 4 (over y, core), head: 4 (over z).
Axes of the slice: x: 2, y: 2, z: 4, core: 2. Of those that a mesh axis runs over, the one named last changes fastest.
Arguments:
- inputs: bfloat16 [2, 8, 512, 1536], P('dp', 'ctx', 'head'), may hold values from -6 to 6
- block_order: int32 [2, 8], P('dp'), may hold values from 0 to 7, each once within a row
- mixer_gain: float32 [1536], replicated, may hold values from 0.5 to 1.5
- query_weight: bfloat16 [1536, 1536], P(None, 'head'), may hold values from -0.15625 to 0.15625
- key_weight: bfloat16 [1536, 1536], P(None, 'head'), may hold values from -0.15625 to 0.15625
- value_weight: bfloat16 [1536, 1536], P(None, 'head'), may hold values from -0.15625 to 0.15625
- lambda_qone: float32 [12, 64], P('head'), may hold values from -0.6 to 0.6
- lambda_kone: float32 [12, 64], P('head'), may hold values from -0.6 to 0.6
- lambda_qtwo: float32 [12, 64], P('head'), may hold values from -0.6 to 0.6
- lambda_ktwo: float32 [12, 64], P('head'), may hold values from -0.6 to 0.6
- group_gain: float32 [1536], P('head'), may hold values from 0.5 to 1.5
- output_weight: bfloat16 [1536, 1536], P('head'), may hold values from -0.625 to 0.625
- feed_gain: float32 [1536], replicated, may hold values from 0.5 to 1.5
- gate_weight: bfloat16 [1536, 4096], P(None, 'head'), may hold values from -0.15625 to 0.15625
- up_weight: bfloat16 [1536, 4096], P(None, 'head'), may hold values from -0.15625 to 0.15625
- down_weight: bfloat16 [4096, 1536], P('head'), may hold values from -0.1875 to 0.1875
- cotangent: bfloat16 [2, 8, 512, 1536], P('dp', 'ctx', 'head'), may hold values from -6 to 6
Outputs:
- block_out: bfloat16 [2, 8, 512, 1536], P('dp', 'ctx', 'head')
- input_grad: float32 [2, 8, 512, 1536], P('dp', 'ctx', 'head')
- mixer_grad: float32 [1536], replicated
- query_grad: float32 [1536, 1536], P(('dp', 'ctx'), 'head')
- key_grad: float32 [1536, 1536], P(('dp', 'ctx'), 'head')
- value_grad: float32 [1536, 1536], P(('dp', 'ctx'), 'head')
- qone_grad: float32 [12, 64], P('head')
- kone_grad: float32 [12, 64], P('head')
- qtwo_grad: float32 [12, 64], P('head')
- ktwo_grad: float32 [12, 64], P('head')
- group_grad: float32 [1536], P('head')
- output_grad: float32 [1536, 1536], P('head', ('dp', 'ctx'))
- feed_grad: float32 [1536], replicated
- gate_grad: float32 [1536, 4096], P(('dp', 'ctx'), 'head')
- up_grad: float32 [1536, 4096], P(('dp', 'ctx'), 'head')
- down_grad: float32 [4096, 1536], P('head', ('dp', 'ctx'))
Inputs may be any that keep to these rules, and one draw needn't show every extreme that they name: `block_order`: row s lists, for each of the 8 slots of sequence s, which of its 8 blocks of 512 consecutive positions that slot holds; each block once.
All inputs are finite; a program needn't handle non-finite values.
Results may differ from a plain program's by a relative error of at most 0.023.
Values may be sent and summed in bfloat16 or wider, within the bound.
A program may use at most 192 MiB of HBM per device.

v0:
```python
from functools import partial
import math

import jax
import jax.numpy as jnp
from jax import lax
from jax.experimental import pallas as pl
from jax.experimental.pallas import tpu as pltpu
from jax.sharding import PartitionSpec as P

EPSILON = 1e-05
LAMBDA_INIT = 0.8 - 0.6 * math.exp(-0.3 * 12)
SHRINK = 1.0 - LAMBDA_INIT
THETA = 10000.0
NEGATIVE = -1e30
F32 = jnp.float32
BF16 = jnp.bfloat16


def rms_scale(value_rows):
    return lax.rsqrt(jnp.mean(value_rows * value_rows, axis=-1, keepdims=True) + EPSILON)


def norm_back(grad_in, value_rows, scale, gain):
    upstream = grad_in * gain
    return scale * upstream - value_rows * scale**3 * jnp.mean(
        upstream * value_rows, axis=-1, keepdims=True
    )


def rotate(tensor, places, direction):
    half_dim = tensor.shape[-1] // 2
    frequency = THETA ** (-jnp.arange(half_dim, dtype=jnp.float32) / half_dim)
    angles = places.astype(jnp.float32)[..., None] * frequency
    angles = angles.reshape(places.shape + (1,) * (tensor.ndim - places.ndim - 1) + (half_dim,))
    cosine = jnp.cos(angles)
    sine_part = jnp.sin(angles) * direction
    leading = tensor[..., :half_dim]
    trailing = tensor[..., half_dim:]
    return jnp.concatenate(
        [leading * cosine - trailing * sine_part, leading * sine_part + trailing * cosine], axis=-1
    )


def contract_rows(left, right):
    return lax.dot_general(
        left, right, (((0,), (0,)), ((), ())), preferred_element_type=jnp.float32
    )


def contract_cols(left, right):
    return lax.dot_general(
        left, right, (((1,), (1,)), ((), ())), preferred_element_type=jnp.float32
    )


def dot(left, right):
    return lax.dot_general(left, right, (((1,), (0,)), ((), ())), preferred_element_type=F32)


def offsets_of(part, parts, strip, axis, shape):
    index = lax.broadcasted_iota(jnp.int32, shape, axis)
    return (index // strip) * (parts * strip) + part * strip + index % strip


def block_diag_cols(turned, half, lanes):
    row = lax.broadcasted_iota(jnp.int32, (turned.shape[0], lanes), 0)
    zero = jnp.zeros_like(turned)
    return jnp.concatenate(
        [jnp.where(row < half, turned, zero), jnp.where(row >= half, turned, zero)], axis=1
    )


def attend_kernel(dims, slot_ref, part_ref, lam_ref, q_ref, k_ref, v_ref, gain_ref,
                  grouped_ref, mixed_ref, second_ref, lse_ref, vt_ref, qbd_ref, acc_ref):
    slots, parts, heads, tile, width, strip = dims
    half = width // 2
    cols = 2 * tile

    def turn(slot, carry):
        for h in range(heads):
            for c in range(parts):
                vt_ref[h, slot, :, c * tile:(c + 1) * tile] = jnp.transpose(
                    v_ref[c, slot, :, h * width:(h + 1) * width])
        return carry

    lax.fori_loop(0, slots, turn, 0)
    query_off = offsets_of(part_ref[0], parts, strip, 1, (1, tile))
    query_off = jnp.concatenate([query_off, query_off], axis=1)

    def one_block(slot, diag, state):
        out = []
        for h in range(heads):
            peak, total = state[2 * h], state[2 * h + 1]
            scores = []
            for c in range(parts):
                s = dot(k_ref[c, slot, :, h * width:(h + 1) * width], qbd_ref[h])
                if diag:
                    key_off = offsets_of(c, parts, strip, 0, (tile, 1))
                    s = jnp.where(key_off <= query_off, s, NEGATIVE)
                scores.append(s)
            top = scores[0]
            for s in scores[1:]:
                top = jnp.maximum(top, s)
            higher = jnp.maximum(peak, jnp.max(top, axis=0, keepdims=True))
            keep = jnp.exp(peak - higher)
            weights = [jnp.exp(s - higher) for s in scores]
            added = weights[0]
            for w in weights[1:]:
                added = added + w
            total = total * keep + jnp.sum(added, axis=0, keepdims=True)
            low = jnp.concatenate([w.astype(BF16) for w in weights], axis=0)
            acc_ref[h] = acc_ref[h] * keep + dot(vt_ref[h, slot], low)
            out += [higher, total]
        return tuple(out)

    def one_place(place, carry):
        own = slot_ref[place]
        for h in range(heads):
            turned = jnp.transpose(q_ref[own, :, h * width:(h + 1) * width])
            turned = turned * jnp.asarray(half ** -0.5, turned.dtype)
            qbd_ref[h] = block_diag_cols(turned, half, tile)
            acc_ref[h] = jnp.zeros((width, cols), F32)
        state = (jnp.full((1, cols), NEGATIVE, F32), jnp.zeros((1, cols), F32)) * heads
        state = one_block(own, True, state)
        state = lax.fori_loop(
            0, place, lambda j, st: one_block(slot_ref[j], False, st), state)
        for h in range(heads):
            peak, total = state[2 * h], state[2 * h + 1]
            result = acc_ref[h] / total
            second = result[:, tile:]
            mixed = result[:, :tile] - lam_ref[h] * second
            scale = lax.rsqrt(jnp.mean(mixed * mixed, axis=0, keepdims=True) + EPSILON)
            gain = gain_ref[h * width:(h + 1) * width, :] * SHRINK
            grouped = (mixed * scale * gain).astype(BF16)
            grouped_ref[own, :, h * width:(h + 1) * width] = jnp.transpose(grouped)
            mixed_ref[own, h] = mixed
            second_ref[own, h] = second
            lse_ref[own, h] = peak + jnp.log(total)
        return carry

    lax.fori_loop(0, slots, one_place, 0)


def attend_back_kernel(dims, slot_ref, part_ref, lam_ref, q_ref, k_ref, v_ref, gg_ref, gain_ref,
                       mixed_ref, second_ref, lse_ref,
                       dq_ref, dk_ref, dv_ref, gpart_ref, lpart_ref,
                       kt_ref, qbdt_ref, qbd_ref, gt_ref, g_ref, delta_ref, dqt_ref,
                       dka_ref, dva_ref):
    slots, parts, heads, tile, width, strip = dims
    half = width // 2
    scale = half ** -0.5

    def turn(slot, carry):
        for h in range(heads):
            for c in range(parts):
                kt_ref[h, slot, :, c * tile:(c + 1) * tile] = jnp.transpose(
                    k_ref[c, slot, :, h * width:(h + 1) * width])
        return carry

    lax.fori_loop(0, slots, turn, 0)
    gpart_ref[...] = jnp.zeros_like(gpart_ref)
    lpart_ref[...] = jnp.zeros_like(lpart_ref)
    query_off = offsets_of(part_ref[0], parts, strip, 1, (1, tile))
    query_off = jnp.concatenate([query_off, query_off], axis=1)

    def one_block(own, slot, diag):
        for h in range(heads):
            lse = lse_ref[own, h]
            delta = delta_ref[h]
            lanes = slice(h * width, (h + 1) * width)
            turned = []
            for c in range(parts):
                keys = k_ref[c, slot, :, lanes]
                s = dot(keys, qbdt_ref[h])
                if diag:
                    key_off = offsets_of(c, parts, strip, 0, (tile, 1))
                    s = jnp.where(key_off <= query_off, s, NEGATIVE)
                weights = jnp.exp(s - lse)
                probs = dot(v_ref[c, slot, :, lanes], gt_ref[h])
                ds = (weights * (probs - delta)).astype(BF16)
                dv = dot(weights.astype(BF16), g_ref[h])
                dk = dot(ds, qbd_ref[h])
                if diag:
                    dva_ref[h, slot, c] = dv
                    dka_ref[h, slot, c] = dk
                else:
                    dva_ref[h, slot, c] += dv
                    dka_ref[h, slot, c] += dk
                turned.append(ds)
            dq = dot(kt_ref[h, slot], jnp.concatenate(turned, axis=0))
            dqt_ref[h, :half] += dq[:half, :tile]
            dqt_ref[h, half:] += dq[half:, tile:]

    def one_place(place, carry):
        own = slot_ref[place]
        for h in range(heads):
            lanes = slice(h * width, (h + 1) * width)
            lam = lam_ref[h]
            start = pl.multiple_of(own * tile, tile)
            grad = gg_ref[lanes, pl.ds(start, tile)]
            mixed = mixed_ref[own, h]
            second = second_ref[own, h]
            rg = lax.rsqrt(jnp.mean(mixed * mixed, axis=0, keepdims=True) + EPSILON)
            gpart_ref[lanes, :] += grad * (mixed * rg)
            up = grad * (gain_ref[lanes, :] * SHRINK)
            gm = rg * up - mixed * (rg * rg * rg * jnp.mean(up * mixed, axis=0, keepdims=True))
            lpart_ref[h] -= gm * second
            along = jnp.sum(gm * second, axis=0, keepdims=True)
            first = jnp.sum(gm * mixed, axis=0, keepdims=True) + lam * along
            delta_ref[h] = jnp.concatenate([first, -lam * along], axis=1)
            both = jnp.concatenate([gm, -lam * gm], axis=1)
            gt_ref[h] = both.astype(BF16)
            g_ref[h] = jnp.transpose(both).astype(BF16)
            query = q_ref[own, :, lanes]
            query = query * jnp.asarray(scale, query.dtype)
            qbdt_ref[h] = block_diag_cols(jnp.transpose(query), half, tile)
            lane = lax.broadcasted_iota(jnp.int32, (tile, width), 1)
            zero = jnp.zeros_like(query)
            qbd_ref[h, :tile] = jnp.where(lane < half, query, zero)
            qbd_ref[h, tile:] = jnp.where(lane >= half, query, zero)
            dqt_ref[h] = jnp.zeros((width, tile), F32)
        one_block(own, own, True)

        def rest(j, c):
            one_block(own, slot_ref[j], False)
            return c

        lax.fori_loop(0, place, rest, 0)
        for h in range(heads):
            dq_ref[own, :, h * width:(h + 1) * width] = jnp.transpose(dqt_ref[h] * scale)
        return carry

    lax.fori_loop(0, slots, one_place, 0)

    def put(slot, carry):
        for h in range(heads):
            lanes = slice(h * width, (h + 1) * width)
            for c in range(parts):
                dk_ref[c, slot, :, lanes] = dka_ref[h, slot, c].astype(BF16)
                dv_ref[c, slot, :, lanes] = dva_ref[h, slot, c].astype(BF16)
        return carry

    lax.fori_loop(0, slots, put, 0)


def specs(count, smem):
    return [pl.BlockSpec(memory_space=pltpu.SMEM)] * smem + [
        pl.BlockSpec(memory_space=pltpu.VMEM)] * (count - smem)


def attend(dims, slot_of, part, lam, queries, keys_all, values_all, gain):
    slots, parts, heads, tile, width, strip = dims
    return pl.pallas_call(
        partial(attend_kernel, dims),
        out_shape=(
            jax.ShapeDtypeStruct((slots, tile, heads * width), BF16),
            jax.ShapeDtypeStruct((slots, heads, width, tile), F32),
            jax.ShapeDtypeStruct((slots, heads, width, tile), F32),
            jax.ShapeDtypeStruct((slots, heads, 1, 2 * tile), F32),
        ),
        in_specs=specs(7, 3),
        out_specs=specs(4, 0),
        scratch_shapes=[
            pltpu.VMEM((heads, slots, width, parts * tile), BF16),
            pltpu.VMEM((heads, width, 2 * tile), BF16),
            pltpu.VMEM((heads, width, 2 * tile), F32),
        ],
        compiler_params=pltpu.CompilerParams(vmem_limit_bytes=48 << 20),
        cost_estimate=pl.CostEstimate(
            flops=20_000_000_000, bytes_accessed=12_000_000, transcendentals=14_000_000),
        name="attend",
    )(slot_of, part, lam, queries, keys_all, values_all, gain)


def attend_back(dims, slot_of, part, lam, queries, keys_all, values_all, gg, gain, mixed, second, lse):
    slots, parts, heads, tile, width, strip = dims
    full = heads * width
    return pl.pallas_call(
        partial(attend_back_kernel, dims),
        out_shape=(
            jax.ShapeDtypeStruct((slots, tile, full), F32),
            jax.ShapeDtypeStruct((parts, slots, tile, full), BF16),
            jax.ShapeDtypeStruct((parts, slots, tile, full), BF16),
            jax.ShapeDtypeStruct((full, tile), F32),
            jax.ShapeDtypeStruct((heads, width, tile), F32),
        ),
        in_specs=specs(11, 3),
        out_specs=specs(5, 0),
        scratch_shapes=[
            pltpu.VMEM((heads, slots, width, parts * tile), BF16),
            pltpu.VMEM((heads, width, 2 * tile), BF16),
            pltpu.VMEM((heads, 2 * tile, width), BF16),
            pltpu.VMEM((heads, width, 2 * tile), BF16),
            pltpu.VMEM((heads, 2 * tile, width), BF16),
            pltpu.VMEM((heads, 1, 2 * tile), F32),
            pltpu.VMEM((heads, width, tile), F32),
            pltpu.VMEM((heads, slots, parts, tile, width), F32),
            pltpu.VMEM((heads, slots, parts, tile, width), F32),
        ],
        compiler_params=pltpu.CompilerParams(vmem_limit_bytes=56 << 20),
        cost_estimate=pl.CostEstimate(
            flops=60_000_000_000, bytes_accessed=24_000_000, transcendentals=14_000_000),
        name="attend_back",
    )(slot_of, part, lam, queries, keys_all, values_all, gg, gain, mixed, second, lse)


def per_device(
    inputs,
    block_order,
    mixer_gain,
    query_weight,
    key_weight,
    value_weight,
    lambda_qone,
    lambda_kone,
    lambda_qtwo,
    lambda_ktwo,
    group_gain,
    output_weight,
    feed_gain,
    gate_weight,
    up_weight,
    down_weight,
    cotangent,
):
    seq_count, pair_count, short_rows, model_width = inputs.shape
    assert seq_count == 1
    parts = lax.axis_size("ctx")
    head_total = lax.axis_size("head")
    part = lax.axis_index("ctx")
    head_place = lax.axis_index("head")
    block_len = short_rows * head_total
    slots = block_order.shape[1]
    heads_here, head_dim = lambda_qone.shape
    qwidth = query_weight.shape[1]
    width = 2 * head_dim
    tile = block_len // parts
    strip = short_rows // parts
    dims = (slots, parts, heads_here, tile, width, strip)
    row_count = slots * tile
    order = block_order.reshape(slots)
    slot_of = jnp.argsort(order).astype(jnp.int32)
    index = jnp.arange(tile, dtype=jnp.int32)
    row_offsets = (index // strip) * short_rows + part * strip + index % strip
    own_places = order[:, None] * block_len + row_offsets[None, :]
    lambda_one = jnp.exp(jnp.sum(lambda_qone * lambda_kone, axis=-1))
    lambda_two = jnp.exp(jnp.sum(lambda_qtwo * lambda_ktwo, axis=-1))
    lambda_head = lambda_one - lambda_two + LAMBDA_INIT
    split_shape = (slots, tile, heads_here, 2, head_dim)
    rows_shape = (slots, tile, model_width)

    def spread(rows):
        cut = rows.reshape(pair_count, parts, strip, model_width).transpose(1, 0, 2, 3)
        cut = lax.all_to_all(cut, "ctx", 0, 0, tiled=True)
        return cut.reshape(slots, strip, model_width)

    def unspread(rows):
        cut = rows.reshape(parts, pair_count, strip, model_width)
        cut = lax.all_to_all(cut, "ctx", 0, 0, tiled=True)
        return cut.transpose(1, 0, 2, 3).reshape(1, pair_count, short_rows, model_width)

    inputs_here = spread(inputs)
    tokens = inputs_here.astype(jnp.float32)
    scale_one = rms_scale(tokens)
    normed = (tokens * scale_one * mixer_gain).astype(jnp.bfloat16)
    normed_rows = lax.all_gather(normed, "head", axis=1, tiled=True).reshape(row_count, model_width)
    query_lin = jnp.dot(normed_rows, query_weight, preferred_element_type=jnp.float32)
    key_lin = jnp.dot(normed_rows, key_weight, preferred_element_type=jnp.float32)
    value_lin = jnp.dot(normed_rows, value_weight, preferred_element_type=jnp.float32)
    queries = rotate(query_lin.reshape(split_shape), own_places, 1.0).astype(jnp.bfloat16)
    keys_own = rotate(key_lin.reshape(split_shape), own_places, 1.0).astype(jnp.bfloat16)
    values_own = value_lin.astype(jnp.bfloat16)
    part_shape = (slots, tile, qwidth)
    keys_all = lax.all_gather(keys_own.reshape(part_shape), "ctx", axis=0)
    values_all = lax.all_gather(values_own.reshape(part_shape), "ctx", axis=0)
    part_arr = part.reshape(1).astype(jnp.int32)
    gain_col = group_gain.reshape(qwidth, 1)
    grouped, mixed, second, lse = attend(
        dims, slot_of, part_arr, lambda_head, queries.reshape(part_shape), keys_all, values_all,
        gain_col)
    grouped = grouped.reshape(row_count, qwidth)
    attn_terms = jnp.dot(grouped, output_weight, preferred_element_type=jnp.float32).reshape(
        rows_shape
    )
    hidden = tokens + lax.psum_scatter(
        attn_terms.astype(jnp.bfloat16), "head", scatter_dimension=1, tiled=True
    ).astype(jnp.float32)
    cotangent_here = spread(cotangent)
    scale_two = rms_scale(hidden)
    normed_two = (hidden * scale_two * feed_gain).astype(jnp.bfloat16)
    feed_rows = lax.all_gather(normed_two, "head", axis=1, tiled=True).reshape(
        row_count, model_width
    )
    gate_vals = jnp.dot(feed_rows, gate_weight, preferred_element_type=jnp.float32)
    up_vals = jnp.dot(feed_rows, up_weight, preferred_element_type=jnp.float32)
    gate_sigmoid = jax.nn.sigmoid(gate_vals)
    silu_gate = gate_vals * gate_sigmoid
    activation = (silu_gate * up_vals).astype(jnp.bfloat16)
    feed_terms = jnp.dot(activation, down_weight, preferred_element_type=jnp.float32).reshape(
        rows_shape
    )
    block_out = (
        hidden
        + lax.psum_scatter(
            feed_terms.astype(jnp.bfloat16), "head", scatter_dimension=1, tiled=True
        ).astype(jnp.float32)
    ).astype(jnp.bfloat16)
    grad_rows = lax.all_gather(cotangent_here, "head", axis=1, tiled=True).reshape(
        row_count, model_width
    )
    down_term = contract_rows(grad_rows, activation)
    grad_activ = contract_cols(grad_rows, down_weight)
    grad_gate = (
        grad_activ * up_vals * gate_sigmoid * (1.0 + gate_vals * (1.0 - gate_sigmoid))
    ).astype(jnp.bfloat16)
    grad_up = (grad_activ * silu_gate).astype(jnp.bfloat16)
    gate_term = contract_rows(feed_rows, grad_gate)
    up_term = contract_rows(feed_rows, grad_up)
    normed_two_terms = (
        contract_cols(grad_gate, gate_weight) + contract_cols(grad_up, up_weight)
    ).reshape(rows_shape)
    grad_normed_two = lax.psum_scatter(
        normed_two_terms.astype(jnp.bfloat16), "head", scatter_dimension=1, tiled=True
    ).astype(jnp.float32)
    feed_part = jnp.sum(grad_normed_two * hidden * scale_two, axis=(0, 1))
    grad_hidden = cotangent_here.astype(jnp.float32) + norm_back(
        grad_normed_two, hidden, scale_two, feed_gain
    )
    branch_rows = lax.all_gather(
        grad_hidden.astype(jnp.bfloat16), "head", axis=1, tiled=True
    ).reshape(row_count, model_width)
    output_term = contract_rows(branch_rows, grouped)
    grad_grouped = contract_cols(output_weight, branch_rows)
    query_acc, key_acc, value_acc, group_part, lambda_part = attend_back(
        dims, slot_of, part_arr, lambda_head, queries.reshape(part_shape), keys_all, values_all,
        grad_grouped, gain_col, mixed, second, lse)
    group_part = jnp.sum(group_part, axis=1) * SHRINK
    lambda_part = jnp.sum(lambda_part, axis=(1, 2))
    key_sums = lax.psum_scatter(key_acc, "ctx", scatter_dimension=0).astype(jnp.float32)
    value_sums = lax.psum_scatter(value_acc, "ctx", scatter_dimension=0)
    grad_query = (
        rotate(query_acc.reshape(split_shape), own_places, -1.0)
        .astype(jnp.bfloat16)
        .reshape(row_count, qwidth)
    )
    grad_key = (
        rotate(key_sums.reshape(split_shape), own_places, -1.0)
        .astype(jnp.bfloat16)
        .reshape(row_count, qwidth)
    )
    grad_value = value_sums.reshape(row_count, qwidth)
    query_term = contract_rows(normed_rows, grad_query)
    key_term = contract_rows(normed_rows, grad_key)
    value_term = contract_rows(normed_rows, grad_value)
    normed_terms = (
        contract_cols(grad_query, query_weight)
        + contract_cols(grad_key, key_weight)
        + contract_cols(grad_value, value_weight)
    ).reshape(rows_shape)
    grad_normed = lax.psum_scatter(
        normed_terms.astype(jnp.bfloat16), "head", scatter_dimension=1, tiled=True
    ).astype(jnp.float32)
    mixer_part = jnp.sum(grad_normed * tokens * scale_one, axis=(0, 1))
    input_grad = grad_hidden + norm_back(grad_normed, tokens, scale_one, mixer_gain)
    block_out = unspread(block_out)
    input_grad = unspread(input_grad.astype(BF16)).astype(F32)
    group_full = lax.dynamic_update_slice(
        jnp.zeros((qwidth * head_total,), jnp.float32), group_part, (head_place * qwidth,)
    )
    lambda_full = lax.dynamic_update_slice(
        jnp.zeros((heads_here * head_total,), jnp.float32), lambda_part, (head_place * heads_here,)
    )
    mixer_sum, feed_sum, group_sum, lambda_sum = lax.psum(
        (mixer_part, feed_part, group_full, lambda_full), ("dp", "ctx", "head")
    )
    group_grad = lax.dynamic_slice(group_sum, (head_place * qwidth,), (qwidth,))
    lambda_grad = lax.dynamic_slice(lambda_sum, (head_place * heads_here,), (heads_here,))
    qone_grad = (lambda_grad * lambda_one)[:, None] * lambda_kone
    kone_grad = (lambda_grad * lambda_one)[:, None] * lambda_qone
    qtwo_grad = -(lambda_grad * lambda_two)[:, None] * lambda_ktwo
    ktwo_grad = -(lambda_grad * lambda_two)[:, None] * lambda_qtwo

    def over_all(term):
        return lax.psum_scatter(
            term.astype(jnp.bfloat16), ("dp", "ctx"), scatter_dimension=0, tiled=True
        ).astype(jnp.float32)

    return (
        block_out,
        input_grad,
        mixer_sum,
        over_all(query_term),
        over_all(key_term),
        over_all(value_term),
        qone_grad,
        kone_grad,
        qtwo_grad,
        ktwo_grad,
        group_grad,
        over_all(output_term).T,
        feed_sum,
        over_all(gate_term),
        over_all(up_term),
        over_all(down_term).T,
    )


def solution(mesh):
    return jax.shard_map(
        per_device,
        mesh=mesh,
        in_specs=(
            P("dp", "ctx", "head", None),
            P("dp", None),
            P(),
            P(None, "head"),
            P(None, "head"),
            P(None, "head"),
            P("head", None),
            P("head", None),
            P("head", None),
            P("head", None),
            P("head"),
            P("head", None),
            P(),
            P(None, "head"),
            P(None, "head"),
            P("head", None),
            P("dp", "ctx", "head", None),
        ),
        out_specs=(
            P("dp", "ctx", "head", None),
            P("dp", "ctx", "head", None),
            P(),
            P(("dp", "ctx"), "head"),
            P(("dp", "ctx"), "head"),
            P(("dp", "ctx"), "head"),
            P("head", None),
            P("head", None),
            P("head", None),
            P("head", None),
            P("head"),
            P("head", ("dp", "ctx")),
            P(),
            P(("dp", "ctx"), "head"),
            P(("dp", "ctx"), "head"),
            P("head", ("dp", "ctx")),
        ),
        check_vma=False,
    )
```

profile of v0, /device:TPU:0, one launch (start us, length us, event | category | flops | bytes accessed | tf_op | source)
XLA Modules:
  0.0 1228.9 jit_solution(3439359306168216050)
XLA Ops:
  8.6 15.7 %all_to_all.20 = bf16[4,2,32,1536]{3,2,1,0:T(8,128)(2,1)S(1)} all-to-all(bf16[4,2,32,1536]{3,2,1,0:T(8,128)(2,1)S(1)} %bitcast.144), channel_id=1, replica_groups=mesh['dp'=2,'ctx'=4,'head'=4] {'ctx'}, dimensions={0} | all-to-all | bytes 1572864 | tf_op jit(solution)/shard_map/all_to_all | solution.py:355
  26.4 63.8 %all-gather.7.cloned.1.call-done = bf16[8,128,1536]{2,1,0:T(8,128)(2,1)} async-done(((bf16[8,32,1536]{2,1,0:T(8,128)(2,1)}), bf16[8,128,1536]{2,1,0:T(8,128)(2,1)}) %all-gather.7.cloned.1.call-update) | async-done | bytes 3145744 | tf_op jit(solution)/shard_map/all_gather | solution.py:367
  122.5 30.7 %all-gather.9.cloned.1.call-done.k_ref = bf16[4,8,128,384]{3,2,1,0:T(8,128)(2,1)} async-done(((bf16[1,8,128,384]{3,2,1,0:T(8,128)(2,1)}), bf16[4,8,128,384]{3,2,1,0:T(8,128)(2,1)}) %all-gather.9.cloned.1.call-update) | async-done | bytes 3145744 | tf_op jit(solution)/shard_map/all_gather | solution.py:375
  154.3 49.9 %attend.1 = (bf16[8,128,384]{2,1,0:T(8,128)(2,1)S(1)}, f32[8,3,128,128]{3,2,1,0:T(8,128)S(1)}, f32[8,3,128,128]{3,2,1,0:T(8,128)S(1)}, f32[8,3,1,256]{3,2,1,0:T(1,128)S(1)}) custom-call(s32[8]{0:T(128)S(1)} %get-tuple-element.26.slot_ref, s32[1]{0:T(128)} %bitcast.4.part_ref, f32[3]{0:T(128)S(1)} %subtract_add_fusion.lam_ref, ...), custom_call_target="tpu_custom_call" | custom-call | flops 20000000000 | bytes 12000000 | tf_op jit(solution)/shard_map/attend/pallas_call | solution.py:254
  211.5 60.5 %reduce-scatter.16.cloned.1.call-done = bf16[8,32,1536]{2,1,0:T(8,128)(2,1)} async-done(((bf16[8,128,1536]{2,1,0:T(8,128)(2,1)}), bf16[8,32,1536]{2,1,0:T(8,128)(2,1)}) %reduce-scatter.16.cloned.1.call-update) | async-done | bytes 786448 | tf_op jit(solution)/shard_map/reduce_scatter | solution.py:386
  277.4 14.7 %all_to_all.21 = bf16[4,2,32,1536]{3,2,1,0:T(8,128)(2,1)} all-to-all(bf16[4,2,32,1536]{3,2,1,0:T(8,128)(2,1)S(1)} %bitcast.145), channel_id=1, replica_groups=mesh['dp'=2,'ctx'=4,'head'=4] {'ctx'}, dimensions={0} | all-to-all | bytes 1572864 | tf_op jit(solution)/shard_map/all_to_all | solution.py:355
  292.4 47.2 %all-gather.13.cloned.1.call-done = bf16[8,128,1536]{2,1,0:T(8,128)(2,1)} async-done(((bf16[8,32,1536]{2,1,0:T(8,128)(2,1)}), bf16[8,128,1536]{2,1,0:T(8,128)(2,1)}) %all-gather.13.cloned.1.call-update) | async-done | bytes 3145744 | tf_op jit(solution)/shard_map/all_gather | solution.py:392
  353.0 50.1 %all-gather.15.cloned.1.call-done = bf16[8,128,1536]{2,1,0:T(8,128)(2,1)} async-done(((bf16[8,32,1536]{2,1,0:T(8,128)(2,1)}), bf16[8,128,1536]{2,1,0:T(8,128)(2,1)}) %all-gather.15.cloned.1.call-update) | async-done | bytes 3145744 | tf_op jit(solution)/shard_map/all_gather | solution.py:409
  403.2 9.6 multiply_convert_fusion
  421.3 59.2 %reduce-scatter.20.cloned.1.call-done = bf16[8,32,1536]{2,1,0:T(8,128)(2,1)} async-done(((bf16[8,128,1536]{2,1,0:T(8,128)(2,1)}), bf16[8,32,1536]{2,1,0:T(8,128)(2,1)}) %reduce-scatter.20.cloned.1.call-update) | async-done | bytes 786448 | tf_op jit(solution)/shard_map/reduce_scatter | solution.py:423
  485.6 63.0 %all-gather.17.cloned.1.call-done = bf16[8,128,1536]{2,1,0:T(8,128)(2,1)} async-done(((bf16[8,32,1536]{2,1,0:T(8,128)(2,1)}), bf16[8,128,1536]{2,1,0:T(8,128)(2,1)}) %all-gather.17.cloned.1.call-update) | async-done | bytes 3145744 | tf_op jit(solution)/shard_map/all_gather | solution.py:430
  553.4 98.2 %attend_back.1 = (f32[8,128,384]{2,1,0:T(8,128)}, bf16[4,8,128,384]{3,2,1,0:T(8,128)(2,1)}, bf16[4,8,128,384]{3,2,1,0:T(8,128)(2,1)}, f32[384,128]{1,0:T(8,128)}, f32[3,128,128]{2,1,0:T(8,128)}) custom-call(s32[8]{0:T(128)} %copy-done.4, s32[1]{0:T(128)} %bitcast.4.part_ref, f32[3]{0:T(128)} %copy-done.3, bf16[8,128,384]{2,1,0:T(8,128)(2,1)} %copy.68.q_ref, ...), custom_call_target="tpu_custom_call" | custom-call | flops 60000002048 | bytes 24000000 | tf_op jit(solution)/shard_map/attend_back/pallas_call | solution.py:279
  668.0 20.3 %reduce-scatter.22.cloned.1.call-done = bf16[1,8,128,384]{3,2,1,0:T(8,128)(2,1)} async-done(((bf16[4,8,128,384]{3,2,1,0:T(8,128)(2,1)}), bf16[1,8,128,384]{3,2,1,0:T(8,128)(2,1)}) %reduce-scatter.22.cloned.1.call-update) | async-done | bytes 786448 | tf_op jit(solution)/shard_map/reduce_scatter | solution.py:440
  704.0 24.6 %reduce-scatter.24.cloned.1.call-done = bf16[1,8,128,384]{3,2,1,0:T(8,128)(2,1)} async-done(((bf16[4,8,128,384]{3,2,1,0:T(8,128)(2,1)}), bf16[1,8,128,384]{3,2,1,0:T(8,128)(2,1)}) %reduce-scatter.24.cloned.1.call-update) | async-done | bytes 786448 | tf_op jit(solution)/shard_map/reduce_scatter | solution.py:441
  728.6 8.6 add_convert_fusion
  785.1 55.6 %reduce-scatter.26.cloned.1.call-done = bf16[8,32,1536]{2,1,0:T(8,128)(2,1)} async-done(((bf16[8,128,1536]{2,1,0:T(8,128)(2,1)}), bf16[8,32,1536]{2,1,0:T(8,128)(2,1)}) %reduce-scatter.26.cloned.1.call-update) | async-done | bytes 786448 | tf_op jit(solution)/shard_map/reduce_scatter | solution.py:461
  843.1 60.3 %reduce-scatter.18.cloned.1.call-done = bf16[8,32,1536]{2,1,0:T(8,128)(2,1)} async-done(((bf16[8,128,1536]{2,1,0:T(8,128)(2,1)}), bf16[8,32,1536]{2,1,0:T(8,128)(2,1)}) %reduce-scatter.18.cloned.1.call-update) | async-done | bytes 786448 | tf_op jit(solution)/shard_map/reduce_scatter | solution.py:405
  916.9 35.7 %reduce-scatter.38.cloned.1.call-done = bf16[192,1024]{1,0:T(8,128)(2,1)} async-done(((bf16[1536,1024]{1,0:T(8,128)(2,1)}), bf16[192,1024]{1,0:T(8,128)(2,1)}) %reduce-scatter.38.cloned.1.call-update) | async-done | bytes 393232 | tf_op jit(solution)/shard_map/reduce_scatter | solution.py:485
  954.5 47.4 %reduce-scatter.36.cloned.1.call-done = bf16[192,1024]{1,0:T(8,128)(2,1)} async-done(((bf16[1536,1024]{1,0:T(8,128)(2,1)}), bf16[192,1024]{1,0:T(8,128)(2,1)}) %reduce-scatter.36.cloned.1.call-update) | async-done | bytes 393232 | tf_op jit(solution)/shard_map/reduce_scatter | solution.py:485
  1005.6 36.1 %reduce-scatter.34.cloned.1.call-done = bf16[192,384]{1,0:T(8,128)(2,1)} async-done(((bf16[1536,384]{1,0:T(8,128)(2,1)}), bf16[192,384]{1,0:T(8,128)(2,1)}) %reduce-scatter.34.cloned.1.call-update) | async-done | bytes 147472 | tf_op jit(solution)/shard_map/reduce_scatter | solution.py:485
  1043.4 38.1 %reduce-scatter.28.cloned.1.call-done = bf16[192,384]{1,0:T(8,128)(2,1)} async-done(((bf16[1536,384]{1,0:T(8,128)(2,1)}), bf16[192,384]{1,0:T(8,128)(2,1)}) %reduce-scatter.28.cloned.1.call-update) | async-done | bytes 147472 | tf_op jit(solution)/shard_map/reduce_scatter | solution.py:485
  1083.1 38.2 %reduce-scatter.30.cloned.1.call-done = bf16[192,384]{1,0:T(8,128)(2,1)} async-done(((bf16[1536,384]{1,0:T(8,128)(2,1)}), bf16[192,384]{1,0:T(8,128)(2,1)}) %reduce-scatter.30.cloned.1.call-update) | async-done | bytes 147472 | tf_op jit(solution)/shard_map/reduce_scatter | solution.py:485
  1122.9 38.3 %reduce-scatter.32.cloned.1.call-done = bf16[192,384]{1,0:T(8,128)(2,1)} async-done(((bf16[1536,384]{1,0:T(8,128)(2,1)}), bf16[192,384]{1,0:T(8,128)(2,1)}) %reduce-scatter.32.cloned.1.call-update) | async-done | bytes 147472 | tf_op jit(solution)/shard_map/reduce_scatter | solution.py:485
  1162.9 39.9 %all-reduce = (f32[1536]{0:T(1024)}, f32[12]{0:T(128)S(1)}, f32[1536]{0:T(1024)S(1)}, f32[1536]{0:T(1024)}) all-reduce(f32[1536]{0:T(1024)S(1)} %get-tuple-element.86, f32[12]{0:T(128)S(1)} %dynamic_update_slice.6, f32[1536]{0:T(1024)S(1)} %multiply_dynamic-update-slice_fusion, ...), channel_id=1, replica_groups=mesh['dp'=2,'ctx'=4,'head'=4] {'dp','ctx','head'}, use_global_device_ids=true, to_apply=%region_14.15 | all-reduce | flops 4620 | bytes 36960 | tf_op jit(solution)/shard_map/psum | solution.py:474
  (226 shorter events, 208.1 us)
Async XLA Ops:
  7.2 396.0 %copy-start = (bf16[1024,1536]{1,0:T(8,128)(2,1)S(1)}, bf16[1024,1536]{1,0:T(8,128)(2,1)}, u32[]{:S(2)}) copy-start(bf16[1024,1536]{1,0:T(8,128)(2,1)} %param.32) | copy-start | bytes 9437188
  7.2 83.1 %all-gather.7.cloned.1.call-start = ((), (), s32[]{:S(2)}) async-start(), calls=%async_computation.17 | async-start | bytes 3932160 | tf_op jit(solution)/shard_map/all_gather | solution.py:367
  26.4 96.1 %all-gather.11.cloned.1.call-start = ((), (), s32[]{:S(2)}) async-start(), calls=%async_computation.19 | async-start | bytes 3932160 | tf_op jit(solution)/shard_map/all_gather | solution.py:376
  95.2 58.0 %all-gather.9.cloned.1.call-start = ((), (), s32[]{:S(2)}) async-start(), calls=%async_computation.18 | async-start | bytes 3932160 | tf_op jit(solution)/shard_map/all_gather | solution.py:375
  111.3 160.7 %reduce-scatter.16.cloned.1.call-start = ((), (), s32[]{:S(2)}) async-start(), calls=%async_computation.20 | async-start | bytes 3932160 | tf_op jit(solution)/shard_map/reduce_scatter | solution.py:386
  211.5 128.2 %all-gather.13.cloned.1.call-start = ((), (), s32[]{:S(2)}) async-start(), calls=%async_computation.21 | async-start | bytes 3932160 | tf_op jit(solution)/shard_map/all_gather | solution.py:392
  276.1 127.0 %all-gather.15.cloned.1.call-start = ((), (), s32[]{:S(2)}) async-start(), calls=%async_computation.23 | async-start | bytes 3932160 | tf_op jit(solution)/shard_map/all_gather | solution.py:409
  292.2 188.4 %reduce-scatter.20.cloned.1.call-start = ((), (), s32[]{:S(2)}) async-start(), calls=%async_computation.24 | async-start | bytes 3932160 | tf_op jit(solution)/shard_map/reduce_scatter | solution.py:423
  421.3 127.3 %all-gather.17.cloned.1.call-start = ((), (), s32[]{:S(2)}) async-start(), calls=%async_computation.25 | async-start | bytes 3932160 | tf_op jit(solution)/shard_map/all_gather | solution.py:430
  485.1 203.2 %reduce-scatter.22.cloned.1.call-start = ((), (), s32[]{:S(2)}) async-start(), calls=%async_computation.26 | async-start | bytes 3932160 | tf_op jit(solution)/shard_map/reduce_scatter | solution.py:440
  651.6 77.0 %reduce-scatter.24.cloned.1.call-start = ((), (), s32[]{:S(2)}) async-start(), calls=%async_computation.27 | async-start | bytes 3932160 | tf_op jit(solution)/shard_map/reduce_scatter | solution.py:441
  652.2 125.9 %reduce-scatter.40.cloned.1.call-start = ((), (), s32[]{:S(2)}) async-start(), calls=%async_computation.35 | async-start | bytes 3538944
  664.7 176.0 %reduce-scatter.26.cloned.1.call-start = ((), (), s32[]{:S(2)}) async-start(), calls=%async_computation.28 | async-start | bytes 3932160 | tf_op jit(solution)/shard_map/reduce_scatter | solution.py:461
  737.3 166.1 %reduce-scatter.18.cloned.1.call-start = ((), (), s32[]{:S(2)}) async-start(), calls=%async_computation.22 | async-start | bytes 3932160 | tf_op jit(solution)/shard_map/reduce_scatter | solution.py:405
  743.9 208.7 %reduce-scatter.38.cloned.1.call-start = ((), (), s32[]{:S(2)}) async-start(), calls=%async_computation.34 | async-start | bytes 3538944 | tf_op jit(solution)/shard_map/reduce_scatter | solution.py:485
  751.7 250.2 %reduce-scatter.36.cloned.1.call-start = ((), (), s32[]{:S(2)}) async-start(), calls=%async_computation.33 | async-start | bytes 3538944 | tf_op jit(solution)/shard_map/reduce_scatter | solution.py:485
  760.2 281.5 %reduce-scatter.34.cloned.1.call-start = ((), (), s32[]{:S(2)}) async-start(), calls=%async_computation.32 | async-start | bytes 1327104 | tf_op jit(solution)/shard_map/reduce_scatter | solution.py:485
  765.3 316.2 %reduce-scatter.28.cloned.1.call-start = ((), (), s32[]{:S(2)}) async-start(), calls=%async_computation.29 | async-start | bytes 1327104 | tf_op jit(solution)/shard_map/reduce_scatter | solution.py:485
  770.3 351.0 %reduce-scatter.30.cloned.1.call-start = ((), (), s32[]{:S(2)}) async-start(), calls=%async_computation.30 | async-start | bytes 1327104 | tf_op jit(solution)/shard_map/reduce_scatter | solution.py:485
  775.4 385.9 %reduce-scatter.32.cloned.1.call-start = ((), (), s32[]{:S(2)}) async-start(), calls=%async_computation.31 | async-start | bytes 1327104 | tf_op jit(solution)/shard_map/reduce_scatter | solution.py:485
  908.0 295.4 %all-to-all-start.1 = ((bf16[4,2,32,1536]{3,2,1,0:T(8,128)(2,1)}), bf16[4,2,32,1536]{3,2,1,0:T(8,128)(2,1)}, u32[]{:S(2)}, u32[]{:S(2)}) async-start(bf16[4,2,32,1536]{3,2,1,0:T(8,128)(2,1)} %bitcast.141), calls=%async_computation.3 | async-start | bytes 1572864 | tf_op jit(solution)/shard_map/all_to_all | solution.py:360
  1004.5 203.9 %copy-start.34 = (f32[3,64]{1,0:T(4,128)S(1)}, f32[3,64]{1,0:T(4,128)}, u32[]{:S(2)}) copy-start(f32[3,64]{1,0:T(4,128)} %param.23) | copy-start | bytes 2308
  1004.5 203.8 %copy-start.36 = (f32[3,64]{1,0:T(4,128)S(1)}, f32[3,64]{1,0:T(4,128)}, u32[]{:S(2)}) copy-start(f32[3,64]{1,0:T(4,128)} %param.24) | copy-start | bytes 2308
  1203.4 15.9 %all-to-all-start.3 = ((bf16[4,2,32,1536]{3,2,1,0:T(8,128)(2,1)}), bf16[4,2,32,1536]{3,2,1,0:T(8,128)(2,1)}, u32[]{:S(2)}, u32[]{:S(2)}) async-start(bf16[4,2,32,1536]{3,2,1,0:T(8,128)(2,1)} %bitcast.140), calls=%async_computation.9 | async-start | bytes 1572864 | tf_op jit(solution)/shard_map/all_to_all | solution.py:360
  (48 other events, 1610.2 us)
Sparse Core Ops, SparseCore 0:
  26.5 63.7 all-gather.6
  95.3 27.1 all-gather.10
  124.6 28.4 all-gather.8
  211.6 60.3 reduce-scatter.15
  276.3 63.3 all-gather.12
  341.1 62.0 all-gather.14
  421.4 59.0 reduce-scatter.19
  485.2 63.3 all-gather.16
  651.7 36.5 reduce-scatter.21
  690.7 37.8 reduce-scatter.23
  732.0 46.0 reduce-scatter.39
  780.3 60.3 reduce-scatter.25
  843.0 60.2 reduce-scatter.17
  906.6 45.9 reduce-scatter.37
  955.8 46.0 reduce-scatter.35
  1005.0 36.6 reduce-scatter.33
  1044.8 36.6 reduce-scatter.27
  1084.6 36.6 reduce-scatter.29
  1124.5 36.6 reduce-scatter.31
where the time goes:
time: 1240 us; the launch traced here: 1230 us
  waiting for transfers between devices  788 us (64%)
  Pallas kernels  148 us (12%)
  matrix products  118 us (10%)
  blocking collectives  70.3 us (6%)
  other arithmetic  39.8 us (3%)
  local copies, waits for them, and re-layouts  39.4 us (3%)
  between operations  15 us (1%)
    reduce_scatter x6, waiting for transfers between devices, over_all(): lax.psum_scatter(term.astype(jnp.bfloat16), ('dp', 'ctx'), scatter_dimens...  234 us
    pallas_call x1, Pallas kernels, attend_back(): pl.pallas_call(partial(attend_back_kernel, dims), out_shape=(jax.ShapeDty...  98.2 us
    all_gather x1, waiting for transfers between devices, per_device(): lax.all_gather(normed, 'head', axis=1, tiled=True)  63.8 us
    all_gather x1, waiting for transfers between devices, per_device(): lax.all_gather(grad_hidden.astype(jnp.bfloat16), 'head', axis=1, tiled=True)  63 us
    reduce_scatter x1, waiting for transfers between devices, per_device(): lax.psum_scatter(attn_terms.astype(jnp.bfloat16), 'head', scatter_dimensi...  60.5 us
    reduce_scatter x1, waiting for transfers between devices, per_device(): lax.psum_scatter(feed_terms.astype(jnp.bfloat16), 'head', scatter_dimensi...  60.3 us
    reduce_scatter x1, waiting for transfers between devices, per_device(): lax.psum_scatter(normed_two_terms.astype(jnp.bfloat16), 'head', scatter_d...  59.2 us
    reduce_scatter x1, waiting for transfers between devices, per_device(): lax.psum_scatter(normed_terms.astype(jnp.bfloat16), 'head', scatter_dimen...  55.6 us
  transfers between devices with their start and end apart: 21, of which 20 were waited for; matrix products, arithmetic and copies ran while one was open for 12% of the time, Pallas kernels for 0%

commit v1 on v0

--- a/solution.py
+++ b/solution.py
@@ -71,7 +71,7 @@
     )
 
 
-def attend_kernel(dims, slot_ref, part_ref, lam_ref, q_ref, k_ref, v_ref, gain_ref,
+def attend_kernel(dims, part_ref, lam_ref, q_ref, k_ref, v_ref, gain_ref,
                   grouped_ref, mixed_ref, second_ref, lse_ref, vt_ref, qbd_ref, acc_ref):
     slots, parts, heads, tile, width, strip = dims
     half = width // 2
@@ -115,16 +115,15 @@
         return tuple(out)
 
     def one_place(place, carry):
-        own = slot_ref[place]
-        for h in range(heads):
-            turned = jnp.transpose(q_ref[own, :, h * width:(h + 1) * width])
+        for h in range(heads):
+            turned = jnp.transpose(q_ref[place, :, h * width:(h + 1) * width])
             turned = turned * jnp.asarray(half ** -0.5, turned.dtype)
             qbd_ref[h] = block_diag_cols(turned, half, tile)
             acc_ref[h] = jnp.zeros((width, cols), F32)
         state = (jnp.full((1, cols), NEGATIVE, F32), jnp.zeros((1, cols), F32)) * heads
-        state = one_block(own, True, state)
+        state = one_block(place, True, state)
         state = lax.fori_loop(
-            0, place, lambda j, st: one_block(slot_ref[j], False, st), state)
+            0, place, lambda j, st: one_block(j, False, st), state)
         for h in range(heads):
             peak, total = state[2 * h], state[2 * h + 1]
             result = acc_ref[h] / total
@@ -133,74 +132,133 @@
             scale = lax.rsqrt(jnp.mean(mixed * mixed, axis=0, keepdims=True) + EPSILON)
             gain = gain_ref[h * width:(h + 1) * width, :] * SHRINK
             grouped = (mixed * scale * gain).astype(BF16)
-            grouped_ref[own, :, h * width:(h + 1) * width] = jnp.transpose(grouped)
-            mixed_ref[own, h] = mixed
-            second_ref[own, h] = second
-            lse_ref[own, h] = peak + jnp.log(total)
+            grouped_ref[place, :, h * width:(h + 1) * width] = jnp.transpose(grouped)
+            mixed_ref[place, h] = mixed
+            second_ref[place, h] = second
+            lse_ref[place, h] = peak + jnp.log(total)
         return carry
 
     lax.fori_loop(0, slots, one_place, 0)
 
 
-def attend_back_kernel(dims, slot_ref, part_ref, lam_ref, q_ref, k_ref, v_ref, gg_ref, gain_ref,
-                       mixed_ref, second_ref, lse_ref,
-                       dq_ref, dk_ref, dv_ref, gpart_ref, lpart_ref,
+def mesh_copy(src, dst, send_sem, recv_sem, device):
+    return pltpu.make_async_remote_copy(
+        src_ref=src, dst_ref=dst, send_sem=send_sem, recv_sem=recv_sem,
+        device_id=device, device_id_type=pl.DeviceIdType.MESH)
+
+
+def greet(devices):
+    barrier = pltpu.get_barrier_semaphore()
+    for device in devices:
+        pl.semaphore_signal(
+            barrier, inc=1, device_id=device, device_id_type=pl.DeviceIdType.MESH)
+    pl.semaphore_wait(barrier, len(devices))
+
+
+def swap_halves(rows, half):
+    quarter = half // 2
+    lane = lax.broadcasted_iota(jnp.int32, rows.shape, 1)
+    back = pltpu.roll(rows, rows.shape[1] - quarter, 1)
+    ahead = pltpu.roll(rows, quarter, 1)
+    return jnp.where(lane % half < quarter, back, ahead)
+
+
+def attend_back_kernel(dims, groups, lam_ref, q_ref, k_ref, v_ref, gg_ref, gain_ref,
+                       mixed_ref, second_ref, lse_ref, cost_ref, sint_ref, cosn_ref, sinn_ref,
+                       wg_ref,
+                       gq_ref, gk_ref, gv_ref, gpart_ref, lpart_ref, wsum_ref,
                        kt_ref, qbdt_ref, qbd_ref, gt_ref, g_ref, delta_ref, dqt_ref,
-                       dka_ref, dva_ref):
+                       dka_ref, dva_ref, sb_ref, r1_ref, s2_ref, r2_ref,
+                       wown_ref, wr1_ref, wr2_ref,
+                       s1_sem, r1_sem, s2_sem, r2_sem, w1_sem, w2s_sem, w2r_sem):
     slots, parts, heads, tile, width, strip = dims
     half = width // 2
     scale = half ** -0.5
-
-    def turn(slot, carry):
-        for h in range(heads):
-            for c in range(parts):
-                kt_ref[h, slot, :, c * tile:(c + 1) * tile] = jnp.transpose(
-                    k_ref[c, slot, :, h * width:(h + 1) * width])
-        return carry
-
-    lax.fori_loop(0, slots, turn, 0)
+    part = lax.axis_index("ctx")
+    row = lax.axis_index("dp")
+    core = part % 2
+    y = part // 2
+    other_core = 1 - core
+    other_y = 1 - y
+    me = row * 2 + y
+    sibling = {"ctx": y * 2 + other_core}
+    across = {"ctx": other_y * 2 + core}
+
+    def group_device(index):
+        return {"dp": index // 2, "ctx": (index % 2) * 2 + core}
+
+    others = [lax.rem(me + step, groups) for step in range(1, groups)]
+    greet([sibling] + [group_device(index) for index in others])
+
+    weights_out = mesh_copy(
+        wg_ref.at[:, :, other_core], wr1_ref, w1_sem.at[0], w1_sem.at[1], sibling)
+    weights_out.start()
+    weights_own = pltpu.make_async_copy(wg_ref.at[:, :, core], wown_ref, w1_sem.at[2])
+    weights_own.start()
+
+    def weights_send(step):
+        index = others[step]
+        return mesh_copy(wown_ref.at[:, index], wr2_ref.at[step], w2s_sem.at[step],
+                         w2r_sem.at[step], group_device(index))
+
+    def weights_cross():
+        weights_out.wait()
+        weights_own.wait()
+
+        def add(index, carry):
+            for t in range(wown_ref.shape[0]):
+                wown_ref[t, index] = (
+                    wown_ref[t, index].astype(F32) + wr1_ref[t, index].astype(F32)).astype(BF16)
+            return carry
+
+        lax.fori_loop(0, groups, add, 0)
+        for step in range(groups - 1):
+            weights_send(step).start()
+
+    def weights_finish():
+        for step in range(groups - 1):
+            weights_send(step).wait()
+        for t in range(wown_ref.shape[0]):
+            total = wown_ref[t, me].astype(F32)
+            for step in range(groups - 1):
+                total = total + wr2_ref[step, t].astype(F32)
+            wsum_ref[t] = total
+
+    def first_copy(j):
+        return mesh_copy(sb_ref.at[j, other_core], r1_ref.at[j], s1_sem.at[j], r1_sem.at[j],
+                         sibling)
+
+    def second_copy(j):
+        return mesh_copy(s2_ref.at[j], r2_ref.at[j], s2_sem.at[j], r2_sem.at[j], across)
+
+    def pass_on(j):
+        first_copy(j).wait()
+        s2_ref[j] = (
+            sb_ref[j, core, other_y].astype(F32) + r1_ref[j, other_y].astype(F32)).astype(BF16)
+
+    def finish(j):
+        second_copy(j).wait()
+        total = (sb_ref[j, core, y].astype(F32) + r1_ref[j, y].astype(F32)
+                 + r2_ref[j].astype(F32))
+        gv_ref[j] = total[1].astype(BF16)
+        for h in range(heads):
+            lanes = slice(h * width, (h + 1) * width)
+            grad = total[0, :, lanes]
+            gk_ref[j, :, lanes] = (
+                grad * cosn_ref[j] + swap_halves(grad, half) * sinn_ref[j]).astype(BF16)
+
     gpart_ref[...] = jnp.zeros_like(gpart_ref)
     lpart_ref[...] = jnp.zeros_like(lpart_ref)
-    query_off = offsets_of(part_ref[0], parts, strip, 1, (1, tile))
+    query_off = offsets_of(part, parts, strip, 1, (1, tile))
     query_off = jnp.concatenate([query_off, query_off], axis=1)
 
-    def one_block(own, slot, diag):
-        for h in range(heads):
-            lse = lse_ref[own, h]
-            delta = delta_ref[h]
-            lanes = slice(h * width, (h + 1) * width)
-            turned = []
-            for c in range(parts):
-                keys = k_ref[c, slot, :, lanes]
-                s = dot(keys, qbdt_ref[h])
-                if diag:
-                    key_off = offsets_of(c, parts, strip, 0, (tile, 1))
-                    s = jnp.where(key_off <= query_off, s, NEGATIVE)
-                weights = jnp.exp(s - lse)
-                probs = dot(v_ref[c, slot, :, lanes], gt_ref[h])
-                ds = (weights * (probs - delta)).astype(BF16)
-                dv = dot(weights.astype(BF16), g_ref[h])
-                dk = dot(ds, qbd_ref[h])
-                if diag:
-                    dva_ref[h, slot, c] = dv
-                    dka_ref[h, slot, c] = dk
-                else:
-                    dva_ref[h, slot, c] += dv
-                    dka_ref[h, slot, c] += dk
-                turned.append(ds)
-            dq = dot(kt_ref[h, slot], jnp.concatenate(turned, axis=0))
-            dqt_ref[h, :half] += dq[:half, :tile]
-            dqt_ref[h, half:] += dq[half:, tile:]
-
-    def one_place(place, carry):
-        own = slot_ref[place]
+    def prepare(place, carry):
         for h in range(heads):
             lanes = slice(h * width, (h + 1) * width)
             lam = lam_ref[h]
-            start = pl.multiple_of(own * tile, tile)
-            grad = gg_ref[lanes, pl.ds(start, tile)]
-            mixed = mixed_ref[own, h]
-            second = second_ref[own, h]
+            grad = gg_ref[lanes, pl.ds(pl.multiple_of(place * tile, tile), tile)]
+            mixed = mixed_ref[place, h]
+            second = second_ref[place, h]
             rg = lax.rsqrt(jnp.mean(mixed * mixed, axis=0, keepdims=True) + EPSILON)
             gpart_ref[lanes, :] += grad * (mixed * rg)
             up = grad * (gain_ref[lanes, :] * SHRINK)
@@ -208,40 +266,112 @@
             lpart_ref[h] -= gm * second
             along = jnp.sum(gm * second, axis=0, keepdims=True)
             first = jnp.sum(gm * mixed, axis=0, keepdims=True) + lam * along
-            delta_ref[h] = jnp.concatenate([first, -lam * along], axis=1)
+            delta_ref[place, h] = jnp.concatenate([first, -lam * along], axis=1)
             both = jnp.concatenate([gm, -lam * gm], axis=1)
-            gt_ref[h] = both.astype(BF16)
-            g_ref[h] = jnp.transpose(both).astype(BF16)
-            query = q_ref[own, :, lanes]
+            gt_ref[place, h] = both.astype(BF16)
+            g_ref[place, h] = jnp.transpose(both).astype(BF16)
+            query = q_ref[place, :, lanes]
             query = query * jnp.asarray(scale, query.dtype)
-            qbdt_ref[h] = block_diag_cols(jnp.transpose(query), half, tile)
+            qbdt_ref[place, h] = block_diag_cols(jnp.transpose(query), half, tile)
             lane = lax.broadcasted_iota(jnp.int32, (tile, width), 1)
             zero = jnp.zeros_like(query)
-            qbd_ref[h, :tile] = jnp.where(lane < half, query, zero)
-            qbd_ref[h, tile:] = jnp.where(lane >= half, query, zero)
-            dqt_ref[h] = jnp.zeros((width, tile), F32)
-        one_block(own, own, True)
-
-        def rest(j, c):
-            one_block(own, slot_ref[j], False)
-            return c
-
-        lax.fori_loop(0, place, rest, 0)
-        for h in range(heads):
-            dq_ref[own, :, h * width:(h + 1) * width] = jnp.transpose(dqt_ref[h] * scale)
+            qbd_ref[place, h, :tile] = jnp.where(lane < half, query, zero)
+            qbd_ref[place, h, tile:] = jnp.where(lane >= half, query, zero)
+            dqt_ref[place, h] = jnp.zeros((width, tile), F32)
         return carry
 
-    lax.fori_loop(0, slots, one_place, 0)
-
-    def put(slot, carry):
+    lax.fori_loop(0, slots, prepare, 0)
+
+    def one_block(place, slot, diag):
+        for h in range(heads):
+            lse = lse_ref[place, h]
+            delta = delta_ref[place, h]
+            lanes = slice(h * width, (h + 1) * width)
+            turned = []
+            for c in range(parts):
+                keys = k_ref[c, slot, :, lanes]
+                s = dot(keys, qbdt_ref[place, h])
+                if diag:
+                    key_off = offsets_of(c, parts, strip, 0, (tile, 1))
+                    s = jnp.where(key_off <= query_off, s, NEGATIVE)
+                weights = jnp.exp(s - lse)
+                probs = dot(v_ref[c, slot, :, lanes], gt_ref[place, h])
+                ds = (weights * (probs - delta)).astype(BF16)
+                dv = dot(weights.astype(BF16), g_ref[place, h])
+                dk = dot(ds, qbd_ref[place, h])
+                if diag:
+                    dva_ref[h, c] = dv
+                    dka_ref[h, c] = dk
+                else:
+                    dva_ref[h, c] += dv
+                    dka_ref[h, c] += dk
+                turned.append(ds)
+            dq = dot(kt_ref[h], jnp.concatenate(turned, axis=0))
+            dqt_ref[place, h, :half] += dq[:half, :tile]
+            dqt_ref[place, h, half:] += dq[half:, tile:]
+
+    def one_key_block(j, carry):
+        slot = j
+        for h in range(heads):
+            for c in range(parts):
+                kt_ref[h, :, c * tile:(c + 1) * tile] = jnp.transpose(
+                    k_ref[c, slot, :, h * width:(h + 1) * width])
+        one_block(j, slot, True)
+
+        def rest(place, inner):
+            one_block(place, slot, False)
+            return inner
+
+        lax.fori_loop(j + 1, slots, rest, 0)
         for h in range(heads):
             lanes = slice(h * width, (h + 1) * width)
             for c in range(parts):
-                dk_ref[c, slot, :, lanes] = dka_ref[h, slot, c].astype(BF16)
-                dv_ref[c, slot, :, lanes] = dva_ref[h, slot, c].astype(BF16)
+                sb_ref[j, c % 2, c // 2, 0, :, lanes] = dka_ref[h, c].astype(BF16)
+                sb_ref[j, c % 2, c // 2, 1, :, lanes] = dva_ref[h, c].astype(BF16)
+
+        @pl.when(j >= 1)
+        def _():
+            pass_on(j - 1)
+
+        @pl.when(j == 0)
+        def _():
+            weights_cross()
+
+        @pl.when(j >= 2)
+        def _():
+            finish(j - 2)
+
+        first_copy(j).start()
+
+        @pl.when(j >= 1)
+        def _():
+            second_copy(j - 1).start()
+
         return carry
 
-    lax.fori_loop(0, slots, put, 0)
+    lax.fori_loop(0, slots, one_key_block, 0)
+
+    pass_on(slots - 1)
+
+    def put(place, carry):
+        quarter = half // 2
+        for h in range(heads):
+            pieces = []
+            for m in range(2):
+                lead = dqt_ref[place, h, m * half:m * half + quarter]
+                trail = dqt_ref[place, h, m * half + quarter:(m + 1) * half]
+                pieces.append(lead * cost_ref[place] + trail * sint_ref[place])
+                pieces.append(trail * cost_ref[place] - lead * sint_ref[place])
+            turned = jnp.concatenate(pieces, axis=0) * scale
+            gq_ref[place, :, h * width:(h + 1) * width] = jnp.transpose(turned).astype(BF16)
+        return carry
+
+    lax.fori_loop(0, 1, put, 0)
+    second_copy(slots - 1).start()
+    lax.fori_loop(1, slots, put, 0)
+    finish(slots - 2)
+    weights_finish()
+    finish(slots - 1)
 
 
 def specs(count, smem):
@@ -249,7 +379,7 @@
         pl.BlockSpec(memory_space=pltpu.VMEM)] * (count - smem)
 
 
-def attend(dims, slot_of, part, lam, queries, keys_all, values_all, gain):
+def attend(dims, part, lam, queries, keys_all, values_all, gain):
     slots, parts, heads, tile, width, strip = dims
     return pl.pallas_call(
         partial(attend_kernel, dims),
@@ -259,7 +389,7 @@
             jax.ShapeDtypeStruct((slots, heads, width, tile), F32),
             jax.ShapeDtypeStruct((slots, heads, 1, 2 * tile), F32),
         ),
-        in_specs=specs(7, 3),
+        in_specs=specs(6, 2),
         out_specs=specs(4, 0),
         scratch_shapes=[
             pltpu.VMEM((heads, slots, width, parts * tile), BF16),
@@ -270,39 +400,59 @@
         cost_estimate=pl.CostEstimate(
             flops=20_000_000_000, bytes_accessed=12_000_000, transcendentals=14_000_000),
         name="attend",
-    )(slot_of, part, lam, queries, keys_all, values_all, gain)
-
-
-def attend_back(dims, slot_of, part, lam, queries, keys_all, values_all, gg, gain, mixed, second, lse):
+    )(part, lam, queries, keys_all, values_all, gain)
+
+
+def attend_back(dims, groups, lam, queries, keys_all, values_all, gg, gain, mixed, second,
+                lse, tables, wgrads):
     slots, parts, heads, tile, width, strip = dims
+    assert parts == 4
     full = heads * width
+    kinds, rows, cols = wgrads.shape[0], wgrads.shape[-2], wgrads.shape[-1]
+    rows_low = jax.ShapeDtypeStruct((slots, tile, full), BF16)
     return pl.pallas_call(
-        partial(attend_back_kernel, dims),
+        partial(attend_back_kernel, dims, groups),
         out_shape=(
-            jax.ShapeDtypeStruct((slots, tile, full), F32),
-            jax.ShapeDtypeStruct((parts, slots, tile, full), BF16),
-            jax.ShapeDtypeStruct((parts, slots, tile, full), BF16),
+            rows_low,
+            rows_low,
+            rows_low,
             jax.ShapeDtypeStruct((full, tile), F32),
             jax.ShapeDtypeStruct((heads, width, tile), F32),
+            jax.ShapeDtypeStruct((kinds, rows, cols), F32),
         ),
-        in_specs=specs(11, 3),
-        out_specs=specs(5, 0),
+        in_specs=specs(13, 1) + [pl.BlockSpec(memory_space=pl.ANY)],
+        out_specs=specs(6, 0),
         scratch_shapes=[
-            pltpu.VMEM((heads, slots, width, parts * tile), BF16),
-            pltpu.VMEM((heads, width, 2 * tile), BF16),
-            pltpu.VMEM((heads, 2 * tile, width), BF16),
-            pltpu.VMEM((heads, width, 2 * tile), BF16),
-            pltpu.VMEM((heads, 2 * tile, width), BF16),
-            pltpu.VMEM((heads, 1, 2 * tile), F32),
-            pltpu.VMEM((heads, width, tile), F32),
-            pltpu.VMEM((heads, slots, parts, tile, width), F32),
-            pltpu.VMEM((heads, slots, parts, tile, width), F32),
+            pltpu.VMEM((heads, width, parts * tile), BF16),
+            pltpu.VMEM((slots, heads, width, 2 * tile), BF16),
+            pltpu.VMEM((slots, heads, 2 * tile, width), BF16),
+            pltpu.VMEM((slots, heads, width, 2 * tile), BF16),
+            pltpu.VMEM((slots, heads, 2 * tile, width), BF16),
+            pltpu.VMEM((slots, heads, 1, 2 * tile), F32),
+            pltpu.VMEM((slots, heads, width, tile), F32),
+            pltpu.VMEM((heads, parts, tile, width), F32),
+            pltpu.VMEM((heads, parts, tile, width), F32),
+            pltpu.VMEM((slots, 2, 2, 2, tile, full), BF16),
+            pltpu.VMEM((slots, 2, 2, tile, full), BF16),
+            pltpu.VMEM((slots, 2, tile, full), BF16),
+            pltpu.VMEM((slots, 2, tile, full), BF16),
+            pltpu.VMEM((kinds, groups, rows, cols), BF16),
+            pltpu.VMEM((kinds, groups, rows, cols), BF16),
+            pltpu.VMEM((groups - 1, kinds, rows, cols), BF16),
+            pltpu.SemaphoreType.DMA((slots,)),
+            pltpu.SemaphoreType.DMA((slots,)),
+            pltpu.SemaphoreType.DMA((slots,)),
+            pltpu.SemaphoreType.DMA((slots,)),
+            pltpu.SemaphoreType.DMA((3,)),
+            pltpu.SemaphoreType.DMA((groups - 1,)),
+            pltpu.SemaphoreType.DMA((groups - 1,)),
         ],
-        compiler_params=pltpu.CompilerParams(vmem_limit_bytes=56 << 20),
+        compiler_params=pltpu.CompilerParams(
+            vmem_limit_bytes=60 << 20, collective_id=1, has_side_effects=True),
         cost_estimate=pl.CostEstimate(
             flops=60_000_000_000, bytes_accessed=24_000_000, transcendentals=14_000_000),
         name="attend_back",
-    )(slot_of, part, lam, queries, keys_all, values_all, gg, gain, mixed, second, lse)
+    )(lam, queries, keys_all, values_all, gg, gain, mixed, second, lse, *tables, wgrads)
 
 
 def per_device(
@@ -343,7 +493,17 @@
     slot_of = jnp.argsort(order).astype(jnp.int32)
     index = jnp.arange(tile, dtype=jnp.int32)
     row_offsets = (index // strip) * short_rows + part * strip + index % strip
-    own_places = order[:, None] * block_len + row_offsets[None, :]
+    own_places = jnp.arange(slots, dtype=jnp.int32)[:, None] * block_len + row_offsets[None, :]
+    groups = lax.axis_size("dp") * parts // 2
+    quarter = head_dim // 2
+    frequency = THETA ** (-jnp.arange(quarter, dtype=jnp.float32) / quarter)
+    angles = own_places.astype(F32)[:, None, :] * frequency[None, :, None]
+    cos_turned, sin_turned = jnp.cos(angles), jnp.sin(angles)
+    cos_rows = jnp.tile(cos_turned.transpose(0, 2, 1), (1, 1, 4))
+    sin_rows = jnp.tile(sin_turned.transpose(0, 2, 1), (1, 1, 4))
+    lane = jnp.arange(width)
+    sin_rows = jnp.where(lane % head_dim < quarter, sin_rows, -sin_rows)
+    tables = (cos_turned, sin_turned, cos_rows, sin_rows)
     lambda_one = jnp.exp(jnp.sum(lambda_qone * lambda_kone, axis=-1))
     lambda_two = jnp.exp(jnp.sum(lambda_qtwo * lambda_ktwo, axis=-1))
     lambda_head = lambda_one - lambda_two + LAMBDA_INIT
@@ -353,10 +513,10 @@
     def spread(rows):
         cut = rows.reshape(pair_count, parts, strip, model_width).transpose(1, 0, 2, 3)
         cut = lax.all_to_all(cut, "ctx", 0, 0, tiled=True)
-        return cut.reshape(slots, strip, model_width)
+        return jnp.take(cut.reshape(slots, strip, model_width), slot_of, axis=0)
 
     def unspread(rows):
-        cut = rows.reshape(parts, pair_count, strip, model_width)
+        cut = jnp.take(rows, order, axis=0).reshape(parts, pair_count, strip, model_width)
         cut = lax.all_to_all(cut, "ctx", 0, 0, tiled=True)
         return cut.transpose(1, 0, 2, 3).reshape(1, pair_count, short_rows, model_width)
 
@@ -377,7 +537,7 @@
     part_arr = part.reshape(1).astype(jnp.int32)
     gain_col = group_gain.reshape(qwidth, 1)
     grouped, mixed, second, lse = attend(
-        dims, slot_of, part_arr, lambda_head, queries.reshape(part_shape), keys_all, values_all,
+        dims, part_arr, lambda_head, queries.reshape(part_shape), keys_all, values_all,
         gain_col)
     grouped = grouped.reshape(row_count, qwidth)
     attn_terms = jnp.dot(grouped, output_weight, preferred_element_type=jnp.float32).reshape(
@@ -432,24 +592,17 @@
     ).reshape(row_count, model_width)
     output_term = contract_rows(branch_rows, grouped)
     grad_grouped = contract_cols(output_weight, branch_rows)
-    query_acc, key_acc, value_acc, group_part, lambda_part = attend_back(
-        dims, slot_of, part_arr, lambda_head, queries.reshape(part_shape), keys_all, values_all,
-        grad_grouped, gain_col, mixed, second, lse)
+    shares = lax.axis_size("dp") * parts
+    wgrads = jnp.stack([gate_term.astype(BF16), up_term.astype(BF16), down_term.astype(BF16)])
+    wgrads = wgrads.reshape(3, groups, 2, model_width // shares, wgrads.shape[-1])
+    grad_query, grad_key, grad_value, group_part, lambda_part, feed_sums = attend_back(
+        dims, groups, lambda_head, queries.reshape(part_shape), keys_all, values_all,
+        grad_grouped, gain_col, mixed, second, lse, tables, wgrads)
     group_part = jnp.sum(group_part, axis=1) * SHRINK
     lambda_part = jnp.sum(lambda_part, axis=(1, 2))
-    key_sums = lax.psum_scatter(key_acc, "ctx", scatter_dimension=0).astype(jnp.float32)
-    value_sums = lax.psum_scatter(value_acc, "ctx", scatter_dimension=0)
-    grad_query = (
-        rotate(query_acc.reshape(split_shape), own_places, -1.0)
-        .astype(jnp.bfloat16)
-        .reshape(row_count, qwidth)
-    )
-    grad_key = (
-        rotate(key_sums.reshape(split_shape), own_places, -1.0)
-        .astype(jnp.bfloat16)
-        .reshape(row_count, qwidth)
-    )
-    grad_value = value_sums.reshape(row_count, qwidth)
+    grad_query, grad_key, grad_value = (
+        grad.reshape(row_count, qwidth)
+        for grad in (grad_query, grad_key, grad_value))
     query_term = contract_rows(normed_rows, grad_query)
     key_term = contract_rows(normed_rows, grad_key)
     value_term = contract_rows(normed_rows, grad_value)
@@ -500,9 +653,9 @@
         group_grad,
         over_all(output_term).T,
         feed_sum,
-        over_all(gate_term),
-        over_all(up_term),
-        over_all(down_term).T,
+        feed_sums[0],
+        feed_sums[1],
+        feed_sums[2].T,
     )
 
 

time: 1240 us -> 1070 us (0.86)
  waiting for transfers between devices: 788 us -> 601 us
  Pallas kernels: 148 us -> 189 us
  matrix products: 118 us -> 99.1 us
  blocking collectives: 70.3 us -> 54.6 us
    reduce_scatter x6 -> x4, waiting for transfers between devices: 234 us -> 136 us  [over_all(): lax.psum_scatter(term.astype(jnp.bfloat16), ('dp', 'ctx'), scatter_dimens...]
    reduce_scatter x2 -> x0, waiting for transfers between devices: 44.9 us -> none  [the longest x1 24.6 us: per_device(): value_sums = lax.psum_scatter(value_acc, 'ctx', scatter_dimension=0)]
    pallas_call x1, Pallas kernels: 98.2 us -> 139 us  [attend_back(): pl.pallas_call(partial(attend_back_kernel, dims, groups), out_shape=(rows...]
    all_gather x1, waiting for transfers between devices: 63 us -> 36.2 us  [per_device(): lax.all_gather(grad_hidden.astype(jnp.bfloat16), 'head', axis=1, tiled=True)]
    reduce_scatter x1, waiting for transfers between devices: 55.6 us -> 31.5 us  [per_device(): lax.psum_scatter(normed_terms.astype(jnp.bfloat16), 'head', scatter_dimen...]
    all_to_all x2 -> x1, blocking collectives: 30.4 us -> 14.7 us  [spread(): cut = lax.all_to_all(cut, 'ctx', 0, 0, tiled=True)]
  transfers between devices with their start and end apart: 21 -> 17, of which waited for: 20 -> 16; matrix products, arithmetic and copies ran while one was open for 12% -> 11% of each run, Pallas kernels for 0% -> 0%
where the time goes in v1:
time: 1070 us; the launch traced here: 1060 us
  waiting for transfers between devices  601 us (56%)
  Pallas kernels  189 us (18%)
  matrix products  99.1 us (9%)
  blocking collectives  54.6 us (5%)
  other arithmetic  45.5 us (4%)
  local copies, waits for them, and re-layouts  42.3 us (4%)
  between operations  15.1 us (1%)
  starting transfers between devices  14.2 us (1%)
    pallas_call x1, Pallas kernels, attend_back(): pl.pallas_call(partial(attend_back_kernel, dims, groups), out_shape=(rows...  139 us
    reduce_scatter x4, waiting for transfers between devices, over_all(): lax.psum_scatter(term.astype(jnp.bfloat16), ('dp', 'ctx'), scatter_dimens...  136 us
    all_gather x1, waiting for transfers between devices, per_device(): lax.all_gather(normed, 'head', axis=1, tiled=True)  64.6 us
    reduce_scatter x1, waiting for transfers between devices, per_device(): lax.psum_scatter(attn_terms.astype(jnp.bfloat16), 'head', scatter_dimensi...  60.5 us
    reduce_scatter x1, waiting for transfers between devices, per_device(): lax.psum_scatter(feed_terms.astype(jnp.bfloat16), 'head', scatter_dimensi...  60.5 us
    reduce_scatter x1, waiting for transfers between devices, per_device(): lax.psum_scatter(normed_two_terms.astype(jnp.bfloat16), 'head', scatter_d...  59.2 us
    all_gather x1, waiting for transfers between devices, per_device(): lax.all_gather(cotangent_here, 'head', axis=1, tiled=True)  50.7 us
    pallas_call x1, Pallas kernels, attend(): pl.pallas_call(partial(attend_kernel, dims), out_shape=(jax.ShapeDtypeStr...  49.9 us
  transfers between devices with their start and end apart: 17, of which 16 were waited for; matrix products, arithmetic and copies ran while one was open for 11% of the time, Pallas kernels for 0%

profile of v1, /device:TPU:0, one launch (start us, length us, event | category | flops | bytes accessed | tf_op | source)
XLA Modules:
  0.0 1060.2 jit_solution(688236418343814236)
XLA Ops:
  14.8 11.3 %all-to-all-done = bf16[4,2,32,1536]{3,2,1,0:T(8,128)(2,1)} async-done(((bf16[4,2,32,1536]{3,2,1,0:T(8,128)(2,1)}), bf16[4,2,32,1536]{3,2,1,0:T(8,128)(2,1)}, u32[]{:S(2)}, u32[]{:S(2)}) %all-to-all-start) | async-done | bytes 786464 | tf_op jit(solution)/shard_map/all_to_all | solution.py:515
  33.8 64.6 %all-gather.7.cloned.1.call-done = bf16[8,128,1536]{2,1,0:T(8,128)(2,1)} async-done(((bf16[8,32,1536]{2,1,0:T(8,128)(2,1)}), bf16[8,128,1536]{2,1,0:T(8,128)(2,1)}) %all-gather.7.cloned.1.call-update) | async-done | bytes 3145744 | tf_op jit(solution)/shard_map/all_gather | solution.py:527
  121.7 8.9 all-gather.11.cloned.1.call-done.v_ref
  130.7 30.7 %all-gather.9.cloned.1.call-done.k_ref = bf16[4,8,128,384]{3,2,1,0:T(8,128)(2,1)} async-done(((bf16[1,8,128,384]{3,2,1,0:T(8,128)(2,1)}), bf16[4,8,128,384]{3,2,1,0:T(8,128)(2,1)}) %all-gather.9.cloned.1.call-update) | async-done | bytes 3145744 | tf_op jit(solution)/shard_map/all_gather | solution.py:535
  162.5 49.9 %attend.1 = (bf16[8,128,384]{2,1,0:T(8,128)(2,1)S(1)}, f32[8,3,128,128]{3,2,1,0:T(8,128)S(1)}, f32[8,3,128,128]{3,2,1,0:T(8,128)S(1)}, f32[8,3,1,256]{3,2,1,0:T(1,128)S(1)}) custom-call(s32[1]{0:T(128)} %bitcast.4.part_ref, f32[3]{0:T(128)S(1)} %subtract_add_fusion.lam_ref, bf16[8,128,384]{2,1,0:T(8,128)(2,1)S(1)} %copy-done.1, ...), custom_call_target="tpu_custom_call" | custom-call | flops 20000000000 | bytes 12000000 | tf_op jit(solution)/shard_map/attend/pallas_call | solution.py:384
  219.7 60.5 %reduce-scatter.9.cloned.1.call-done = bf16[8,32,1536]{2,1,0:T(8,128)(2,1)} async-done(((bf16[8,128,1536]{2,1,0:T(8,128)(2,1)}), bf16[8,32,1536]{2,1,0:T(8,128)(2,1)}) %reduce-scatter.9.cloned.1.call-update) | async-done | bytes 786448 | tf_op jit(solution)/shard_map/reduce_scatter | solution.py:546
  284.8 14.7 %all_to_all.20 = bf16[4,2,32,1536]{3,2,1,0:T(8,128)(2,1)} all-to-all(bf16[4,2,32,1536]{3,2,1,0:T(8,128)(2,1)S(1)} %copy.77), channel_id=1, replica_groups=mesh['dp'=2,'ctx'=4,'head'=4] {'ctx'}, dimensions={0} | all-to-all | bytes 1572864 | tf_op jit(solution)/shard_map/all_to_all | solution.py:515
  304.8 42.2 %all-gather.13.cloned.1.call-done = bf16[8,128,1536]{2,1,0:T(8,128)(2,1)} async-done(((bf16[8,32,1536]{2,1,0:T(8,128)(2,1)}), bf16[8,128,1536]{2,1,0:T(8,128)(2,1)}) %all-gather.13.cloned.1.call-update) | async-done | bytes 3145744 | tf_op jit(solution)/shard_map/all_gather | solution.py:552
  347.0 8.4 fusion.34
  360.4 50.7 %all-gather.15.cloned.1.call-done = bf16[8,128,1536]{2,1,0:T(8,128)(2,1)} async-done(((bf16[8,32,1536]{2,1,0:T(8,128)(2,1)}), bf16[8,128,1536]{2,1,0:T(8,128)(2,1)}) %all-gather.15.cloned.1.call-update) | async-done | bytes 3145744 | tf_op jit(solution)/shard_map/all_gather | solution.py:569
  411.1 9.6 multiply_convert_fusion
  429.3 59.2 %reduce-scatter.13.cloned.1.call-done = bf16[8,32,1536]{2,1,0:T(8,128)(2,1)} async-done(((bf16[8,128,1536]{2,1,0:T(8,128)(2,1)}), bf16[8,32,1536]{2,1,0:T(8,128)(2,1)}) %reduce-scatter.13.cloned.1.call-update) | async-done | bytes 786448 | tf_op jit(solution)/shard_map/reduce_scatter | solution.py:583
  503.1 6.2 convolution_convert_fusion.2
  521.1 36.2 %all-gather.17.cloned.1.call-done = bf16[8,128,1536]{2,1,0:T(8,128)(2,1)} async-done(((bf16[8,32,1536]{2,1,0:T(8,128)(2,1)}), bf16[8,128,1536]{2,1,0:T(8,128)(2,1)}) %all-gather.17.cloned.1.call-update) | async-done | bytes 3145744 | tf_op jit(solution)/shard_map/all_gather | solution.py:590
  562.1 138.8 %attend_back.1 = (bf16[8,128,384]{2,1,0:T(8,128)(2,1)}, bf16[8,128,384]{2,1,0:T(8,128)(2,1)}, bf16[8,128,384]{2,1,0:T(8,128)(2,1)}, f32[384,128]{1,0:T(8,128)}, ...) custom-call(f32[3]{0:T(128)} %copy-done.3, bf16[8,128,384]{2,1,0:T(8,128)(2,1)} %copy.74.q_ref, ...), custom_call_target="tpu_custom_call" | custom-call | flops 60000002048 | bytes 24000000 | tf_op jit(solution)/shard_map/attend_back/pallas_call | solution.py:413
  709.9 6.5 convolution_convert_fusion.4
  737.1 31.5 %reduce-scatter.15.cloned.1.call-done = bf16[8,32,1536]{2,1,0:T(8,128)(2,1)} async-done(((bf16[8,128,1536]{2,1,0:T(8,128)(2,1)}), bf16[8,32,1536]{2,1,0:T(8,128)(2,1)}) %reduce-scatter.15.cloned.1.call-update) | async-done | bytes 786448 | tf_op jit(solution)/shard_map/reduce_scatter | solution.py:614
  770.7 60.5 %reduce-scatter.11.cloned.1.call-done = bf16[8,32,1536]{2,1,0:T(8,128)(2,1)} async-done(((bf16[8,128,1536]{2,1,0:T(8,128)(2,1)}), bf16[8,32,1536]{2,1,0:T(8,128)(2,1)}) %reduce-scatter.11.cloned.1.call-update) | async-done | bytes 786448 | tf_op jit(solution)/shard_map/reduce_scatter | solution.py:565
  851.7 21.3 %reduce-scatter.17.cloned.1.call-done = bf16[192,384]{1,0:T(8,128)(2,1)} async-done(((bf16[1536,384]{1,0:T(8,128)(2,1)}), bf16[192,384]{1,0:T(8,128)(2,1)}) %reduce-scatter.17.cloned.1.call-update) | async-done | bytes 147472 | tf_op jit(solution)/shard_map/reduce_scatter | solution.py:638
  874.7 38.2 %reduce-scatter.19.cloned.1.call-done = bf16[192,384]{1,0:T(8,128)(2,1)} async-done(((bf16[1536,384]{1,0:T(8,128)(2,1)}), bf16[192,384]{1,0:T(8,128)(2,1)}) %reduce-scatter.19.cloned.1.call-update) | async-done | bytes 147472 | tf_op jit(solution)/shard_map/reduce_scatter | solution.py:638
  914.5 38.3 %reduce-scatter.21.cloned.1.call-done = bf16[192,384]{1,0:T(8,128)(2,1)} async-done(((bf16[1536,384]{1,0:T(8,128)(2,1)}), bf16[192,384]{1,0:T(8,128)(2,1)}) %reduce-scatter.21.cloned.1.call-update) | async-done | bytes 147472 | tf_op jit(solution)/shard_map/reduce_scatter | solution.py:638
  954.4 38.2 %reduce-scatter.23.cloned.1.call-done = bf16[192,384]{1,0:T(8,128)(2,1)} async-done(((bf16[1536,384]{1,0:T(8,128)(2,1)}), bf16[192,384]{1,0:T(8,128)(2,1)}) %reduce-scatter.23.cloned.1.call-update) | async-done | bytes 147472 | tf_op jit(solution)/shard_map/reduce_scatter | solution.py:638
  994.2 39.9 %all-reduce = (f32[1536]{0:T(1024)}, f32[12]{0:T(128)S(1)}, f32[1536]{0:T(1024)S(1)}, f32[1536]{0:T(1024)}) all-reduce(f32[1536]{0:T(1024)S(1)} %get-tuple-element.41, f32[12]{0:T(128)S(1)} %dynamic_update_slice.6, f32[1536]{0:T(1024)S(1)} %multiply_dynamic-update-slice_fusion, ...), channel_id=1, replica_groups=mesh['dp'=2,'ctx'=4,'head'=4] {'dp','ctx','head'}, use_global_device_ids=true, to_apply=%region_12.14 | all-reduce | flops 4620 | bytes 36960 | tf_op jit(solution)/shard_map/psum | solution.py:627
  1042.4 8.2 all-to-all-done.3
  (227 shorter events, 170.7 us)
Async XLA Ops:
  7.2 404.0 %copy-start = (bf16[1024,1536]{1,0:T(8,128)(2,1)S(1)}, bf16[1024,1536]{1,0:T(8,128)(2,1)}, u32[]{:S(2)}) copy-start(bf16[1024,1536]{1,0:T(8,128)(2,1)} %param.34) | copy-start | bytes 9437188
  9.4 16.7 %all-to-all-start = ((bf16[4,2,32,1536]{3,2,1,0:T(8,128)(2,1)}), bf16[4,2,32,1536]{3,2,1,0:T(8,128)(2,1)}, u32[]{:S(2)}, u32[]{:S(2)}) async-start(bf16[4,2,32,1536]{3,2,1,0:T(8,128)(2,1)} %copy.70), calls=%async_computation | async-start | bytes 1572864 | tf_op jit(solution)/shard_map/all_to_all | solution.py:515
  13.8 84.6 %all-gather.7.cloned.1.call-start = ((), (), s32[]{:S(2)}) async-start(), calls=%async_computation.12 | async-start | bytes 3932160 | tf_op jit(solution)/shard_map/all_gather | solution.py:527
  33.8 96.9 %all-gather.11.cloned.1.call-start = ((), (), s32[]{:S(2)}) async-start(), calls=%async_computation.14 | async-start | bytes 3932160 | tf_op jit(solution)/shard_map/all_gather | solution.py:536
  103.4 58.0 %all-gather.9.cloned.1.call-start = ((), (), s32[]{:S(2)}) async-start(), calls=%async_computation.13 | async-start | bytes 3932160 | tf_op jit(solution)/shard_map/all_gather | solution.py:535
  119.0 161.2 %reduce-scatter.9.cloned.1.call-start = ((), (), s32[]{:S(2)}) async-start(), calls=%async_computation.15 | async-start | bytes 3932160 | tf_op jit(solution)/shard_map/reduce_scatter | solution.py:546
  219.7 127.3 %all-gather.13.cloned.1.call-start = ((), (), s32[]{:S(2)}) async-start(), calls=%async_computation.16 | async-start | bytes 3932160 | tf_op jit(solution)/shard_map/all_gather | solution.py:552
  283.5 127.6 %all-gather.15.cloned.1.call-start = ((), (), s32[]{:S(2)}) async-start(), calls=%async_computation.18 | async-start | bytes 3932160 | tf_op jit(solution)/shard_map/all_gather | solution.py:569
  304.3 184.2 %reduce-scatter.13.cloned.1.call-start = ((), (), s32[]{:S(2)}) async-start(), calls=%async_computation.19 | async-start | bytes 3932160 | tf_op jit(solution)/shard_map/reduce_scatter | solution.py:583
  429.3 128.1 %all-gather.17.cloned.1.call-start = ((), (), s32[]{:S(2)}) async-start(), calls=%async_computation.20 | async-start | bytes 3932160 | tf_op jit(solution)/shard_map/all_gather | solution.py:590
  493.9 274.7 %reduce-scatter.15.cloned.1.call-start = ((), (), s32[]{:S(2)}) async-start(), calls=%async_computation.21 | async-start | bytes 3932160 | tf_op jit(solution)/shard_map/reduce_scatter | solution.py:614
  709.8 121.3 %reduce-scatter.11.cloned.1.call-start = ((), (), s32[]{:S(2)}) async-start(), calls=%async_computation.17 | async-start | bytes 3932160 | tf_op jit(solution)/shard_map/reduce_scatter | solution.py:565
  716.4 156.7 %reduce-scatter.17.cloned.1.call-start = ((), (), s32[]{:S(2)}) async-start(), calls=%async_computation.22 | async-start | bytes 1327104 | tf_op jit(solution)/shard_map/reduce_scatter | solution.py:638
  721.4 191.5 %reduce-scatter.19.cloned.1.call-start = ((), (), s32[]{:S(2)}) async-start(), calls=%async_computation.23 | async-start | bytes 1327104 | tf_op jit(solution)/shard_map/reduce_scatter | solution.py:638
  726.5 226.3 %reduce-scatter.21.cloned.1.call-start = ((), (), s32[]{:S(2)}) async-start(), calls=%async_computation.24 | async-start | bytes 1327104 | tf_op jit(solution)/shard_map/reduce_scatter | solution.py:638
  731.5 261.1 %reduce-scatter.23.cloned.1.call-start = ((), (), s32[]{:S(2)}) async-start(), calls=%async_computation.25 | async-start | bytes 1327104 | tf_op jit(solution)/shard_map/reduce_scatter | solution.py:638
  843.9 190.8 %all-to-all-start.1 = ((bf16[4,2,32,1536]{3,2,1,0:T(8,128)(2,1)}), bf16[4,2,32,1536]{3,2,1,0:T(8,128)(2,1)}, u32[]{:S(2)}, u32[]{:S(2)}) async-start(bf16[4,2,32,1536]{3,2,1,0:T(8,128)(2,1)} %bitcast.135), calls=%async_computation.3 | async-start | bytes 1572864 | tf_op jit(solution)/shard_map/all_to_all | solution.py:520
  851.7 187.3 %copy-start.38 = (f32[3]{0:T(128)S(1)}, f32[3]{0:T(128)}, u32[]{:S(2)}) copy-start(f32[3]{0:T(128)} %copy-done.37) | copy-start | bytes 40
  851.7 187.3 %copy-start.40 = (f32[3]{0:T(128)S(1)}, f32[3]{0:T(128)}, u32[]{:S(2)}) copy-start(f32[3]{0:T(128)} %copy-done.39) | copy-start | bytes 40
  851.7 187.4 %copy-start.29 = (f32[3,64]{1,0:T(4,128)S(1)}, f32[3,64]{1,0:T(4,128)}, u32[]{:S(2)}) copy-start(f32[3,64]{1,0:T(4,128)} %param.27) | copy-start | bytes 2308
  851.7 187.4 %copy-start.31 = (f32[3,64]{1,0:T(4,128)S(1)}, f32[3,64]{1,0:T(4,128)}, u32[]{:S(2)}) copy-start(f32[3,64]{1,0:T(4,128)} %param.28) | copy-start | bytes 2308
  851.7 188.0 %copy-start.33 = (f32[3,64]{1,0:T(4,128)S(1)}, f32[3,64]{1,0:T(4,128)}, u32[]{:S(2)}) copy-start(f32[3,64]{1,0:T(4,128)} %param.25) | copy-start | bytes 2308
  851.7 188.0 %copy-start.35 = (f32[3,64]{1,0:T(4,128)S(1)}, f32[3,64]{1,0:T(4,128)}, u32[]{:S(2)}) copy-start(f32[3,64]{1,0:T(4,128)} %param.26) | copy-start | bytes 2308
  1034.7 15.9 %all-to-all-start.3 = ((bf16[4,2,32,1536]{3,2,1,0:T(8,128)(2,1)}), bf16[4,2,32,1536]{3,2,1,0:T(8,128)(2,1)}, u32[]{:S(2)}, u32[]{:S(2)}) async-start(bf16[4,2,32,1536]{3,2,1,0:T(8,128)(2,1)} %bitcast.134), calls=%async_computation.7 | async-start | bytes 1572864 | tf_op jit(solution)/shard_map/all_to_all | solution.py:520
  (48 other events, 823.7 us)
Sparse Core Ops, SparseCore 0:
  33.9 64.5 all-gather.6
  103.5 27.1 all-gather.10
  132.8 28.4 all-gather.8
  219.8 60.3 reduce-scatter.8
  283.6 63.3 all-gather.12
  349.0 62.0 all-gather.14
  429.4 59.0 reduce-scatter.12
  494.0 63.3 all-gather.16
  710.0 58.5 reduce-scatter.14
  770.8 60.3 reduce-scatter.10
  834.9 38.0 reduce-scatter.16
  876.1 36.6 reduce-scatter.18
  916.1 36.6 reduce-scatter.20
  955.9 36.6 reduce-scatter.22

commit v2 on v1

--- a/solution.py
+++ b/solution.py
@@ -453,6 +453,285 @@
             flops=60_000_000_000, bytes_accessed=24_000_000, transcendentals=14_000_000),
         name="attend_back",
     )(lam, queries, keys_all, values_all, gg, gain, mixed, second, lse, *tables, wgrads)
+
+
+def dot_turned(left, right):
+    return lax.dot_general(left, right, (((1,), (1,)), ((), ())), preferred_element_type=F32)
+
+
+def dot_rows(left, right):
+    return lax.dot_general(left, right, (((0,), (0,)), ((), ())), preferred_element_type=F32)
+
+
+class LineSum:
+    def __init__(self, axis, size, own, from_left, from_right, sems):
+        self.axis, self.size = axis, size
+        self.me = lax.axis_index(axis)
+        self.own, self.buffers, self.sems = own, (from_left, from_right), sems
+
+    def copy(self, q, t, side):
+        target = self.size - 1 - t + self.me if side == 0 else t - (self.size - 1) + self.me
+        target = jnp.clip(target, 0, self.size - 1)
+        neighbour = jnp.clip(self.me + (1 if side == 0 else -1), 0, self.size - 1)
+        return target, mesh_copy(
+            self.own.at[q, target], self.buffers[side].at[q, t], self.sems.at[0, side, q, t],
+            self.sems.at[1, side, q, t], {self.axis: neighbour})
+
+    def rank(self, side):
+        return self.me if side == 0 else self.size - 1 - self.me
+
+    def step(self, q, t):
+        for side in range(2):
+            rank = self.rank(side)
+            target, copy = self.copy(q, t, side)
+
+            if t > 0:
+                @pl.when((rank <= t) & (rank > 0))
+                def _():
+                    self.copy(q, t - 1, side)[1].wait_recv()
+                    self.own[q, target] = (
+                        self.own[q, target].astype(F32)
+                        + self.buffers[side][q, t - 1].astype(F32)).astype(BF16)
+
+            @pl.when(rank <= t)
+            def _():
+                copy.start()
+
+    def total(self, q, acc):
+        acc[...] = self.own[q, self.me].astype(F32)
+        for side in range(2):
+            @pl.when(self.rank(side) > 0)
+            def _():
+                self.copy(q, self.size - 2, side)[1].wait_recv()
+                acc[...] += self.buffers[side][q, self.size - 2].astype(F32)
+
+    def drain(self, q):
+        for t in range(self.size - 1):
+            for side in range(2):
+                @pl.when(self.rank(side) <= t)
+                def _():
+                    self.copy(q, t, side)[1].wait_send()
+
+
+def line_scratch(chunks, size, rows, width):
+    return [
+        pltpu.VMEM((chunks, size, rows, width), BF16),
+        pltpu.VMEM((chunks, size - 1, rows, width), BF16),
+        pltpu.VMEM((chunks, size - 1, rows, width), BF16),
+        pltpu.VMEM((rows, width), F32),
+        pltpu.SemaphoreType.DMA((2, 2, chunks, size - 1)),
+    ]
+
+
+def finish_kernel(dims, groups, lines, gq_ref, gk_ref, gv_ref, wq_ref, wk_ref, wv_ref, normed_ref,
+                  branch_ref, grouped_ref, inputs_ref, gh_ref, gain_ref, small_ref,
+                  ig_ref, wsum_ref, vec_ref,
+                  own_ref, left_ref, right_ref, acc_ref, line_sem,
+                  wloc_ref, wr1_ref, wr2_ref, mixer_ref, va_ref, vb_ref, vc_ref, v2_ref,
+                  w1_sem, w2_sem, va_sem, vb_sem, vc_sem):
+    slots, parts, heads, tile, width, strip = dims
+    full = heads * width
+    model = normed_ref.shape[-1]
+    chunks = own_ref.shape[0]
+    per = slots // chunks
+    part = lax.axis_index("ctx")
+    row = lax.axis_index("dp")
+    place = lax.axis_index("head")
+    core = part % 2
+    y = part // 2
+    other_core = 1 - core
+    me = row * 2 + y
+    sibling = {"ctx": y * 2 + other_core}
+
+    def group_device(index):
+        return {"dp": index // 2, "ctx": (index % 2) * 2 + core}
+
+    others = [lax.rem(me + step, groups) for step in range(1, groups)]
+    line_others = [lax.rem(place + step, lines) for step in range(1, lines)]
+    greet([sibling] + [group_device(index) for index in others]
+          + [{"head": index} for index in line_others])
+    line = LineSum("head", lines, own_ref, left_ref, right_ref, line_sem)
+    mixer_ref[...] = jnp.zeros_like(mixer_ref)
+    block = 256
+
+    def product(q):
+        grads = [ref[q * per:(q + 1) * per].reshape(per * tile, full)
+                 for ref in (gq_ref, gk_ref, gv_ref)]
+
+        def columns(index, carry):
+            cols = pl.ds(pl.multiple_of(index * block, block), block)
+            terms = dot_turned(grads[0], wq_ref[cols, :])
+            terms += dot_turned(grads[1], wk_ref[cols, :])
+            terms += dot_turned(grads[2], wv_ref[cols, :])
+            terms = terms.astype(BF16)
+            for p in range(per):
+                for z in range(lines):
+                    own_ref[q, z, p * strip:(p + 1) * strip, cols] = (
+                        terms[p * tile + z * strip:p * tile + (z + 1) * strip])
+            return carry
+
+        lax.fori_loop(0, model // block, columns, 0)
+
+    rows = wsum_ref.shape[1]
+    narrow = 128
+
+    def weight_term(kind):
+        rows_ref = branch_ref if kind == 3 else normed_ref
+        grad_ref = (gq_ref, gk_ref, gv_ref, grouped_ref)[kind]
+
+        def columns(index, carry):
+            cols = pl.ds(pl.multiple_of(index * narrow, narrow), narrow)
+            term = jnp.zeros((narrow, full), F32)
+            for s in range(0, slots, 2):
+                left = rows_ref[s:s + 2, :, cols].reshape(2 * tile, narrow)
+                grad = grad_ref[s:s + 2].reshape(2 * tile, full)
+                term += dot(jnp.transpose(left), grad)
+            wloc_ref[kind, cols] = term.astype(BF16)
+            return carry
+
+        lax.fori_loop(0, model // narrow, columns, 0)
+
+    def share(index, which):
+        return pl.ds(pl.multiple_of((index * 2 + which) * rows, 16), rows)
+
+    def weights_out(index):
+        return mesh_copy(wloc_ref.at[:, share(index, other_core)], wr1_ref.at[:, index],
+                         w1_sem.at[0, index], w1_sem.at[1, index], sibling)
+
+    def weights_send(step):
+        index = others[step]
+        return mesh_copy(wloc_ref.at[:, share(index, core)], wr2_ref.at[step], w2_sem.at[0, step],
+                         w2_sem.at[1, step], group_device(index))
+
+    def weights_cross():
+        for index in range(groups):
+            weights_out(index).wait()
+
+        def add(index, carry):
+            for k in range(4):
+                wloc_ref[k, share(index, core)] = (
+                    wloc_ref[k, share(index, core)].astype(F32) + wr1_ref[k, index].astype(F32)
+                ).astype(BF16)
+            return carry
+
+        lax.fori_loop(0, groups, add, 0)
+
+    def weights_finish():
+        for step in range(groups - 1):
+            weights_send(step).wait()
+        for k in range(4):
+            total = wloc_ref[k, share(me, core)].astype(F32)
+            for step in range(groups - 1):
+                total = total + wr2_ref[step, k].astype(F32)
+            wsum_ref[k] = total
+
+    def close(q):
+        line.total(q, acc_ref)
+        grad = acc_ref[...]
+        x = inputs_ref[q * per:(q + 1) * per].reshape(per * strip, model).astype(F32)
+        scale = lax.rsqrt(jnp.mean(x * x, axis=1, keepdims=True) + EPSILON)
+        mixer_ref[...] += jnp.sum((grad * (x * scale)).reshape(per * strip // 8, 8, model), axis=0)
+        up = grad * gain_ref[...]
+        result = (gh_ref[q * per:(q + 1) * per].reshape(per * strip, model) + scale * up
+                  - x * (scale * scale * scale * jnp.mean(up * x, axis=1, keepdims=True)))
+        ig_ref[q * per:(q + 1) * per] = result.astype(BF16).reshape(per, strip, model)
+
+    for slot in range(chunks + lines - 1):
+        if slot < chunks:
+            product(slot)
+        for t in range(lines - 1):
+            if 0 <= slot - t < chunks:
+                line.step(slot - t, t)
+        if slot < 4:
+            weight_term(slot)
+            if slot == 3:
+                for index in range(groups):
+                    weights_out(index).start()
+        if slot == 4:
+            weights_cross()
+        if slot == 5:
+            for step in range(groups - 1):
+                weights_send(step).start()
+        if slot - lines + 1 >= 0:
+            close(slot - lines + 1)
+    first_row = lax.broadcasted_iota(jnp.int32, small_ref.shape, 0) == 0
+    mixer = jnp.broadcast_to(jnp.sum(mixer_ref[...], axis=0, keepdims=True), small_ref.shape)
+    va_ref[0] = jnp.where(first_row, mixer, small_ref[...])
+    for q in range(chunks):
+        line.drain(q)
+    swap = mesh_copy(va_ref.at[0], va_ref.at[1], va_sem.at[0], va_sem.at[1], sibling)
+    swap.start()
+    weights_finish()
+    swap.wait()
+    vb_ref[me] = va_ref[0] + va_ref[1]
+
+    def group_copy(source, target, sem):
+        return mesh_copy(vb_ref.at[source], vb_ref.at[source], vb_sem.at[0, sem],
+                         vb_sem.at[1, source], group_device(target))
+
+    for step, index in enumerate(others):
+        group_copy(me, index, step).start()
+    for step, index in enumerate(others):
+        group_copy(index, index, step).wait_recv()
+    total = vb_ref[0]
+    for index in range(1, groups):
+        total = total + vb_ref[index]
+    vc_ref[place] = total
+    v2_ref[...] = total
+
+    def line_copy(source, target, sem):
+        return mesh_copy(vc_ref.at[source], vc_ref.at[source], vc_sem.at[0, sem],
+                         vc_sem.at[1, source], {"head": target})
+
+    for step, index in enumerate(line_others):
+        line_copy(place, index, step).start()
+    for step, index in enumerate(line_others):
+        line_copy(index, index, step).wait_recv()
+    total = vc_ref[0]
+    for index in range(1, lines):
+        total = total + vc_ref[index]
+    row_index = lax.broadcasted_iota(jnp.int32, total.shape, 0)
+    vec_ref[...] = jnp.where(row_index < 2, total, v2_ref[...])
+    for step, index in enumerate(others):
+        group_copy(me, index, step).wait_send()
+    for step, index in enumerate(line_others):
+        line_copy(place, index, step).wait_send()
+
+
+def finish(dims, groups, lines, chunks, rows, *operands):
+    slots, parts, heads, tile, width, strip = dims
+    full = heads * width
+    model = operands[6].shape[-1]
+    return pl.pallas_call(
+        partial(finish_kernel, dims, groups, lines),
+        out_shape=(
+            jax.ShapeDtypeStruct((slots, strip, model), BF16),
+            jax.ShapeDtypeStruct((4, rows, full), F32),
+            jax.ShapeDtypeStruct((8, model), F32),
+        ),
+        in_specs=specs(13, 0),
+        out_specs=specs(3, 0),
+        scratch_shapes=line_scratch(chunks, lines, slots // chunks * strip, model) + [
+            pltpu.VMEM((4, model, full), BF16),
+            pltpu.VMEM((4, groups, rows, full), BF16),
+            pltpu.VMEM((groups - 1, 4, rows, full), BF16),
+            pltpu.VMEM((8, model), F32),
+            pltpu.VMEM((2, 8, model), F32),
+            pltpu.VMEM((groups, 8, model), F32),
+            pltpu.VMEM((lines, 8, model), F32),
+            pltpu.VMEM((8, model), F32),
+            pltpu.SemaphoreType.DMA((2, groups)),
+            pltpu.SemaphoreType.DMA((2, groups - 1)),
+            pltpu.SemaphoreType.DMA((2,)),
+            pltpu.SemaphoreType.DMA((2, groups)),
+            pltpu.SemaphoreType.DMA((2, lines)),
+        ],
+        compiler_params=pltpu.CompilerParams(
+            vmem_limit_bytes=60 << 20, collective_id=2, has_side_effects=True),
+        cost_estimate=pl.CostEstimate(
+            flops=8_000_000_000, bytes_accessed=24_000_000, transcendentals=0),
+        name="finish",
+    )(*operands)
 
 
 def per_device(
@@ -590,7 +869,6 @@
     branch_rows = lax.all_gather(
         grad_hidden.astype(jnp.bfloat16), "head", axis=1, tiled=True
     ).reshape(row_count, model_width)
-    output_term = contract_rows(branch_rows, grouped)
     grad_grouped = contract_cols(output_weight, branch_rows)
     shares = lax.axis_size("dp") * parts
     wgrads = jnp.stack([gate_term.astype(BF16), up_term.astype(BF16), down_term.astype(BF16)])
@@ -600,59 +878,37 @@
         grad_grouped, gain_col, mixed, second, lse, tables, wgrads)
     group_part = jnp.sum(group_part, axis=1) * SHRINK
     lambda_part = jnp.sum(lambda_part, axis=(1, 2))
-    grad_query, grad_key, grad_value = (
-        grad.reshape(row_count, qwidth)
-        for grad in (grad_query, grad_key, grad_value))
-    query_term = contract_rows(normed_rows, grad_query)
-    key_term = contract_rows(normed_rows, grad_key)
-    value_term = contract_rows(normed_rows, grad_value)
-    normed_terms = (
-        contract_cols(grad_query, query_weight)
-        + contract_cols(grad_key, key_weight)
-        + contract_cols(grad_value, value_weight)
-    ).reshape(rows_shape)
-    grad_normed = lax.psum_scatter(
-        normed_terms.astype(jnp.bfloat16), "head", scatter_dimension=1, tiled=True
-    ).astype(jnp.float32)
-    mixer_part = jnp.sum(grad_normed * tokens * scale_one, axis=(0, 1))
-    input_grad = grad_hidden + norm_back(grad_normed, tokens, scale_one, mixer_gain)
+    third = jnp.pad(
+        jnp.concatenate([group_part, lambda_part]), (0, model_width - qwidth - heads_here))
+    small = jnp.pad(jnp.stack([jnp.zeros_like(feed_part), feed_part, third]), ((0, 5), (0, 0)))
+    grad_rows_shape = (slots, tile, model_width)
+    input_grad, attn_sums, vectors = finish(
+        dims, groups, head_total, 4, model_width // shares, grad_query, grad_key, grad_value,
+        query_weight, key_weight, value_weight, normed_rows.reshape(grad_rows_shape),
+        branch_rows.reshape(grad_rows_shape), grouped.reshape(part_shape), inputs_here,
+        grad_hidden, mixer_gain.reshape(1, model_width), small)
     block_out = unspread(block_out)
-    input_grad = unspread(input_grad.astype(BF16)).astype(F32)
-    group_full = lax.dynamic_update_slice(
-        jnp.zeros((qwidth * head_total,), jnp.float32), group_part, (head_place * qwidth,)
-    )
-    lambda_full = lax.dynamic_update_slice(
-        jnp.zeros((heads_here * head_total,), jnp.float32), lambda_part, (head_place * heads_here,)
-    )
-    mixer_sum, feed_sum, group_sum, lambda_sum = lax.psum(
-        (mixer_part, feed_part, group_full, lambda_full), ("dp", "ctx", "head")
-    )
-    group_grad = lax.dynamic_slice(group_sum, (head_place * qwidth,), (qwidth,))
-    lambda_grad = lax.dynamic_slice(lambda_sum, (head_place * heads_here,), (heads_here,))
+    input_grad = unspread(input_grad).astype(F32)
+    group_grad = vectors[2, :qwidth]
+    lambda_grad = vectors[2, qwidth:qwidth + heads_here]
     qone_grad = (lambda_grad * lambda_one)[:, None] * lambda_kone
     kone_grad = (lambda_grad * lambda_one)[:, None] * lambda_qone
     qtwo_grad = -(lambda_grad * lambda_two)[:, None] * lambda_ktwo
     ktwo_grad = -(lambda_grad * lambda_two)[:, None] * lambda_qtwo
-
-    def over_all(term):
-        return lax.psum_scatter(
-            term.astype(jnp.bfloat16), ("dp", "ctx"), scatter_dimension=0, tiled=True
-        ).astype(jnp.float32)
-
     return (
         block_out,
         input_grad,
-        mixer_sum,
-        over_all(query_term),
-        over_all(key_term),
-        over_all(value_term),
+        vectors[0],
+        attn_sums[0],
+        attn_sums[1],
+        attn_sums[2],
         qone_grad,
         kone_grad,
         qtwo_grad,
         ktwo_grad,
         group_grad,
-        over_all(output_term).T,
-        feed_sum,
+        attn_sums[3].T,
+        vectors[1],
         feed_sums[0],
         feed_sums[1],
         feed_sums[2].T,

time: 1070 us -> 907 us (0.85)
  waiting for transfers between devices: 601 us -> 427 us
  Pallas kernels: 189 us -> 280 us
  blocking collectives: 54.6 us -> 14.8 us
  matrix products: 99.1 us -> 79.2 us
  other arithmetic: 45.5 us -> 30.3 us
    reduce_scatter x5 -> x0, waiting for transfers between devices: 167 us -> none  [the longest x4 136 us: over_all(): lax.psum_scatter(term.astype(jnp.bfloat16), ('dp', 'ctx'), scatter_dimens...]
    pallas_call x0 -> x1, Pallas kernels: none -> 90.9 us  [finish(): pl.pallas_call(partial(finish_kernel, dims, groups, lines), out_shape=(ja...]
    psum x1 -> x0, blocking collectives: 39.9 us -> none  [per_device(): lax.psum((mixer_part, feed_part, group_full, lambda_full), ('dp', 'ctx',...]
    dot_general x7 -> x3, matrix products: 33.5 us -> 22.4 us  [contract_rows(): lax.dot_general(left, right, (((0,), (0,)), ((), ())), preferred_element_...]
    dot_general x7 -> x4, matrix products: 31.6 us -> 22.9 us  [contract_cols(): lax.dot_general(left, right, (((1,), (1,)), ((), ())), preferred_element_...]
  transfers between devices with their start and end apart: 17 -> 12, of which waited for: 16 -> 12; matrix products, arithmetic and copies ran while one was open for 11% -> 10% of each run, Pallas kernels for 0% -> 0%
where the time goes in v2:
time: 907 us; the launch traced here: 898 us
  waiting for transfers between devices  427 us (47%)
  Pallas kernels  280 us (31%)
  matrix products  79.2 us (9%)
  local copies, waits for them, and re-layouts  39.4 us (4%)
  other arithmetic  30.3 us (3%)
  blocking collectives  14.8 us (2%)
  between operations  14.7 us (2%)
  starting transfers between devices  12.7 us (1%)
    pallas_call x1, Pallas kernels, attend_back(): pl.pallas_call(partial(attend_back_kernel, dims, groups), out_shape=(rows...  139 us
    pallas_call x1, Pallas kernels, finish(): pl.pallas_call(partial(finish_kernel, dims, groups, lines), out_shape=(ja...  90.9 us
    all_gather x1, waiting for transfers between devices, per_device(): lax.all_gather(normed, 'head', axis=1, tiled=True)  64.6 us
    reduce_scatter x1, waiting for transfers between devices, per_device(): lax.psum_scatter(feed_terms.astype(jnp.bfloat16), 'head', scatter_dimensi...  60.9 us
    reduce_scatter x1, waiting for transfers between devices, per_device(): lax.psum_scatter(attn_terms.astype(jnp.bfloat16), 'head', scatter_dimensi...  60.5 us
    reduce_scatter x1, waiting for transfers between devices, per_device(): lax.psum_scatter(normed_two_terms.astype(jnp.bfloat16), 'head', scatter_d...  52.7 us
    all_gather x1, waiting for transfers between devices, per_device(): lax.all_gather(cotangent_here, 'head', axis=1, tiled=True)  50.7 us
    pallas_call x1, Pallas kernels, attend(): pl.pallas_call(partial(attend_kernel, dims), out_shape=(jax.ShapeDtypeStr...  49.8 us
  transfers between devices with their start and end apart: 12, of which 12 were waited for; matrix products, arithmetic and copies ran while one was open for 10% of the time, Pallas kernels for 0%

profile of v2, /device:TPU:0, one launch (start us, length us, event | category | flops | bytes accessed | tf_op | source)
XLA Modules:
  0.0 897.7 jit_solution(16507602684707173821)
XLA Ops:
  14.8 11.3 %all-to-all-done = bf16[4,2,32,1536]{3,2,1,0:T(8,128)(2,1)} async-done(((bf16[4,2,32,1536]{3,2,1,0:T(8,128)(2,1)}), bf16[4,2,32,1536]{3,2,1,0:T(8,128)(2,1)}, u32[]{:S(2)}, u32[]{:S(2)}) %all-to-all-start) | async-done | bytes 786464 | tf_op jit(solution)/shard_map/all_to_all | solution.py:794
  32.4 64.6 %all-gather.7.cloned.1.call-done.normed_ref = bf16[8,128,1536]{2,1,0:T(8,128)(2,1)} async-done(((bf16[8,32,1536]{2,1,0:T(8,128)(2,1)}), bf16[8,128,1536]{2,1,0:T(8,128)(2,1)}) %all-gather.7.cloned.1.call-update) | async-done | bytes 3145744 | tf_op jit(solution)/shard_map/all_gather | solution.py:806
  97.0 4.9 convolution_convert_fusion.5
  120.7 8.5 all-gather.11.cloned.1.call-done.v_ref
  129.2 30.7 %all-gather.9.cloned.1.call-done.k_ref = bf16[4,8,128,384]{3,2,1,0:T(8,128)(2,1)} async-done(((bf16[1,8,128,384]{3,2,1,0:T(8,128)(2,1)}), bf16[4,8,128,384]{3,2,1,0:T(8,128)(2,1)}) %all-gather.9.cloned.1.call-update) | async-done | bytes 3145744 | tf_op jit(solution)/shard_map/all_gather | solution.py:814
  161.0 49.8 %attend.1 = (bf16[8,128,384]{2,1,0:T(8,128)(2,1)S(1)}, f32[8,3,128,128]{3,2,1,0:T(8,128)S(1)}, f32[8,3,128,128]{3,2,1,0:T(8,128)S(1)}, f32[8,3,1,256]{3,2,1,0:T(1,128)S(1)}) custom-call(s32[1]{0:T(128)} %bitcast.4.part_ref, f32[3]{0:T(128)S(1)} %subtract_add_fusion.lam_ref, bf16[8,128,384]{2,1,0:T(8,128)(2,1)S(1)} %copy-done.2, ...), custom_call_target="tpu_custom_call" | custom-call | flops 20000000000 | bytes 12000000 | tf_op jit(solution)/shard_map/attend/pallas_call | solution.py:384
  218.2 60.5 %reduce-scatter.4.cloned.1.call-done = bf16[8,32,1536]{2,1,0:T(8,128)(2,1)} async-done(((bf16[8,128,1536]{2,1,0:T(8,128)(2,1)}), bf16[8,32,1536]{2,1,0:T(8,128)(2,1)}) %reduce-scatter.4.cloned.1.call-update) | async-done | bytes 786448 | tf_op jit(solution)/shard_map/reduce_scatter | solution.py:825
  283.1 14.8 %all_to_all.20 = bf16[4,2,32,1536]{3,2,1,0:T(8,128)(2,1)} all-to-all(bf16[4,2,32,1536]{3,2,1,0:T(8,128)(2,1)S(1)} %copy.77), channel_id=1, replica_groups=mesh['dp'=2,'ctx'=4,'head'=4] {'ctx'}, dimensions={0} | all-to-all | bytes 1572864 | tf_op jit(solution)/shard_map/all_to_all | solution.py:794
  302.9 42.4 %all-gather.13.cloned.1.call-done = bf16[8,128,1536]{2,1,0:T(8,128)(2,1)} async-done(((bf16[8,32,1536]{2,1,0:T(8,128)(2,1)}), bf16[8,128,1536]{2,1,0:T(8,128)(2,1)}) %all-gather.13.cloned.1.call-update) | async-done | bytes 3145744 | tf_op jit(solution)/shard_map/all_gather | solution.py:831
  345.3 8.4 fusion.24
  353.8 5.0 fusion.23
  358.8 50.7 %all-gather.15.cloned.1.call-done = bf16[8,128,1536]{2,1,0:T(8,128)(2,1)} async-done(((bf16[8,32,1536]{2,1,0:T(8,128)(2,1)}), bf16[8,128,1536]{2,1,0:T(8,128)(2,1)}) %all-gather.15.cloned.1.call-update) | async-done | bytes 3145744 | tf_op jit(solution)/shard_map/all_gather | solution.py:848
  409.5 9.6 %multiply_convert_fusion = (bf16[1024,1024]{1,0:T(8,128)(2,1)S(1)}, bf16[1024,1024]{1,0:T(8,128)(2,1)S(1)}, bf16[1024,1024]{1,0:T(8,128)(2,1)}) fusion(f32[1024,1024]{1,0:T(8,128)} %fusion.23, f32[1024,1024]{1,0:T(8,128)} %fusion.24, bf16[1024,1536]{1,0:T(8,128)(2,1)} %bitcast.128, bf16[1024,1536]{1,0:T(8,128)(2,1)S(1)} %copy-done), kind=kOutput, calls=%fused_computation.6 | convolution fusion | flops 3236954112 | bytes 20971520 | tf_op jit(solution)/shard_map/dot_general | solution.py:52
  422.5 5.1 add_convert_fusion
  427.7 6.4 convolution_convert_fusion.4
  434.2 52.7 %reduce-scatter.8.cloned.1.call-done = bf16[8,32,1536]{2,1,0:T(8,128)(2,1)} async-done(((bf16[8,128,1536]{2,1,0:T(8,128)(2,1)}), bf16[8,32,1536]{2,1,0:T(8,128)(2,1)}) %reduce-scatter.8.cloned.1.call-update) | async-done | bytes 786448 | tf_op jit(solution)/shard_map/reduce_scatter | solution.py:862
  488.6 60.9 %reduce-scatter.6.cloned.1.call-done = bf16[8,32,1536]{2,1,0:T(8,128)(2,1)} async-done(((bf16[8,128,1536]{2,1,0:T(8,128)(2,1)}), bf16[8,32,1536]{2,1,0:T(8,128)(2,1)}) %reduce-scatter.6.cloned.1.call-update) | async-done | bytes 786448 | tf_op jit(solution)/shard_map/reduce_scatter | solution.py:844
  557.2 6.2 convolution_convert_fusion.1
  563.5 12.4 %convolution_convert_fusion.2 = bf16[1536,1024]{1,0:T(8,128)(2,1)S(1)} fusion(bf16[1024,1536]{1,0:T(8,128)(2,1)S(1)} %bitcast.126, bf16[1024,1024]{1,0:T(8,128)(2,1)S(1)} %copy-done.46), kind=kOutput, calls=%fused_computation.13 | convolution fusion | flops 3222798336 | bytes 8388608 | tf_op jit(solution)/shard_map/dot_general | solution.py:46
  585.7 31.0 %all-gather.17.cloned.1.call-done.branch_ref = bf16[8,128,1536]{2,1,0:T(8,128)(2,1)} async-done(((bf16[8,32,1536]{2,1,0:T(8,128)(2,1)}), bf16[8,128,1536]{2,1,0:T(8,128)(2,1)}) %all-gather.17.cloned.1.call-update) | async-done | bytes 3145744 | tf_op jit(solution)/shard_map/all_gather | solution.py:869
  621.5 138.8 %attend_back.1 = (bf16[8,128,384]{2,1,0:T(8,128)(2,1)}, bf16[8,128,384]{2,1,0:T(8,128)(2,1)}, bf16[8,128,384]{2,1,0:T(8,128)(2,1)}, f32[384,128]{1,0:T(8,128)}, ...) custom-call(f32[3]{0:T(128)} %copy-done.4, bf16[8,128,384]{2,1,0:T(8,128)(2,1)} %copy.74.q_ref, ...), custom_call_target="tpu_custom_call" | custom-call | flops 60000002048 | bytes 24000000 | tf_op jit(solution)/shard_map/attend_back/pallas_call | solution.py:413
  763.1 90.9 %finish.1 = (bf16[8,32,1536]{2,1,0:T(8,128)(2,1)}, f32[4,192,384]{2,1,0:T(8,128)}, f32[8,1536]{1,0:T(8,128)}) custom-call(bf16[8,128,384]{2,1,0:T(8,128)(2,1)} %get-tuple-element.36.gq_ref, bf16[8,128,384]{2,1,0:T(8,128)(2,1)} %get-tuple-element.37.gk_ref, bf16[8,128,384]{2,1,0:T(8,128)(2,1)} %get-tuple-element.38.gv_ref, bf16[1536,384]{1,0:T(8,128)(2,1)} %wq_ref.1, ...), custom_call_target="tpu_custom_call" | custom-call | flops 8000000000 | bytes 24000000 | tf_op jit(solution)/shard_map/finish/pallas_call | solution.py:705
  864.4 7.9 all-to-all-done.1
  882.5 5.7 all-to-all-done.3
  (188 shorter events, 103.8 us)
Async XLA Ops:
  7.2 402.3 %copy-start = (bf16[1024,1536]{1,0:T(8,128)(2,1)S(1)}, bf16[1024,1536]{1,0:T(8,128)(2,1)}, u32[]{:S(2)}) copy-start(bf16[1024,1536]{1,0:T(8,128)(2,1)} %param.34) | copy-start | bytes 9437188
  9.4 21.7 %copy-start.21 = (f32[1536]{0:T(1024)S(1)}, f32[1536]{0:T(1024)}, u32[]{:S(2)}) copy-start(f32[1536]{0:T(1024)} %param.21) | copy-start | bytes 18436
  9.4 16.7 %all-to-all-start = ((bf16[4,2,32,1536]{3,2,1,0:T(8,128)(2,1)}), bf16[4,2,32,1536]{3,2,1,0:T(8,128)(2,1)}, u32[]{:S(2)}, u32[]{:S(2)}) async-start(bf16[4,2,32,1536]{3,2,1,0:T(8,128)(2,1)} %copy.70), calls=%async_computation | async-start | bytes 1572864 | tf_op jit(solution)/shard_map/all_to_all | solution.py:794
  13.8 83.2 %all-gather.7.cloned.1.call-start = ((), (), s32[]{:S(2)}) async-start(), calls=%async_computation.7 | async-start | bytes 3932160 | tf_op jit(solution)/shard_map/all_gather | solution.py:806
  32.3 96.9 %all-gather.11.cloned.1.call-start = ((), (), s32[]{:S(2)}) async-start(), calls=%async_computation.9 | async-start | bytes 3932160 | tf_op jit(solution)/shard_map/all_gather | solution.py:815
  101.9 58.0 %all-gather.9.cloned.1.call-start = ((), (), s32[]{:S(2)}) async-start(), calls=%async_computation.8 | async-start | bytes 3932160 | tf_op jit(solution)/shard_map/all_gather | solution.py:814
  117.5 161.3 %reduce-scatter.4.cloned.1.call-start = ((), (), s32[]{:S(2)}) async-start(), calls=%async_computation.10 | async-start | bytes 3932160 | tf_op jit(solution)/shard_map/reduce_scatter | solution.py:825
  117.7 93.2 %copy-start.3 = (f32[384,1]{1,0:T(8,128)}, f32[384,1]{1,0:T(8,128)S(1)}, u32[]{:S(2)}) copy-start(f32[384,1]{1,0:T(8,128)S(1)} %reshape.353.gain_ref) | copy-start | bytes 4612
  117.9 93.0 %copy-start.31 = (f32[3]{0:T(128)}, f32[3]{0:T(128)S(1)}, u32[]{:S(2)}) copy-start(f32[3]{0:T(128)S(1)} %get-tuple-element.84) | copy-start | bytes 40
  118.4 92.5 %copy-start.4 = (f32[3]{0:T(128)}, f32[3]{0:T(128)S(1)}, u32[]{:S(2)}) copy-start(f32[3]{0:T(128)S(1)} %subtract_add_fusion.lam_ref) | copy-start | bytes 40
  161.0 53.7 %copy-start.41 = (bf16[384,1536]{1,0:T(8,128)(2,1)S(1)}, bf16[384,1536]{1,0:T(8,128)(2,1)}, u32[]{:S(2)}) copy-start(bf16[384,1536]{1,0:T(8,128)(2,1)} %param.30) | copy-start | bytes 3538948
  218.2 62.4 %copy-start.20 = (f32[1536]{0:T(1024)S(1)}, f32[1536]{0:T(1024)}, u32[]{:S(2)}) copy-start(f32[1536]{0:T(1024)} %param.31) | copy-start | bytes 18436
  218.2 127.1 %all-gather.13.cloned.1.call-start = ((), (), s32[]{:S(2)}) async-start(), calls=%async_computation.11 | async-start | bytes 3932160 | tf_op jit(solution)/shard_map/all_gather | solution.py:831
  281.8 127.6 %all-gather.15.cloned.1.call-start = ((), (), s32[]{:S(2)}) async-start(), calls=%async_computation.13 | async-start | bytes 3932160 | tf_op jit(solution)/shard_map/all_gather | solution.py:848
  302.6 184.2 %reduce-scatter.8.cloned.1.call-start = ((), (), s32[]{:S(2)}) async-start(), calls=%async_computation.14 | async-start | bytes 3932160 | tf_op jit(solution)/shard_map/reduce_scatter | solution.py:862
  427.6 121.9 %reduce-scatter.6.cloned.1.call-start = ((), (), s32[]{:S(2)}) async-start(), calls=%async_computation.12 | async-start | bytes 3932160 | tf_op jit(solution)/shard_map/reduce_scatter | solution.py:844
  434.1 52.8 %copy-start.11 = (bf16[8,32,1536]{2,1,0:T(8,128)(2,1)S(1)}, bf16[8,32,1536]{2,1,0:T(8,128)(2,1)}, u32[]{:S(2)}) copy-start(bf16[8,32,1536]{2,1,0:T(8,128)(2,1)} %copy-done.9) | copy-start | bytes 2359300
  434.1 52.8 %copy-start.13 = (bf16[8,32,1536]{2,1,0:T(8,128)(2,1)S(1)}, bf16[8,32,1536]{2,1,0:T(8,128)(2,1)}, u32[]{:S(2)}) copy-start(bf16[8,32,1536]{2,1,0:T(8,128)(2,1)} %reduce-scatter.4.cloned.1.call-done) | copy-start | bytes 2359300
  434.1 115.4 %copy-start.14 = (bf16[8,32,1536]{2,1,0:T(8,128)(2,1)S(1)}, bf16[8,32,1536]{2,1,0:T(8,128)(2,1)}, u32[]{:S(2)}) copy-start(bf16[8,32,1536]{2,1,0:T(8,128)(2,1)} %gather_fusion.2) | copy-start | bytes 2359300
  434.1 182.5 %all-gather.17.cloned.1.call-start = ((), (), s32[]{:S(2)}) async-start(), calls=%async_computation.15 | async-start | bytes 3932160 | tf_op jit(solution)/shard_map/all_gather | solution.py:869
  486.8 62.6 %copy-start.15 = (bf16[8,32,1536]{2,1,0:T(8,128)(2,1)S(1)}, bf16[8,32,1536]{2,1,0:T(8,128)(2,1)}, u32[]{:S(2)}) copy-start(bf16[8,32,1536]{2,1,0:T(8,128)(2,1)} %reduce-scatter.8.cloned.1.call-done) | copy-start | bytes 2359300
  857.2 15.1 %all-to-all-start.1 = ((bf16[4,2,32,1536]{3,2,1,0:T(8,128)(2,1)}), bf16[4,2,32,1536]{3,2,1,0:T(8,128)(2,1)S(1)}, u32[]{:S(2)}, u32[]{:S(2)}) async-start(bf16[4,2,32,1536]{3,2,1,0:T(8,128)(2,1)} %bitcast.21), calls=%async_computation.3 | async-start | bytes 1572864 | tf_op jit(solution)/shard_map/all_to_all | solution.py:799
  860.7 19.3 %copy-start.16 = (f32[3,192,1024]{2,1,0:T(8,128)S(1)}, f32[3,192,1024]{2,1,0:T(8,128)}, u32[]{:S(2)}) copy-start(f32[3,192,1024]{2,1,0:T(8,128)} %get-tuple-element.44) | copy-start | bytes 7077892
  872.3 15.9 %all-to-all-start.3 = ((bf16[4,2,32,1536]{3,2,1,0:T(8,128)(2,1)}), bf16[4,2,32,1536]{3,2,1,0:T(8,128)(2,1)}, u32[]{:S(2)}, u32[]{:S(2)}) async-start(bf16[4,2,32,1536]{3,2,1,0:T(8,128)(2,1)} %bitcast.36), calls=%async_computation.6 | async-start | bytes 1572864 | tf_op jit(solution)/shard_map/all_to_all | solution.py:799
  (35 other events, 159.9 us)
Sparse Core Ops, SparseCore 0:
  32.4 64.5 all-gather.6
  102.0 27.1 all-gather.10
  131.4 28.4 all-gather.8
  218.3 60.4 reduce-scatter.3
  282.0 63.3 all-gather.12
  347.3 62.0 all-gather.14
  427.7 59.0 reduce-scatter.7
  489.1 60.3 reduce-scatter.5
  553.3 63.3 all-gather.16

commit v3 on v2

--- a/solution.py
+++ b/solution.py
@@ -804,6 +804,8 @@
     scale_one = rms_scale(tokens)
     normed = (tokens * scale_one * mixer_gain).astype(jnp.bfloat16)
     normed_rows = lax.all_gather(normed, "head", axis=1, tiled=True).reshape(row_count, model_width)
+    cotangent_here = spread(cotangent)
+    normed_rows, cotangent_here = lax.optimization_barrier((normed_rows, cotangent_here))
     query_lin = jnp.dot(normed_rows, query_weight, preferred_element_type=jnp.float32)
     key_lin = jnp.dot(normed_rows, key_weight, preferred_element_type=jnp.float32)
     value_lin = jnp.dot(normed_rows, value_weight, preferred_element_type=jnp.float32)
@@ -813,19 +815,22 @@
     part_shape = (slots, tile, qwidth)
     keys_all = lax.all_gather(keys_own.reshape(part_shape), "ctx", axis=0)
     values_all = lax.all_gather(values_own.reshape(part_shape), "ctx", axis=0)
+    keys_all, values_all, late = lax.optimization_barrier((keys_all, values_all, cotangent_here))
+    grad_rows = lax.all_gather(late, "head", axis=1, tiled=True)
     part_arr = part.reshape(1).astype(jnp.int32)
     gain_col = group_gain.reshape(qwidth, 1)
     grouped, mixed, second, lse = attend(
         dims, part_arr, lambda_head, queries.reshape(part_shape), keys_all, values_all,
         gain_col)
+    grouped, grad_rows = lax.optimization_barrier((grouped, grad_rows))
     grouped = grouped.reshape(row_count, qwidth)
+    grad_rows = grad_rows.reshape(row_count, model_width)
     attn_terms = jnp.dot(grouped, output_weight, preferred_element_type=jnp.float32).reshape(
         rows_shape
     )
     hidden = tokens + lax.psum_scatter(
         attn_terms.astype(jnp.bfloat16), "head", scatter_dimension=1, tiled=True
     ).astype(jnp.float32)
-    cotangent_here = spread(cotangent)
     scale_two = rms_scale(hidden)
     normed_two = (hidden * scale_two * feed_gain).astype(jnp.bfloat16)
     feed_rows = lax.all_gather(normed_two, "head", axis=1, tiled=True).reshape(
@@ -838,15 +843,6 @@
     activation = (silu_gate * up_vals).astype(jnp.bfloat16)
     feed_terms = jnp.dot(activation, down_weight, preferred_element_type=jnp.float32).reshape(
         rows_shape
-    )
-    block_out = (
-        hidden
-        + lax.psum_scatter(
-            feed_terms.astype(jnp.bfloat16), "head", scatter_dimension=1, tiled=True
-        ).astype(jnp.float32)
-    ).astype(jnp.bfloat16)
-    grad_rows = lax.all_gather(cotangent_here, "head", axis=1, tiled=True).reshape(
-        row_count, model_width
     )
     down_term = contract_rows(grad_rows, activation)
     grad_activ = contract_cols(grad_rows, down_weight)
@@ -869,6 +865,8 @@
     branch_rows = lax.all_gather(
         grad_hidden.astype(jnp.bfloat16), "head", axis=1, tiled=True
     ).reshape(row_count, model_width)
+    branch_rows, feed_terms = lax.optimization_barrier((branch_rows, feed_terms.astype(BF16)))
+    feed_sum = lax.psum_scatter(feed_terms, "head", scatter_dimension=1, tiled=True)
     grad_grouped = contract_cols(output_weight, branch_rows)
     shares = lax.axis_size("dp") * parts
     wgrads = jnp.stack([gate_term.astype(BF16), up_term.astype(BF16), down_term.astype(BF16)])
@@ -876,6 +874,8 @@
     grad_query, grad_key, grad_value, group_part, lambda_part, feed_sums = attend_back(
         dims, groups, lambda_head, queries.reshape(part_shape), keys_all, values_all,
         grad_grouped, gain_col, mixed, second, lse, tables, wgrads)
+    feed_sum, grad_query = lax.optimization_barrier((feed_sum, grad_query))
+    block_out = (hidden + feed_sum.astype(F32)).astype(BF16)
     group_part = jnp.sum(group_part, axis=1) * SHRINK
     lambda_part = jnp.sum(lambda_part, axis=(1, 2))
     third = jnp.pad(

time: 907 us -> 807 us (0.89)
  waiting for transfers between devices: 427 us -> 335 us
  starting transfers between devices: 12.7 us -> 27.9 us
  blocking collectives: 14.8 us -> 0 us
  matrix products: 79.2 us -> 67.5 us
    reduce_scatter x1, waiting for transfers between devices: 60.9 us -> 0.01 us  [per_device(): lax.psum_scatter(feed_terms, 'head', scatter_dimension=1, tiled=True)]
    all_gather x1, waiting for transfers between devices: 50.7 us -> 7.36 us  [per_device(): grad_rows = lax.all_gather(late, 'head', axis=1, tiled=True)]
    all_gather x1, waiting for transfers between devices: 64.6 us -> 42 us  [per_device(): lax.all_gather(normed, 'head', axis=1, tiled=True)]
    all_gather x1, waiting for transfers between devices: 8.51 us -> 30.7 us  [per_device(): values_all = lax.all_gather(values_own.reshape(part_shape), 'ctx', axis=0)]
    all_to_all x1 -> x0, blocking collectives: 14.8 us -> none  [spread(): cut = lax.all_to_all(cut, 'ctx', 0, 0, tiled=True)]
    all_gather x1, waiting for transfers between devices: 42.4 us -> 54.9 us  [per_device(): lax.all_gather(normed_two, 'head', axis=1, tiled=True)]
    reduce_scatter x1, starting transfers between devices: 0.04 us -> 11 us  [per_device(): lax.psum_scatter(feed_terms, 'head', scatter_dimension=1, tiled=True)]
    all_to_all x1 -> x2, waiting for transfers between devices: 11.3 us -> 22.3 us  [spread(): cut = lax.all_to_all(cut, 'ctx', 0, 0, tiled=True)]
  transfers between devices with their start and end apart: 12 -> 13, of which waited for: 12 -> 12; matrix products, arithmetic and copies ran while one was open for 10% -> 8% of each run, Pallas kernels for 0% -> 24%
where the time goes in v3:
time: 807 us; the launch traced here: 797 us
  waiting for transfers between devices  335 us (42%)
  Pallas kernels  280 us (35%)
  matrix products  67.5 us (8%)
  local copies, waits for them, and re-layouts  40 us (5%)
  other arithmetic  32.2 us (4%)
  starting transfers between devices  27.9 us (3%)
  between operations  14.8 us (2%)
    pallas_call x1, Pallas kernels, attend_back(): pl.pallas_call(partial(attend_back_kernel, dims, groups), out_shape=(rows...  139 us
    pallas_call x1, Pallas kernels, finish(): pl.pallas_call(partial(finish_kernel, dims, groups, lines), out_shape=(ja...  91.1 us
    reduce_scatter x1, waiting for transfers between devices, per_device(): lax.psum_scatter(attn_terms.astype(jnp.bfloat16), 'head', scatter_dimensi...  59.2 us
    reduce_scatter x1, waiting for transfers between devices, per_device(): lax.psum_scatter(normed_two_terms.astype(jnp.bfloat16), 'head', scatter_d...  55.5 us
    all_gather x1, waiting for transfers between devices, per_device(): lax.all_gather(normed_two, 'head', axis=1, tiled=True)  54.9 us
    pallas_call x1, Pallas kernels, attend(): pl.pallas_call(partial(attend_kernel, dims), out_shape=(jax.ShapeDtypeStr...  49.8 us
    all_gather x1, waiting for transfers between devices, per_device(): lax.all_gather(normed, 'head', axis=1, tiled=True)  42 us
    all_gather x1, waiting for transfers between devices, per_device(): values_all = lax.all_gather(values_own.reshape(part_shape), 'ctx', axis=0)  30.7 us
  transfers between devices with their start and end apart: 13, of which 12 were waited for; matrix products, arithmetic and copies ran while one was open for 8% of the time, Pallas kernels for 24%

profile of v3, /device:TPU:0, one launch (start us, length us, event | category | flops | bytes accessed | tf_op | source)
XLA Modules:
  0.0 797.3 jit_solution(14120597878031965060)
XLA Ops:
  14.8 11.3 %all-to-all-done = bf16[4,2,32,1536]{3,2,1,0:T(8,128)(2,1)} async-done(((bf16[4,2,32,1536]{3,2,1,0:T(8,128)(2,1)}), bf16[4,2,32,1536]{3,2,1,0:T(8,128)(2,1)}, u32[]{:S(2)}, u32[]{:S(2)}) %all-to-all-start) | async-done | bytes 786464 | tf_op jit(solution)/shard_map/all_to_all | solution.py:794
  39.3 11.0 %all-to-all-done.1 = bf16[4,2,32,1536]{3,2,1,0:T(8,128)(2,1)} async-done(((bf16[4,2,32,1536]{3,2,1,0:T(8,128)(2,1)}), bf16[4,2,32,1536]{3,2,1,0:T(8,128)(2,1)}, u32[]{:S(2)}, u32[]{:S(2)}) %all-to-all-start.1) | async-done | bytes 786464 | tf_op jit(solution)/shard_map/all_to_all | solution.py:794
  55.0 42.0 %all-gather.7.cloned.1.call-done = bf16[8,128,1536]{2,1,0:T(8,128)(2,1)} async-done(((bf16[8,32,1536]{2,1,0:T(8,128)(2,1)}), bf16[8,128,1536]{2,1,0:T(8,128)(2,1)}) %all-gather.7.cloned.1.call-update) | async-done | bytes 3145744 | tf_op jit(solution)/shard_map/all_gather | solution.py:806
  108.7 4.9 convolution_convert_fusion.5
  113.7 22.2 %all-gather.9.cloned.1.call-done.k_ref = bf16[4,8,128,384]{3,2,1,0:T(8,128)(2,1)} async-done(((bf16[1,8,128,384]{3,2,1,0:T(8,128)(2,1)}), bf16[4,8,128,384]{3,2,1,0:T(8,128)(2,1)}) %all-gather.9.cloned.1.call-update) | async-done | bytes 3145744 | tf_op jit(solution)/shard_map/all_gather | solution.py:816
  135.9 30.7 %all-gather.11.cloned.1.call-done.v_ref = bf16[4,8,128,384]{3,2,1,0:T(8,128)(2,1)} async-done(((bf16[1,8,128,384]{3,2,1,0:T(8,128)(2,1)}), bf16[4,8,128,384]{3,2,1,0:T(8,128)(2,1)}) %all-gather.11.cloned.1.call-update) | async-done | bytes 3145744 | tf_op jit(solution)/shard_map/all_gather | solution.py:817
  171.1 49.8 %attend.1 = (bf16[8,128,384]{2,1,0:T(8,128)(2,1)S(1)}, f32[8,3,128,128]{3,2,1,0:T(8,128)S(1)}, f32[8,3,128,128]{3,2,1,0:T(8,128)S(1)}, f32[8,3,1,256]{3,2,1,0:T(1,128)S(1)}) custom-call(s32[1]{0:T(128)} %bitcast.4.part_ref, f32[3]{0:T(128)S(1)} %subtract_add_fusion.lam_ref, bf16[8,128,384]{2,1,0:T(8,128)(2,1)S(1)} %copy-done.2, ...), custom_call_target="tpu_custom_call" | custom-call | flops 20000000000 | bytes 12000000 | tf_op jit(solution)/shard_map/attend/pallas_call | solution.py:384
  224.7 7.4 all-gather.13.cloned.1.call-done
  232.1 4.9 convolution_convert_fusion
  237.1 59.2 %reduce-scatter.4.cloned.1.call-done = bf16[8,32,1536]{2,1,0:T(8,128)(2,1)} async-done(((bf16[8,128,1536]{2,1,0:T(8,128)(2,1)}), bf16[8,32,1536]{2,1,0:T(8,128)(2,1)}) %reduce-scatter.4.cloned.1.call-update) | async-done | bytes 786448 | tf_op jit(solution)/shard_map/reduce_scatter | solution.py:831
  300.8 8.2 %fusion.19 = f32[1024,1024]{1,0:T(8,128)} fusion(bf16[1024,1536]{1,0:T(8,128)(2,1)} %bitcast.125, bf16[1024,1536]{1,0:T(8,128)(2,1)} %param.34), kind=kOutput, calls=%fused_computation.103 | convolution fusion | flops 3221225472 | bytes 10485760 | tf_op jit(solution)/shard_map/dot_general | solution.py:52
  309.1 54.9 %all-gather.15.cloned.1.call-done = bf16[8,128,1536]{2,1,0:T(8,128)(2,1)} async-done(((bf16[8,32,1536]{2,1,0:T(8,128)(2,1)}), bf16[8,128,1536]{2,1,0:T(8,128)(2,1)}) %all-gather.15.cloned.1.call-update) | async-done | bytes 3145744 | tf_op jit(solution)/shard_map/all_gather | solution.py:836
  364.0 6.4 fusion.20
  370.5 6.3 multiply_convert_fusion
  380.3 5.0 add_convert_fusion
  389.1 55.5 %reduce-scatter.6.cloned.1.call-done = bf16[8,32,1536]{2,1,0:T(8,128)(2,1)} async-done(((bf16[8,128,1536]{2,1,0:T(8,128)(2,1)}), bf16[8,32,1536]{2,1,0:T(8,128)(2,1)}) %reduce-scatter.6.cloned.1.call-update) | async-done | bytes 786448 | tf_op jit(solution)/shard_map/reduce_scatter | solution.py:858
  448.4 11.0 %reduce-scatter.8.cloned.1.call-start = ((), (), s32[]{:S(2)}) async-start(), calls=%async_computation.15 | async-start | bytes 3932160 | tf_op jit(solution)/shard_map/reduce_scatter | solution.py:869
  462.6 6.2 convolution_convert_fusion.3
  476.3 4.9 convolution_convert_fusion.4
  485.5 26.4 %all-gather.17.cloned.1.call-done = bf16[8,128,1536]{2,1,0:T(8,128)(2,1)} async-done(((bf16[8,32,1536]{2,1,0:T(8,128)(2,1)}), bf16[8,128,1536]{2,1,0:T(8,128)(2,1)}) %all-gather.17.cloned.1.call-update) | async-done | bytes 3145744 | tf_op jit(solution)/shard_map/all_gather | solution.py:865
  516.4 138.8 %attend_back.1 = (bf16[8,128,384]{2,1,0:T(8,128)(2,1)}, bf16[8,128,384]{2,1,0:T(8,128)(2,1)}, bf16[8,128,384]{2,1,0:T(8,128)(2,1)}, f32[384,128]{1,0:T(8,128)}, ...) custom-call(f32[3]{0:T(128)} %copy-done.4, bf16[8,128,384]{2,1,0:T(8,128)(2,1)} %copy.79.q_ref, ...), custom_call_target="tpu_custom_call" | custom-call | flops 60000002048 | bytes 24000000 | tf_op jit(solution)/shard_map/attend_back/pallas_call | solution.py:413
  663.2 91.1 %finish.1 = (bf16[8,32,1536]{2,1,0:T(8,128)(2,1)}, f32[4,192,384]{2,1,0:T(8,128)}, f32[8,1536]{1,0:T(8,128)}) custom-call(bf16[8,128,384]{2,1,0:T(8,128)(2,1)} %get-tuple-element.58.gq_ref, bf16[8,128,384]{2,1,0:T(8,128)(2,1)} %get-tuple-element.59.gk_ref, bf16[8,128,384]{2,1,0:T(8,128)(2,1)} %get-tuple-element.60.gv_ref, bf16[1536,384]{1,0:T(8,128)(2,1)} %wq_ref.1, ...), custom_call_target="tpu_custom_call" | custom-call | flops 8000000000 | bytes 24000000 | tf_op jit(solution)/shard_map/finish/pallas_call | solution.py:705
  765.6 7.0 all-to-all-done.3
  780.9 7.6 all-to-all-done.2
  (192 shorter events, 109.8 us)
Async XLA Ops:
  7.2 363.2 %copy-start = (bf16[1536,1024]{1,0:T(8,128)(2,1)S(1)}, bf16[1536,1024]{1,0:T(8,128)(2,1)}, u32[]{:S(2)}) copy-start(bf16[1536,1024]{1,0:T(8,128)(2,1)} %param.33) | copy-start | bytes 9437188
  9.4 16.7 %all-to-all-start = ((bf16[4,2,32,1536]{3,2,1,0:T(8,128)(2,1)}), bf16[4,2,32,1536]{3,2,1,0:T(8,128)(2,1)}, u32[]{:S(2)}, u32[]{:S(2)}) async-start(bf16[4,2,32,1536]{3,2,1,0:T(8,128)(2,1)} %copy.72), calls=%async_computation | async-start | bytes 1572864 | tf_op jit(solution)/shard_map/all_to_all | solution.py:794
  13.8 83.2 %all-gather.7.cloned.1.call-start = ((), (), s32[]{:S(2)}) async-start(), calls=%async_computation.7 | async-start | bytes 3932160 | tf_op jit(solution)/shard_map/all_gather | solution.py:806
  34.4 15.9 %all-to-all-start.1 = ((bf16[4,2,32,1536]{3,2,1,0:T(8,128)(2,1)}), bf16[4,2,32,1536]{3,2,1,0:T(8,128)(2,1)}, u32[]{:S(2)}, u32[]{:S(2)}) async-start(bf16[4,2,32,1536]{3,2,1,0:T(8,128)(2,1)} %copy.73), calls=%async_computation.1 | async-start | bytes 1572864 | tf_op jit(solution)/shard_map/all_to_all | solution.py:794
  38.6 97.3 %all-gather.9.cloned.1.call-start = ((), (), s32[]{:S(2)}) async-start(), calls=%async_computation.8 | async-start | bytes 3932160 | tf_op jit(solution)/shard_map/all_gather | solution.py:816
  39.3 65.1 %copy-start.15 = (f32[8,128,32]{1,0,2:T(8,128)}, f32[8,128,32]{1,0,2:T(8,128)S(1)}, u32[]{:S(2)}) copy-start(f32[8,128,32]{1,0,2:T(8,128)S(1)} %get-tuple-element.96) | copy-start | bytes 393220
  108.6 58.1 %copy-start.28 = (f32[384]{0:T(512)S(1)}, f32[384]{0:T(512)}, u32[]{:S(2)}) copy-start(f32[384]{0:T(512)} %param.29) | copy-start | bytes 4612
  108.6 58.2 %copy-start.20 = (f32[3,64]{1,0:T(4,128)S(1)}, f32[3,64]{1,0:T(4,128)}, u32[]{:S(2)}) copy-start(f32[3,64]{1,0:T(4,128)} %param.27) | copy-start | bytes 2308
  108.6 58.2 %copy-start.22 = (f32[3,64]{1,0:T(4,128)S(1)}, f32[3,64]{1,0:T(4,128)}, u32[]{:S(2)}) copy-start(f32[3,64]{1,0:T(4,128)} %param.28) | copy-start | bytes 2308
  108.6 58.2 %copy-start.24 = (f32[3,64]{1,0:T(4,128)S(1)}, f32[3,64]{1,0:T(4,128)}, u32[]{:S(2)}) copy-start(f32[3,64]{1,0:T(4,128)} %param.25) | copy-start | bytes 2308
  108.7 58.2 %copy-start.26 = (f32[3,64]{1,0:T(4,128)S(1)}, f32[3,64]{1,0:T(4,128)}, u32[]{:S(2)}) copy-start(f32[3,64]{1,0:T(4,128)} %param.26) | copy-start | bytes 2308
  108.7 57.9 %all-gather.11.cloned.1.call-start = ((), (), s32[]{:S(2)}) async-start(), calls=%async_computation.9 | async-start | bytes 3932160 | tf_op jit(solution)/shard_map/all_gather | solution.py:817
  113.6 118.5 %all-gather.13.cloned.1.call-start = ((), (), s32[]{:S(2)}) async-start(), calls=%async_computation.10 | async-start | bytes 3932160 | tf_op jit(solution)/shard_map/all_gather | solution.py:819
  166.6 129.6 %reduce-scatter.4.cloned.1.call-start = ((), (), s32[]{:S(2)}) async-start(), calls=%async_computation.11 | async-start | bytes 3932160 | tf_op jit(solution)/shard_map/reduce_scatter | solution.py:831
  237.0 60.9 %copy-start.18 = (f32[1536]{0:T(1024)S(1)}, f32[1536]{0:T(1024)}, u32[]{:S(2)}) copy-start(f32[1536]{0:T(1024)} %param.31) | copy-start | bytes 18436
  237.0 127.0 %all-gather.15.cloned.1.call-start = ((), (), s32[]{:S(2)}) async-start(), calls=%async_computation.12 | async-start | bytes 3932160 | tf_op jit(solution)/shard_map/all_gather | solution.py:836
  300.5 144.0 %reduce-scatter.6.cloned.1.call-start = ((), (), s32[]{:S(2)}) async-start(), calls=%async_computation.13 | async-start | bytes 3932160 | tf_op jit(solution)/shard_map/reduce_scatter | solution.py:858
  385.3 59.2 %copy-start.10 = (bf16[8,32,1536]{2,1,0:T(8,128)(2,1)S(1)}, bf16[8,32,1536]{2,1,0:T(8,128)(2,1)}, u32[]{:S(2)}) copy-start(bf16[8,32,1536]{2,1,0:T(8,128)(2,1)} %copy-done.9) | copy-start | bytes 2359300
  385.4 59.2 %copy-start.11 = (bf16[8,32,1536]{2,1,0:T(8,128)(2,1)S(1)}, bf16[8,32,1536]{2,1,0:T(8,128)(2,1)}, u32[]{:S(2)}) copy-start(bf16[8,32,1536]{2,1,0:T(8,128)(2,1)} %reduce-scatter.4.cloned.1.call-done) | copy-start | bytes 2359300
  385.4 126.5 %all-gather.17.cloned.1.call-start = ((), (), s32[]{:S(2)}) async-start(), calls=%async_computation.14 | async-start | bytes 3932160 | tf_op jit(solution)/shard_map/all_gather | solution.py:865
  386.9 59.3 %copy-start.12 = (bf16[8,32,1536]{2,1,0:T(8,128)(2,1)S(1)}, bf16[8,32,1536]{2,1,0:T(8,128)(2,1)}, u32[]{:S(2)}) copy-start(bf16[8,32,1536]{2,1,0:T(8,128)(2,1)} %broadcast_select_fusion.2) | copy-start | bytes 2359300
  448.4 212.8 %reduce-scatter.8.cloned.1.call-start = ((), (), s32[]{:S(2)}) async-start(), calls=%async_computation.15 | async-start | bytes 3932160 | tf_op jit(solution)/shard_map/reduce_scatter | solution.py:869
  757.5 15.1 %all-to-all-start.3 = ((bf16[4,2,32,1536]{3,2,1,0:T(8,128)(2,1)}), bf16[4,2,32,1536]{3,2,1,0:T(8,128)(2,1)S(1)}, u32[]{:S(2)}, u32[]{:S(2)}) async-start(bf16[4,2,32,1536]{3,2,1,0:T(8,128)(2,1)} %bitcast.31), calls=%async_computation.6 | async-start | bytes 1572864 | tf_op jit(solution)/shard_map/all_to_all | solution.py:799
  772.6 15.9 %all-to-all-start.2 = ((bf16[4,2,32,1536]{3,2,1,0:T(8,128)(2,1)}), bf16[4,2,32,1536]{3,2,1,0:T(8,128)(2,1)}, u32[]{:S(2)}, u32[]{:S(2)}) async-start(bf16[4,2,32,1536]{3,2,1,0:T(8,128)(2,1)} %bitcast.26), calls=%async_computation.5 | async-start | bytes 1572864 | tf_op jit(solution)/shard_map/all_to_all | solution.py:799
  (36 other events, 346.9 us)
Sparse Core Ops, SparseCore 0:
  32.4 64.4 all-gather.6
  108.7 27.1 all-gather.8
  138.1 28.4 all-gather.10
  168.6 63.4 all-gather.12
  237.1 59.0 reduce-scatter.3
  300.6 63.3 all-gather.14
  385.5 59.0 reduce-scatter.5
  448.5 63.3 all-gather.16
  516.5 59.0 reduce-scatter.7

commit v4 on v3

--- a/solution.py
+++ b/solution.py
@@ -71,7 +71,7 @@
     )
 
 
-def attend_kernel(dims, part_ref, lam_ref, q_ref, k_ref, v_ref, gain_ref,
+def attend_kernel(dims, part_ref, lam_ref, q_ref, kv_ref, gain_ref,
                   grouped_ref, mixed_ref, second_ref, lse_ref, vt_ref, qbd_ref, acc_ref):
     slots, parts, heads, tile, width, strip = dims
     half = width // 2
@@ -81,7 +81,7 @@
         for h in range(heads):
             for c in range(parts):
                 vt_ref[h, slot, :, c * tile:(c + 1) * tile] = jnp.transpose(
-                    v_ref[c, slot, :, h * width:(h + 1) * width])
+                    kv_ref[c, slot, 1, :, h * width:(h + 1) * width])
         return carry
 
     lax.fori_loop(0, slots, turn, 0)
@@ -94,7 +94,7 @@
             peak, total = state[2 * h], state[2 * h + 1]
             scores = []
             for c in range(parts):
-                s = dot(k_ref[c, slot, :, h * width:(h + 1) * width], qbd_ref[h])
+                s = dot(kv_ref[c, slot, 0, :, h * width:(h + 1) * width], qbd_ref[h])
                 if diag:
                     key_off = offsets_of(c, parts, strip, 0, (tile, 1))
                     s = jnp.where(key_off <= query_off, s, NEGATIVE)
@@ -163,7 +163,7 @@
     return jnp.where(lane % half < quarter, back, ahead)
 
 
-def attend_back_kernel(dims, groups, lam_ref, q_ref, k_ref, v_ref, gg_ref, gain_ref,
+def attend_back_kernel(dims, groups, lam_ref, q_ref, kv_ref, gg_ref, gain_ref,
                        mixed_ref, second_ref, lse_ref, cost_ref, sint_ref, cosn_ref, sinn_ref,
                        wg_ref,
                        gq_ref, gk_ref, gv_ref, gpart_ref, lpart_ref, wsum_ref,
@@ -289,13 +289,13 @@
             lanes = slice(h * width, (h + 1) * width)
             turned = []
             for c in range(parts):
-                keys = k_ref[c, slot, :, lanes]
+                keys = kv_ref[c, slot, 0, :, lanes]
                 s = dot(keys, qbdt_ref[place, h])
                 if diag:
                     key_off = offsets_of(c, parts, strip, 0, (tile, 1))
                     s = jnp.where(key_off <= query_off, s, NEGATIVE)
                 weights = jnp.exp(s - lse)
-                probs = dot(v_ref[c, slot, :, lanes], gt_ref[place, h])
+                probs = dot(kv_ref[c, slot, 1, :, lanes], gt_ref[place, h])
                 ds = (weights * (probs - delta)).astype(BF16)
                 dv = dot(weights.astype(BF16), g_ref[place, h])
                 dk = dot(ds, qbd_ref[place, h])
@@ -315,7 +315,7 @@
         for h in range(heads):
             for c in range(parts):
                 kt_ref[h, :, c * tile:(c + 1) * tile] = jnp.transpose(
-                    k_ref[c, slot, :, h * width:(h + 1) * width])
+                    kv_ref[c, slot, 0, :, h * width:(h + 1) * width])
         one_block(j, slot, True)
 
         def rest(place, inner):
@@ -379,7 +379,7 @@
         pl.BlockSpec(memory_space=pltpu.VMEM)] * (count - smem)
 
 
-def attend(dims, part, lam, queries, keys_all, values_all, gain):
+def attend(dims, part, lam, queries, kv_all, gain):
     slots, parts, heads, tile, width, strip = dims
     return pl.pallas_call(
         partial(attend_kernel, dims),
@@ -389,7 +389,7 @@
             jax.ShapeDtypeStruct((slots, heads, width, tile), F32),
             jax.ShapeDtypeStruct((slots, heads, 1, 2 * tile), F32),
         ),
-        in_specs=specs(6, 2),
+        in_specs=specs(5, 2),
         out_specs=specs(4, 0),
         scratch_shapes=[
             pltpu.VMEM((heads, slots, width, parts * tile), BF16),
@@ -400,10 +400,10 @@
         cost_estimate=pl.CostEstimate(
             flops=20_000_000_000, bytes_accessed=12_000_000, transcendentals=14_000_000),
         name="attend",
-    )(part, lam, queries, keys_all, values_all, gain)
-
-
-def attend_back(dims, groups, lam, queries, keys_all, values_all, gg, gain, mixed, second,
+    )(part, lam, queries, kv_all, gain)
+
+
+def attend_back(dims, groups, lam, queries, kv_all, gg, gain, mixed, second,
                 lse, tables, wgrads):
     slots, parts, heads, tile, width, strip = dims
     assert parts == 4
@@ -420,7 +420,7 @@
             jax.ShapeDtypeStruct((heads, width, tile), F32),
             jax.ShapeDtypeStruct((kinds, rows, cols), F32),
         ),
-        in_specs=specs(13, 1) + [pl.BlockSpec(memory_space=pl.ANY)],
+        in_specs=specs(12, 1) + [pl.BlockSpec(memory_space=pl.ANY)],
         out_specs=specs(6, 0),
         scratch_shapes=[
             pltpu.VMEM((heads, width, parts * tile), BF16),
@@ -452,7 +452,7 @@
         cost_estimate=pl.CostEstimate(
             flops=60_000_000_000, bytes_accessed=24_000_000, transcendentals=14_000_000),
         name="attend_back",
-    )(lam, queries, keys_all, values_all, gg, gain, mixed, second, lse, *tables, wgrads)
+    )(lam, queries, kv_all, gg, gain, mixed, second, lse, *tables, wgrads)
 
 
 def dot_turned(left, right):
@@ -524,11 +524,11 @@
 
 
 def finish_kernel(dims, groups, lines, gq_ref, gk_ref, gv_ref, wq_ref, wk_ref, wv_ref, normed_ref,
-                  branch_ref, grouped_ref, inputs_ref, gh_ref, gain_ref, small_ref,
-                  ig_ref, wsum_ref, vec_ref,
+                  branch_ref, grouped_ref, inputs_ref, gh_ref, gain_ref, small_ref, bo_ref,
+                  ig_ref, wsum_ref, vec_ref, bout_ref,
                   own_ref, left_ref, right_ref, acc_ref, line_sem,
                   wloc_ref, wr1_ref, wr2_ref, mixer_ref, va_ref, vb_ref, vc_ref, v2_ref,
-                  w1_sem, w2_sem, va_sem, vb_sem, vc_sem):
+                  w1_sem, w2_sem, va_sem, vb_sem, vc_sem, bo_sem):
     slots, parts, heads, tile, width, strip = dims
     full = heads * width
     model = normed_ref.shape[-1]
@@ -548,10 +548,17 @@
 
     others = [lax.rem(me + step, groups) for step in range(1, groups)]
     line_others = [lax.rem(place + step, lines) for step in range(1, lines)]
-    greet([sibling] + [group_device(index) for index in others]
+    targets = [lax.rem(part + step, parts) for step in range(1, parts)]
+    greet([sibling, {"ctx": (1 - y) * 2 + other_core}]
+          + [group_device(index) for index in others]
           + [{"head": index} for index in line_others])
     line = LineSum("head", lines, own_ref, left_ref, right_ref, line_sem)
     mixer_ref[...] = jnp.zeros_like(mixer_ref)
+
+    def out_copy(step):
+        return mesh_copy(bo_ref.at[targets[step]], bout_ref.at[:, part], bo_sem.at[0, step],
+                         bo_sem.at[1, step], {"ctx": targets[step]})
+
     block = 256
 
     def product(q):
@@ -642,6 +649,10 @@
         for t in range(lines - 1):
             if 0 <= slot - t < chunks:
                 line.step(slot - t, t)
+        if slot == 0:
+            for step in range(parts - 1):
+                out_copy(step).start()
+            bout_ref[:, part] = bo_ref[part]
         if slot < 4:
             weight_term(slot)
             if slot == 3:
@@ -659,6 +670,8 @@
     va_ref[0] = jnp.where(first_row, mixer, small_ref[...])
     for q in range(chunks):
         line.drain(q)
+    for step in range(parts - 1):
+        out_copy(step).wait()
     swap = mesh_copy(va_ref.at[0], va_ref.at[1], va_sem.at[0], va_sem.at[1], sibling)
     swap.start()
     weights_finish()
@@ -702,15 +715,17 @@
     slots, parts, heads, tile, width, strip = dims
     full = heads * width
     model = operands[6].shape[-1]
+    pairs = operands[-1].shape[1]
     return pl.pallas_call(
         partial(finish_kernel, dims, groups, lines),
         out_shape=(
             jax.ShapeDtypeStruct((slots, strip, model), BF16),
             jax.ShapeDtypeStruct((4, rows, full), F32),
             jax.ShapeDtypeStruct((8, model), F32),
+            jax.ShapeDtypeStruct((pairs, parts, strip, model), BF16),
         ),
-        in_specs=specs(13, 0),
-        out_specs=specs(3, 0),
+        in_specs=specs(14, 0),
+        out_specs=specs(4, 0),
         scratch_shapes=line_scratch(chunks, lines, slots // chunks * strip, model) + [
             pltpu.VMEM((4, model, full), BF16),
             pltpu.VMEM((4, groups, rows, full), BF16),
@@ -725,12 +740,190 @@
             pltpu.SemaphoreType.DMA((2,)),
             pltpu.SemaphoreType.DMA((2, groups)),
             pltpu.SemaphoreType.DMA((2, lines)),
+            pltpu.SemaphoreType.DMA((2, parts - 1)),
         ],
         compiler_params=pltpu.CompilerParams(
             vmem_limit_bytes=60 << 20, collective_id=2, has_side_effects=True),
         cost_estimate=pl.CostEstimate(
             flops=8_000_000_000, bytes_accessed=24_000_000, transcendentals=0),
         name="finish",
+    )(*operands)
+
+
+class LineGather:
+    def __init__(self, axis, size, view, sems):
+        self.axis, self.size, self.view, self.sems = axis, size, view, sems
+        self.me = lax.axis_index(axis)
+
+    def copy(self, q, t, side):
+        source = jnp.clip(self.me - t if side == 0 else self.me + t, 0, self.size - 1)
+        neighbour = jnp.clip(self.me + (1 if side == 0 else -1), 0, self.size - 1)
+        return mesh_copy(
+            self.view(q, source), self.view(q, source), self.sems.at[0, side, q, t],
+            self.sems.at[1, side, q, source], {self.axis: neighbour})
+
+    def rank(self, side):
+        return self.me if side == 0 else self.size - 1 - self.me
+
+    def step(self, q, t):
+        for side in range(2):
+            rank = self.rank(side)
+
+            if t > 0:
+                @pl.when(rank >= t)
+                def _():
+                    self.copy(q, t, side).wait_recv()
+
+            if t < self.size - 1:
+                @pl.when((rank >= t) & (rank < self.size - 1))
+                def _():
+                    self.copy(q, t, side).start()
+
+    def drain(self, q):
+        for t in range(self.size - 1):
+            for side in range(2):
+                rank = self.rank(side)
+
+                @pl.when((rank >= t) & (rank < self.size - 1))
+                def _():
+                    self.copy(q, t, side).wait_send()
+
+
+def open_kernel(dims, lines, chunks, x_ref, gain_ref, wq_ref, wk_ref, wv_ref, cosn_ref, sinn_ref,
+                cot_ref, normed_ref, q_ref, kv_ref, cout_ref,
+                line_sem, c_sem, sib_sem, far_sem, fwd_sem):
+    slots, parts, heads, tile, width, strip = dims
+    half = width // 2
+    per = slots // chunks
+    model = x_ref.shape[-1]
+    part = lax.axis_index("ctx")
+    place = lax.axis_index("head")
+    core = part % 2
+    y = part // 2
+    sibling = {"ctx": y * 2 + 1 - core}
+    across = {"ctx": (1 - y) * 2 + core}
+    far = (1 - y) * 2 + core
+    far_other = (1 - y) * 2 + 1 - core
+    near = y * 2 + 1 - core
+    targets = [lax.rem(part + step, parts) for step in range(1, parts)]
+    greet([{"ctx": target} for target in targets]
+          + [{"head": lax.rem(place + step, lines)} for step in range(1, lines)])
+    line = LineGather(
+        "head", lines, lambda q, s: normed_ref.at[pl.ds(q * per, per), s], line_sem)
+
+    def norm(q):
+        x = x_ref[q * per:(q + 1) * per].reshape(per * strip, model).astype(F32)
+        scale = lax.rsqrt(jnp.mean(x * x, axis=1, keepdims=True) + EPSILON)
+        low = (x * scale * gain_ref[...]).astype(BF16).reshape(per, strip, model)
+        for p in range(per):
+            normed_ref[q * per + p, place] = low[p]
+
+    def cot_copy(step):
+        return mesh_copy(cot_ref.at[:, targets[step]], cout_ref.at[part], c_sem.at[0, step],
+                         c_sem.at[1, step], {"ctx": targets[step]})
+
+    def chunk_view(source, q):
+        return kv_ref.at[source, pl.ds(q * per, per)]
+
+    def to_sibling(q):
+        return mesh_copy(chunk_view(part, q), chunk_view(part, q), sib_sem.at[0, q],
+                         sib_sem.at[1, q], sibling)
+
+    def from_sibling(q):
+        return mesh_copy(chunk_view(near, q), chunk_view(near, q), sib_sem.at[0, q],
+                         sib_sem.at[1, q], sibling)
+
+    def to_far(q):
+        return mesh_copy(chunk_view(part, q), chunk_view(part, q), far_sem.at[0, q],
+                         far_sem.at[1, q], across)
+
+    def from_far(q):
+        return mesh_copy(chunk_view(far, q), chunk_view(far, q), far_sem.at[0, q],
+                         far_sem.at[1, q], across)
+
+    def forward(q):
+        return mesh_copy(chunk_view(far, q), chunk_view(far, q), fwd_sem.at[0, q],
+                         fwd_sem.at[1, q], sibling)
+
+    def forwarded(q):
+        return mesh_copy(chunk_view(far_other, q), chunk_view(far_other, q), fwd_sem.at[0, q],
+                         fwd_sem.at[1, q], sibling)
+
+    def project(q):
+        rows = normed_ref[q * per:(q + 1) * per].reshape(per * tile, model)
+        for kind, weight_ref in ((1, wv_ref), (0, wk_ref), (2, wq_ref)):
+            result = dot(rows, weight_ref[...])
+            for p in range(per):
+                at = q * per + p
+                for h in range(heads):
+                    lanes = slice(h * width, (h + 1) * width)
+                    piece = result[p * tile:(p + 1) * tile, lanes]
+                    if kind != 1:
+                        piece = piece * cosn_ref[at] - swap_halves(piece, half) * sinn_ref[at]
+                    if kind == 2:
+                        q_ref[at, :, lanes] = piece.astype(BF16)
+                    else:
+                        kv_ref[part, at, kind, :, lanes] = piece.astype(BF16)
+
+    for slot in range(chunks + lines - 1):
+        if slot < chunks:
+            norm(slot)
+        for t in range(lines):
+            if 0 <= slot - t < chunks:
+                line.step(slot - t, t)
+        if slot == 0:
+            for step in range(parts - 1):
+                cot_copy(step).start()
+            cout_ref[part] = cot_ref[:, part]
+        q = slot - lines + 1
+        if q >= 0:
+            project(q)
+            to_far(q).start()
+            to_sibling(q).start()
+        if q >= 1:
+            from_far(q - 1).wait_recv()
+            forward(q - 1).start()
+    from_far(chunks - 1).wait_recv()
+    forward(chunks - 1).start()
+    for step in range(parts - 1):
+        cot_copy(step).wait()
+    for q in range(chunks):
+        line.drain(q)
+        from_sibling(q).wait_recv()
+        to_sibling(q).wait_send()
+        to_far(q).wait_send()
+    for q in range(chunks):
+        forwarded(q).wait_recv()
+        forward(q).wait_send()
+
+
+def open_rows(dims, lines, chunks, *operands):
+    slots, parts, heads, tile, width, strip = dims
+    full = heads * width
+    model = operands[0].shape[-1]
+    pairs = operands[-1].shape[0]
+    return pl.pallas_call(
+        partial(open_kernel, dims, lines, chunks),
+        out_shape=(
+            jax.ShapeDtypeStruct((slots, lines, strip, model), BF16),
+            jax.ShapeDtypeStruct((slots, tile, full), BF16),
+            jax.ShapeDtypeStruct((parts, slots, 2, tile, full), BF16),
+            jax.ShapeDtypeStruct((parts, pairs, strip, model), BF16),
+        ),
+        in_specs=specs(8, 0),
+        out_specs=specs(4, 0),
+        scratch_shapes=[
+            pltpu.SemaphoreType.DMA((2, 2, chunks, lines)),
+            pltpu.SemaphoreType.DMA((2, parts - 1)),
+            pltpu.SemaphoreType.DMA((2, chunks)),
+            pltpu.SemaphoreType.DMA((2, chunks)),
+            pltpu.SemaphoreType.DMA((2, chunks)),
+        ],
+        compiler_params=pltpu.CompilerParams(
+            vmem_limit_bytes=60 << 20, collective_id=3, has_side_effects=True),
+        cost_estimate=pl.CostEstimate(
+            flops=4_000_000_000, bytes_accessed=16_000_000, transcendentals=0),
+        name="open_rows",
     )(*operands)
 
 
@@ -801,26 +994,18 @@
 
     inputs_here = spread(inputs)
     tokens = inputs_here.astype(jnp.float32)
-    scale_one = rms_scale(tokens)
-    normed = (tokens * scale_one * mixer_gain).astype(jnp.bfloat16)
-    normed_rows = lax.all_gather(normed, "head", axis=1, tiled=True).reshape(row_count, model_width)
-    cotangent_here = spread(cotangent)
-    normed_rows, cotangent_here = lax.optimization_barrier((normed_rows, cotangent_here))
-    query_lin = jnp.dot(normed_rows, query_weight, preferred_element_type=jnp.float32)
-    key_lin = jnp.dot(normed_rows, key_weight, preferred_element_type=jnp.float32)
-    value_lin = jnp.dot(normed_rows, value_weight, preferred_element_type=jnp.float32)
-    queries = rotate(query_lin.reshape(split_shape), own_places, 1.0).astype(jnp.bfloat16)
-    keys_own = rotate(key_lin.reshape(split_shape), own_places, 1.0).astype(jnp.bfloat16)
-    values_own = value_lin.astype(jnp.bfloat16)
     part_shape = (slots, tile, qwidth)
-    keys_all = lax.all_gather(keys_own.reshape(part_shape), "ctx", axis=0)
-    values_all = lax.all_gather(values_own.reshape(part_shape), "ctx", axis=0)
-    keys_all, values_all, late = lax.optimization_barrier((keys_all, values_all, cotangent_here))
-    grad_rows = lax.all_gather(late, "head", axis=1, tiled=True)
+    cut_shape = (pair_count, parts, strip, model_width)
+    normed_rows, queries, kv_all, cotangent_slots = open_rows(
+        dims, head_total, 4, inputs_here, mixer_gain.reshape(1, model_width), query_weight,
+        key_weight, value_weight, cos_rows, sin_rows, cotangent.reshape(cut_shape))
+    cotangent_here = jnp.take(
+        cotangent_slots.reshape(slots, strip, model_width), slot_of, axis=0)
+    grad_rows = lax.all_gather(cotangent_here, "head", axis=1, tiled=True)
     part_arr = part.reshape(1).astype(jnp.int32)
     gain_col = group_gain.reshape(qwidth, 1)
     grouped, mixed, second, lse = attend(
-        dims, part_arr, lambda_head, queries.reshape(part_shape), keys_all, values_all,
+        dims, part_arr, lambda_head, queries, kv_all,
         gain_col)
     grouped, grad_rows = lax.optimization_barrier((grouped, grad_rows))
     grouped = grouped.reshape(row_count, qwidth)
@@ -872,7 +1057,7 @@
     wgrads = jnp.stack([gate_term.astype(BF16), up_term.astype(BF16), down_term.astype(BF16)])
     wgrads = wgrads.reshape(3, groups, 2, model_width // shares, wgrads.shape[-1])
     grad_query, grad_key, grad_value, group_part, lambda_part, feed_sums = attend_back(
-        dims, groups, lambda_head, queries.reshape(part_shape), keys_all, values_all,
+        dims, groups, lambda_head, queries, kv_all,
         grad_grouped, gain_col, mixed, second, lse, tables, wgrads)
     feed_sum, grad_query = lax.optimization_barrier((feed_sum, grad_query))
     block_out = (hidden + feed_sum.astype(F32)).astype(BF16)
@@ -882,12 +1067,14 @@
         jnp.concatenate([group_part, lambda_part]), (0, model_width - qwidth - heads_here))
     small = jnp.pad(jnp.stack([jnp.zeros_like(feed_part), feed_part, third]), ((0, 5), (0, 0)))
     grad_rows_shape = (slots, tile, model_width)
-    input_grad, attn_sums, vectors = finish(
+    block_slots = jnp.take(block_out, order, axis=0).reshape(
+        parts, pair_count, strip, model_width)
+    input_grad, attn_sums, vectors, block_out = finish(
         dims, groups, head_total, 4, model_width // shares, grad_query, grad_key, grad_value,
         query_weight, key_weight, value_weight, normed_rows.reshape(grad_rows_shape),
         branch_rows.reshape(grad_rows_shape), grouped.reshape(part_shape), inputs_here,
-        grad_hidden, mixer_gain.reshape(1, model_width), small)
-    block_out = unspread(block_out)
+        grad_hidden, mixer_gain.reshape(1, model_width), small, block_slots)
+    block_out = block_out.reshape(inputs.shape)
     input_grad = unspread(input_grad).astype(F32)
     group_grad = vectors[2, :qwidth]
     lambda_grad = vectors[2, qwidth:qwidth + heads_here]

time: 807 us -> 744 us (0.922)
  waiting for transfers between devices: 335 us -> 228 us
  Pallas kernels: 280 us -> 361 us
  starting transfers between devices: 27.9 us -> 9.31 us
  matrix products: 67.5 us -> 57.4 us
    all_gather x4 -> x1, waiting for transfers between devices: 102 us -> 6.56 us  [per_device(): grad_rows = lax.all_gather(cotangent_here, 'head', axis=1, tiled=True)]
    pallas_call x0 -> x1, Pallas kernels: none -> 79.9 us  [open_rows(): pl.pallas_call(partial(open_kernel, dims, lines, chunks), out_shape=(jax....]
    all_to_all x2 -> x1, waiting for transfers between devices: 22.3 us -> 2.38 us  [spread(): cut = lax.all_to_all(cut, 'ctx', 0, 0, tiled=True)]
    all_gather x1, waiting for transfers between devices: 26.4 us -> 39.2 us  [per_device(): lax.all_gather(grad_hidden.astype(jnp.bfloat16), 'head', axis=1, tiled=True)]
    reduce_scatter x1, starting transfers between devices: 11 us -> 0.21 us  [per_device(): lax.psum_scatter(feed_terms, 'head', scatter_dimension=1, tiled=True)]
    dot_general x3 -> x0, matrix products: 10.1 us -> none  [the longest x1 4.88 us: per_device(): jnp.dot(normed_rows, value_weight, preferred_element_type=jnp.float32)]
  transfers between devices with their start and end apart: 13 -> 8, of which waited for: 12 -> 7; matrix products, arithmetic and copies ran while one was open for 8% -> 7% of each run, Pallas kernels for 24% -> 26%
where the time goes in v4:
time: 744 us; the launch traced here: 737 us
  Pallas kernels  361 us (49%)
  waiting for transfers between devices  228 us (31%)
  matrix products  57.4 us (8%)
  local copies, waits for them, and re-layouts  33.1 us (4%)
  other arithmetic  32.2 us (4%)
  between operations  14.9 us (2%)
  starting transfers between devices  9.31 us (1%)
    pallas_call x1, Pallas kernels, attend_back(): pl.pallas_call(partial(attend_back_kernel, dims, groups), out_shape=(rows...  139 us
    pallas_call x1, Pallas kernels, finish(): pl.pallas_call(partial(finish_kernel, dims, groups, lines), out_shape=(ja...  92.7 us
    pallas_call x1, Pallas kernels, open_rows(): pl.pallas_call(partial(open_kernel, dims, lines, chunks), out_shape=(jax....  79.9 us
    reduce_scatter x1, waiting for transfers between devices, per_device(): lax.psum_scatter(normed_two_terms.astype(jnp.bfloat16), 'head', scatter_d...  59.2 us
    reduce_scatter x1, waiting for transfers between devices, per_device(): lax.psum_scatter(attn_terms.astype(jnp.bfloat16), 'head', scatter_dimensi...  59.2 us
    all_gather x1, waiting for transfers between devices, per_device(): lax.all_gather(normed_two, 'head', axis=1, tiled=True)  55.2 us
    pallas_call x1, Pallas kernels, attend(): pl.pallas_call(partial(attend_kernel, dims), out_shape=(jax.ShapeDtypeStr...  49.7 us
    all_gather x1, waiting for transfers between devices, per_device(): lax.all_gather(grad_hidden.astype(jnp.bfloat16), 'head', axis=1, tiled=True)  39.2 us
  transfers between devices with their start and end apart: 8, of which 7 were waited for; matrix products, arithmetic and copies ran while one was open for 7% of the time, Pallas kernels for 26%

profile of v4, /device:TPU:0, one launch (start us, length us, event | category | flops | bytes accessed | tf_op | source)
XLA Modules:
  0.0 736.6 jit_solution(17276555504309113913)
XLA Ops:
  9.4 4.3 all-to-all-start
  30.8 79.9 %open_rows.1 = (bf16[8,4,32,1536]{3,2,1,0:T(8,128)(2,1)}, bf16[8,128,384]{2,1,0:T(8,128)(2,1)}, bf16[4,8,2,128,384]{4,3,2,1,0:T(8,128)(2,1)}, bf16[4,2,32,1536]{3,2,1,0:T(8,128)(2,1)}) custom-call(bf16[8,32,1536]{2,1,0:T(8,128)(2,1)} %broadcast_select_fusion.2.x_ref.inputs_ref, f32[1,1536]{1,0:T(1,128)} %reshape.223.gain_ref, bf16[1536,384]{1,0:T(8,128)(2,1)} %wq_ref.3, ...), custom_call_target="tpu_custom_call" | custom-call | flops 4000000000 | bytes 16000000 | tf_op jit(solution)/shard_map/open_rows/pallas_call | solution.py:905
  118.0 49.7 %attend.1 = (bf16[8,128,384]{2,1,0:T(8,128)(2,1)S(1)}, f32[8,3,128,128]{3,2,1,0:T(8,128)S(1)}, f32[8,3,128,128]{3,2,1,0:T(8,128)S(1)}, f32[8,3,1,256]{3,2,1,0:T(1,128)S(1)}) custom-call(s32[1]{0:T(128)} %bitcast.8.part_ref, f32[3]{0:T(128)S(1)} %subtract_add_fusion.lam_ref, bf16[8,128,384]{2,1,0:T(8,128)(2,1)S(1)} %copy-done.5, ...), custom_call_target="tpu_custom_call" | custom-call | flops 20000000000 | bytes 12000000 | tf_op jit(solution)/shard_map/attend/pallas_call | solution.py:384
  171.6 6.6 all-gather.4.cloned.1.call-done
  178.2 4.9 convolution_convert_fusion
  183.2 59.2 %reduce-scatter.4.cloned.1.call-done = bf16[8,32,1536]{2,1,0:T(8,128)(2,1)} async-done(((bf16[8,128,1536]{2,1,0:T(8,128)(2,1)}), bf16[8,32,1536]{2,1,0:T(8,128)(2,1)}) %reduce-scatter.4.cloned.1.call-update) | async-done | bytes 786448 | tf_op jit(solution)/shard_map/reduce_scatter | solution.py:1016
  246.9 8.2 %fusion.16 = f32[1024,1024]{1,0:T(8,128)} fusion(bf16[1024,1536]{1,0:T(8,128)(2,1)} %bitcast.91, bf16[1024,1536]{1,0:T(8,128)(2,1)} %param.34), kind=kOutput, calls=%fused_computation.88 | convolution fusion | flops 3221225472 | bytes 10485760 | tf_op jit(solution)/shard_map/dot_general | solution.py:52
  255.2 55.2 %all-gather.6.cloned.1.call-done = bf16[8,128,1536]{2,1,0:T(8,128)(2,1)} async-done(((bf16[8,32,1536]{2,1,0:T(8,128)(2,1)}), bf16[8,128,1536]{2,1,0:T(8,128)(2,1)}) %all-gather.6.cloned.1.call-update) | async-done | bytes 3145744 | tf_op jit(solution)/shard_map/all_gather | solution.py:1021
  310.4 6.4 fusion.17
  316.8 6.4 multiply_convert_fusion
  323.2 3.5 fusion.18
  326.7 5.1 add_convert_fusion
  331.9 59.2 %reduce-scatter.6.cloned.1.call-done = bf16[8,32,1536]{2,1,0:T(8,128)(2,1)} async-done(((bf16[8,128,1536]{2,1,0:T(8,128)(2,1)}), bf16[8,32,1536]{2,1,0:T(8,128)(2,1)}) %reduce-scatter.6.cloned.1.call-update) | async-done | bytes 786448 | tf_op jit(solution)/shard_map/reduce_scatter | solution.py:1043
  397.7 6.1 convolution_convert_fusion.3
  403.9 3.7 convolution_convert_fusion.2
  407.7 3.7 convolution_convert_fusion.1
  411.4 4.9 convolution_convert_fusion.4
  416.3 4.2 pad_maximum_fusion.wg_ref
  420.5 39.2 %all-gather.8.cloned.1.call-done = bf16[8,128,1536]{2,1,0:T(8,128)(2,1)} async-done(((bf16[8,32,1536]{2,1,0:T(8,128)(2,1)}), bf16[8,128,1536]{2,1,0:T(8,128)(2,1)}) %all-gather.8.cloned.1.call-update) | async-done | bytes 3145744 | tf_op jit(solution)/shard_map/all_gather | solution.py:1050
  459.7 4.4 convolution_bitcast_fusion.gg_ref
  464.2 139.0 %attend_back.1 = (bf16[8,128,384]{2,1,0:T(8,128)(2,1)}, bf16[8,128,384]{2,1,0:T(8,128)(2,1)}, bf16[8,128,384]{2,1,0:T(8,128)(2,1)}, f32[384,128]{1,0:T(8,128)}, ...) custom-call(f32[3]{0:T(128)} %copy-done.3, bf16[8,128,384]{2,1,0:T(8,128)(2,1)} %get-tuple-element.44.q_ref, ...), custom_call_target="tpu_custom_call" | custom-call | flops 60000002048 | bytes 24000000 | tf_op jit(solution)/shard_map/attend_back/pallas_call | solution.py:413
  612.3 92.7 %finish.1 = (bf16[8,32,1536]{2,1,0:T(8,128)(2,1)}, f32[4,192,384]{2,1,0:T(8,128)}, f32[8,1536]{1,0:T(8,128)}, bf16[2,4,32,1536]{3,2,1,0:T(8,128)(2,1)}) custom-call(bf16[8,128,384]{2,1,0:T(8,128)(2,1)} %get-tuple-element.55.gq_ref, bf16[8,128,384]{2,1,0:T(8,128)(2,1)} %get-tuple-element.56.gk_ref, bf16[8,128,384]{2,1,0:T(8,128)(2,1)} %get-tuple-element.57.gv_ref, ...), custom_call_target="tpu_custom_call" | custom-call | flops 8000000000 | bytes 24000000 | tf_op jit(solution)/shard_map/finish/pallas_call | solution.py:719
  710.0 4.2 all-to-all-start.1
  719.3 6.6 all-to-all-done.1
  (153 shorter events, 64.4 us)
Async XLA Ops:
  7.2 309.6 %copy-start = (bf16[1536,1024]{1,0:T(8,128)(2,1)S(1)}, bf16[1536,1024]{1,0:T(8,128)(2,1)}, u32[]{:S(2)}) copy-start(bf16[1536,1024]{1,0:T(8,128)(2,1)} %param.33) | copy-start | bytes 9437188
  7.2 13.9 %copy-start.14 = (f32[1536]{0:T(1024)S(1)}, f32[1536]{0:T(1024)}, u32[]{:S(2)}) copy-start(f32[1536]{0:T(1024)} %param.21) | copy-start | bytes 18436
  9.4 16.6 %all-to-all-start = ((bf16[4,2,32,1536]{3,2,1,0:T(8,128)(2,1)}), bf16[4,2,32,1536]{3,2,1,0:T(8,128)(2,1)}, u32[]{:S(2)}, u32[]{:S(2)}) async-start(bf16[4,2,32,1536]{3,2,1,0:T(8,128)(2,1)} %copy.52), calls=%async_computation | async-start | bytes 1572864 | tf_op jit(solution)/shard_map/all_to_all | solution.py:987
  13.7 164.5 %all-gather.4.cloned.1.call-start = ((), (), s32[]{:S(2)}) async-start(), calls=%async_computation.5 | async-start | bytes 3932160 | tf_op jit(solution)/shard_map/all_gather | solution.py:1004
  115.5 126.9 %reduce-scatter.4.cloned.1.call-start = ((), (), s32[]{:S(2)}) async-start(), calls=%async_computation.6 | async-start | bytes 3932160 | tf_op jit(solution)/shard_map/reduce_scatter | solution.py:1016
  116.2 51.5 %copy-start.2 = (f32[384,1]{1,0:T(8,128)}, f32[384,1]{1,0:T(8,128)S(1)}, u32[]{:S(2)}) copy-start(f32[384,1]{1,0:T(8,128)S(1)} %reshape.282.gain_ref) | copy-start | bytes 4612
  116.4 51.4 %copy-start.24 = (f32[3]{0:T(128)}, f32[3]{0:T(128)S(1)}, u32[]{:S(2)}) copy-start(f32[3]{0:T(128)S(1)} %get-tuple-element.95) | copy-start | bytes 40
  116.4 51.3 %copy-start.3 = (f32[3]{0:T(128)}, f32[3]{0:T(128)S(1)}, u32[]{:S(2)}) copy-start(f32[3]{0:T(128)S(1)} %subtract_add_fusion.lam_ref) | copy-start | bytes 40
  183.1 61.1 %copy-start.13 = (f32[1536]{0:T(1024)S(1)}, f32[1536]{0:T(1024)}, u32[]{:S(2)}) copy-start(f32[1536]{0:T(1024)} %param.31) | copy-start | bytes 18436
  183.2 127.2 %all-gather.6.cloned.1.call-start = ((), (), s32[]{:S(2)}) async-start(), calls=%async_computation.7 | async-start | bytes 3932160 | tf_op jit(solution)/shard_map/all_gather | solution.py:1021
  246.9 144.1 %reduce-scatter.6.cloned.1.call-start = ((), (), s32[]{:S(2)}) async-start(), calls=%async_computation.8 | async-start | bytes 3932160 | tf_op jit(solution)/shard_map/reduce_scatter | solution.py:1043
  331.8 59.2 %copy-start.9 = (bf16[8,32,1536]{2,1,0:T(8,128)(2,1)S(1)}, bf16[8,32,1536]{2,1,0:T(8,128)(2,1)}, u32[]{:S(2)}) copy-start(bf16[8,32,1536]{2,1,0:T(8,128)(2,1)} %gather_fusion) | copy-start | bytes 2359300
  331.8 59.2 %copy-start.10 = (bf16[8,32,1536]{2,1,0:T(8,128)(2,1)S(1)}, bf16[8,32,1536]{2,1,0:T(8,128)(2,1)}, u32[]{:S(2)}) copy-start(bf16[8,32,1536]{2,1,0:T(8,128)(2,1)} %reduce-scatter.4.cloned.1.call-done) | copy-start | bytes 2359300
  331.8 61.1 %copy-start.11 = (bf16[8,32,1536]{2,1,0:T(8,128)(2,1)S(1)}, bf16[8,32,1536]{2,1,0:T(8,128)(2,1)}, u32[]{:S(2)}) copy-start(bf16[8,32,1536]{2,1,0:T(8,128)(2,1)} %gather_fusion.1) | copy-start | bytes 2359300
  331.8 127.9 %all-gather.8.cloned.1.call-start = ((), (), s32[]{:S(2)}) async-start(), calls=%async_computation.9 | async-start | bytes 3932160 | tf_op jit(solution)/shard_map/all_gather | solution.py:1050
  396.2 212.9 %reduce-scatter.8.cloned.1.call-start = ((), (), s32[]{:S(2)}) async-start(), calls=%async_computation.10 | async-start | bytes 3932160 | tf_op jit(solution)/shard_map/reduce_scatter | solution.py:1054
  416.3 43.4 %copy-start.33 = (bf16[384,1536]{1,0:T(8,128)(2,1)S(1)}, bf16[384,1536]{1,0:T(8,128)(2,1)}, u32[]{:S(2)}) copy-start(bf16[384,1536]{1,0:T(8,128)(2,1)} %param.30) | copy-start | bytes 3538948
  612.3 94.3 %copy-start.25 = (f32[3]{0:T(128)S(1)}, f32[3]{0:T(128)}, u32[]{:S(2)}) copy-start(f32[3]{0:T(128)} %copy-done.24) | copy-start | bytes 40
  612.3 94.3 %copy-start.27 = (f32[3]{0:T(128)S(1)}, f32[3]{0:T(128)}, u32[]{:S(2)}) copy-start(f32[3]{0:T(128)} %copy-done.26) | copy-start | bytes 40
  705.0 9.2 %copy-start.16 = (f32[3,64]{1,0:T(4,128)S(1)}, f32[3,64]{1,0:T(4,128)}, u32[]{:S(2)}) copy-start(f32[3,64]{1,0:T(4,128)} %param.25) | copy-start | bytes 2308
  705.0 11.2 %copy-start.20 = (f32[3,64]{1,0:T(4,128)S(1)}, f32[3,64]{1,0:T(4,128)}, u32[]{:S(2)}) copy-start(f32[3,64]{1,0:T(4,128)} %param.27) | copy-start | bytes 2308
  705.0 11.2 %copy-start.22 = (f32[3,64]{1,0:T(4,128)S(1)}, f32[3,64]{1,0:T(4,128)}, u32[]{:S(2)}) copy-start(f32[3,64]{1,0:T(4,128)} %param.28) | copy-start | bytes 2308
  710.0 15.9 %all-to-all-start.1 = ((bf16[4,2,32,1536]{3,2,1,0:T(8,128)(2,1)}), bf16[4,2,32,1536]{3,2,1,0:T(8,128)(2,1)}, u32[]{:S(2)}, u32[]{:S(2)}) async-start(bf16[4,2,32,1536]{3,2,1,0:T(8,128)(2,1)} %bitcast.23), calls=%async_computation.4 | async-start | bytes 1572864 | tf_op jit(solution)/shard_map/all_to_all | solution.py:992
  716.8 12.6 %copy-start.1 = (bf16[1536,1024]{1,0:T(8,128)(2,1)S(1)}, bf16[1536,1024]{1,0:T(8,128)(2,1)}, u32[]{:S(2)}) copy-start(bf16[1536,1024]{1,0:T(8,128)(2,1)} %param.33) | copy-start | bytes 9437188
  (24 other events, 101.1 us)
Sparse Core Ops, SparseCore 0:
  115.6 62.5 all-gather.3
  183.3 59.0 reduce-scatter.3
  247.0 63.3 all-gather.5
  331.9 59.0 reduce-scatter.5
  396.3 63.3 all-gather.7
  464.3 59.0 reduce-scatter.7

commit v5 on v4

--- a/solution.py
+++ b/solution.py
@@ -924,6 +924,204 @@
         cost_estimate=pl.CostEstimate(
             flops=4_000_000_000, bytes_accessed=16_000_000, transcendentals=0),
         name="open_rows",
+    )(*operands)
+
+
+def greet_line(axis, size):
+    place = lax.axis_index(axis)
+    greet([{axis: lax.rem(place + step, size)} for step in range(1, size)])
+
+
+def scatter_terms(own_ref, q, cols, terms, dims, lines):
+    slots, parts, heads, tile, width, strip = dims
+    for p in range(terms.shape[0] // tile):
+        for z in range(lines):
+            own_ref[q, z, p * strip:(p + 1) * strip, cols] = (
+                terms[p * tile + z * strip:p * tile + (z + 1) * strip])
+
+
+def line_turn(lines, chunks, summed, gathered, before, between):
+    for slot in range(chunks + 2 * (lines - 1)):
+        if slot < chunks:
+            before(slot)
+        for t in range(lines - 1):
+            if 0 <= slot - t < chunks:
+                summed.step(slot - t, t)
+        q = slot - lines + 1
+        if 0 <= q < chunks:
+            between(q)
+        for t in range(lines):
+            if 0 <= q - t < chunks:
+                gathered.step(q - t, t)
+    for q in range(chunks):
+        summed.drain(q)
+        gathered.drain(q)
+
+
+def feed_open_kernel(dims, lines, chunks, grouped_ref, wo_ref, inputs_ref, gain_ref, grad_ref,
+                     down_ref, hidden_ref, rows_ref, gact_ref,
+                     own_ref, left_ref, right_ref, acc_ref, line_sem, gather_sem):
+    slots, parts, heads, tile, width, strip = dims
+    full = heads * width
+    per = slots // chunks
+    model = inputs_ref.shape[-1]
+    units = down_ref.shape[0]
+    block = 256
+    place = lax.axis_index("head")
+    greet_line("head", lines)
+    summed = LineSum("head", lines, own_ref, left_ref, right_ref, line_sem)
+    gathered = LineGather(
+        "head", lines, lambda q, s: rows_ref.at[pl.ds(q * per, per), s], gather_sem)
+
+    def before(q):
+        left = grouped_ref[q * per:(q + 1) * per].reshape(per * tile, full)
+
+        def columns(index, carry):
+            cols = pl.ds(pl.multiple_of(index * block, block), block)
+            scatter_terms(own_ref, q, cols, dot(left, wo_ref[:, cols]).astype(BF16), dims, lines)
+            return carry
+
+        lax.fori_loop(0, model // block, columns, 0)
+
+    def between(q):
+        summed.total(q, acc_ref)
+        hidden = inputs_ref[q * per:(q + 1) * per].reshape(per * strip, model).astype(F32)
+        hidden = hidden + acc_ref[...]
+        hidden_ref[q * per:(q + 1) * per] = hidden.reshape(per, strip, model)
+        scale = lax.rsqrt(jnp.mean(hidden * hidden, axis=1, keepdims=True) + EPSILON)
+        low = (hidden * scale * gain_ref[...]).astype(BF16).reshape(per, strip, model)
+        for p in range(per):
+            rows_ref[q * per + p, place] = low[p]
+
+    def extra(q):
+        grads = grad_ref[q * per:(q + 1) * per].reshape(per * tile, model)
+
+        def columns(index, carry):
+            cols = pl.ds(pl.multiple_of(index * block, block), block)
+            result = dot_turned(grads, down_ref[cols, :])
+            gact_ref[q * per:(q + 1) * per, :, cols] = result.reshape(per, tile, block)
+            return carry
+
+        lax.fori_loop(0, units // block, columns, 0)
+
+    def before_all(q):
+        before(q)
+        if q > 0:
+            extra(q - 1)
+        if q == chunks - 1:
+            extra(q)
+
+    line_turn(lines, chunks, summed, gathered, before_all, between)
+
+
+def feed_open(dims, lines, chunks, *operands):
+    slots, parts, heads, tile, width, strip = dims
+    model, units = operands[1].shape[1], operands[5].shape[0]
+    return pl.pallas_call(
+        partial(feed_open_kernel, dims, lines, chunks),
+        out_shape=(
+            jax.ShapeDtypeStruct((slots, strip, model), F32),
+            jax.ShapeDtypeStruct((slots, lines, strip, model), BF16),
+            jax.ShapeDtypeStruct((slots, tile, units), F32),
+        ),
+        in_specs=specs(6, 0),
+        out_specs=specs(3, 0),
+        scratch_shapes=line_scratch(chunks, lines, slots // chunks * strip, model) + [
+            pltpu.SemaphoreType.DMA((2, 2, chunks, lines)),
+        ],
+        compiler_params=pltpu.CompilerParams(
+            vmem_limit_bytes=60 << 20, collective_id=4, has_side_effects=True),
+        cost_estimate=pl.CostEstimate(
+            flops=4_000_000_000, bytes_accessed=20_000_000, transcendentals=0),
+        name="feed_open",
+    )(*operands)
+
+
+def feed_close_kernel(dims, lines, chunks, gg_ref, gu_ref, wg_ref, wu_ref, rows_ref, grad_ref,
+                      act_ref, hidden_ref, cot_ref, gain_ref,
+                      gh_ref, branch_ref, terms_ref, part_ref,
+                      own_ref, left_ref, right_ref, acc_ref, line_sem, gather_sem):
+    slots, parts, heads, tile, width, strip = dims
+    per = slots // chunks
+    model = cot_ref.shape[-1]
+    units = act_ref.shape[-1]
+    block, narrow = 256, 128
+    place = lax.axis_index("head")
+    greet_line("head", lines)
+    summed = LineSum("head", lines, own_ref, left_ref, right_ref, line_sem)
+    gathered = LineGather(
+        "head", lines, lambda q, s: branch_ref.at[pl.ds(q * per, per), s], gather_sem)
+    part_ref[...] = jnp.zeros_like(part_ref)
+
+    def weight_term(kind):
+        left_rows = grad_ref if kind == 2 else rows_ref
+        right_rows = (gg_ref, gu_ref, act_ref)[kind]
+
+        def columns(index, carry):
+            cols = pl.ds(pl.multiple_of(index * narrow, narrow), narrow)
+            term = jnp.zeros((narrow, units), F32)
+            for s in range(0, slots, 2):
+                left = left_rows[s:s + 2, :, cols].reshape(2 * tile, narrow)
+                term += dot(jnp.transpose(left), right_rows[s:s + 2].reshape(2 * tile, units))
+            terms_ref[kind, cols] = term.astype(BF16)
+            return carry
+
+        lax.fori_loop(0, model // narrow, columns, 0)
+
+    def before(q):
+        gate = gg_ref[q * per:(q + 1) * per].reshape(per * tile, units)
+        up = gu_ref[q * per:(q + 1) * per].reshape(per * tile, units)
+
+        def columns(index, carry):
+            cols = pl.ds(pl.multiple_of(index * block, block), block)
+            terms = dot_turned(gate, wg_ref[cols, :]) + dot_turned(up, wu_ref[cols, :])
+            scatter_terms(own_ref, q, cols, terms.astype(BF16), dims, lines)
+            return carry
+
+        lax.fori_loop(0, model // block, columns, 0)
+        if q > 0:
+            weight_term(q - 1)
+
+    def between(q):
+        summed.total(q, acc_ref)
+        grad = acc_ref[...]
+        hidden = hidden_ref[q * per:(q + 1) * per].reshape(per * strip, model)
+        scale = lax.rsqrt(jnp.mean(hidden * hidden, axis=1, keepdims=True) + EPSILON)
+        part_ref[...] += jnp.sum(
+            (grad * (hidden * scale)).reshape(per * strip // 8, 8, model), axis=0)
+        up = grad * gain_ref[...]
+        result = (cot_ref[q * per:(q + 1) * per].reshape(per * strip, model).astype(F32)
+                  + scale * up
+                  - hidden * (scale * scale * scale * jnp.mean(up * hidden, axis=1, keepdims=True)))
+        gh_ref[q * per:(q + 1) * per] = result.reshape(per, strip, model)
+        low = result.astype(BF16).reshape(per, strip, model)
+        for p in range(per):
+            branch_ref[q * per + p, place] = low[p]
+
+    line_turn(lines, chunks, summed, gathered, before, between)
+
+
+def feed_close(dims, lines, chunks, *operands):
+    slots, parts, heads, tile, width, strip = dims
+    model, units = operands[8].shape[-1], operands[6].shape[-1]
+    return pl.pallas_call(
+        partial(feed_close_kernel, dims, lines, chunks),
+        out_shape=(
+            jax.ShapeDtypeStruct((slots, strip, model), F32),
+            jax.ShapeDtypeStruct((slots, lines, strip, model), BF16),
+            jax.ShapeDtypeStruct((3, model, units), BF16),
+            jax.ShapeDtypeStruct((8, model), F32),
+        ),
+        in_specs=specs(10, 0),
+        out_specs=specs(4, 0),
+        scratch_shapes=line_scratch(chunks, lines, slots // chunks * strip, model) + [
+            pltpu.SemaphoreType.DMA((2, 2, chunks, lines)),
+        ],
+        compiler_params=pltpu.CompilerParams(
+            vmem_limit_bytes=60 << 20, collective_id=5, has_side_effects=True),
+        cost_estimate=pl.CostEstimate(
+            flops=16_000_000_000, bytes_accessed=40_000_000, transcendentals=0),
+        name="feed_close",
     )(*operands)
 
 
@@ -1008,53 +1206,34 @@
         dims, part_arr, lambda_head, queries, kv_all,
         gain_col)
     grouped, grad_rows = lax.optimization_barrier((grouped, grad_rows))
-    grouped = grouped.reshape(row_count, qwidth)
-    grad_rows = grad_rows.reshape(row_count, model_width)
-    attn_terms = jnp.dot(grouped, output_weight, preferred_element_type=jnp.float32).reshape(
-        rows_shape
-    )
-    hidden = tokens + lax.psum_scatter(
-        attn_terms.astype(jnp.bfloat16), "head", scatter_dimension=1, tiled=True
-    ).astype(jnp.float32)
-    scale_two = rms_scale(hidden)
-    normed_two = (hidden * scale_two * feed_gain).astype(jnp.bfloat16)
-    feed_rows = lax.all_gather(normed_two, "head", axis=1, tiled=True).reshape(
-        row_count, model_width
-    )
+    hidden, feed_rows, grad_activ = feed_open(
+        dims, head_total, 4, grouped, output_weight, inputs_here,
+        feed_gain.reshape(1, model_width), grad_rows, down_weight)
+    feed_rows = feed_rows.reshape(row_count, model_width)
+    grad_activ = grad_activ.reshape(row_count, grad_activ.shape[-1])
     gate_vals = jnp.dot(feed_rows, gate_weight, preferred_element_type=jnp.float32)
     up_vals = jnp.dot(feed_rows, up_weight, preferred_element_type=jnp.float32)
     gate_sigmoid = jax.nn.sigmoid(gate_vals)
     silu_gate = gate_vals * gate_sigmoid
     activation = (silu_gate * up_vals).astype(jnp.bfloat16)
-    feed_terms = jnp.dot(activation, down_weight, preferred_element_type=jnp.float32).reshape(
-        rows_shape
-    )
-    down_term = contract_rows(grad_rows, activation)
-    grad_activ = contract_cols(grad_rows, down_weight)
     grad_gate = (
         grad_activ * up_vals * gate_sigmoid * (1.0 + gate_vals * (1.0 - gate_sigmoid))
     ).astype(jnp.bfloat16)
     grad_up = (grad_activ * silu_gate).astype(jnp.bfloat16)
-    gate_term = contract_rows(feed_rows, grad_gate)
-    up_term = contract_rows(feed_rows, grad_up)
-    normed_two_terms = (
-        contract_cols(grad_gate, gate_weight) + contract_cols(grad_up, up_weight)
-    ).reshape(rows_shape)
-    grad_normed_two = lax.psum_scatter(
-        normed_two_terms.astype(jnp.bfloat16), "head", scatter_dimension=1, tiled=True
-    ).astype(jnp.float32)
-    feed_part = jnp.sum(grad_normed_two * hidden * scale_two, axis=(0, 1))
-    grad_hidden = cotangent_here.astype(jnp.float32) + norm_back(
-        grad_normed_two, hidden, scale_two, feed_gain
+    unit_shape = (slots, tile, activation.shape[-1])
+    grad_hidden, branch_rows, wgrads, feed_part = feed_close(
+        dims, head_total, 4, grad_gate.reshape(unit_shape), grad_up.reshape(unit_shape),
+        gate_weight, up_weight, feed_rows.reshape(slots, tile, model_width), grad_rows,
+        activation.reshape(unit_shape), hidden, cotangent_here, feed_gain.reshape(1, model_width))
+    feed_part = jnp.sum(feed_part, axis=0)
+    branch_rows = branch_rows.reshape(row_count, model_width)
+    feed_terms = jnp.dot(activation, down_weight, preferred_element_type=jnp.float32).reshape(
+        rows_shape
     )
-    branch_rows = lax.all_gather(
-        grad_hidden.astype(jnp.bfloat16), "head", axis=1, tiled=True
-    ).reshape(row_count, model_width)
     branch_rows, feed_terms = lax.optimization_barrier((branch_rows, feed_terms.astype(BF16)))
     feed_sum = lax.psum_scatter(feed_terms, "head", scatter_dimension=1, tiled=True)
     grad_grouped = contract_cols(output_weight, branch_rows)
     shares = lax.axis_size("dp") * parts
-    wgrads = jnp.stack([gate_term.astype(BF16), up_term.astype(BF16), down_term.astype(BF16)])
     wgrads = wgrads.reshape(3, groups, 2, model_width // shares, wgrads.shape[-1])
     grad_query, grad_key, grad_value, group_part, lambda_part, feed_sums = attend_back(
         dims, groups, lambda_head, queries, kv_all,

time: 744 us -> 688 us (0.925)
  Pallas kernels: 361 us -> 577 us
  waiting for transfers between devices: 228 us -> 21.8 us
  matrix products: 57.4 us -> 21.8 us
  other arithmetic: 32.2 us -> 13.8 us
  local copies, waits for them, and re-layouts: 33.1 us -> 23.3 us
    pallas_call x0 -> x2, Pallas kernels: none -> 215 us  [the longest x1 113 us: feed_close(): pl.pallas_call(partial(feed_close_kernel, dims, lines, chunks), out_shape...]
    reduce_scatter x2 -> x0, waiting for transfers between devices: 118 us -> none  [the longest x1 59.2 us: per_device(): lax.psum_scatter(normed_two_terms.astype(jnp.bfloat16), 'head', scatter_d...]
    all_gather x2 -> x0, waiting for transfers between devices: 94.4 us -> none  [the longest x1 55.2 us: per_device(): lax.all_gather(normed_two, 'head', axis=1, tiled=True)]
    dot_general x4 -> x0, matrix products: 18.5 us -> none  [the longest x3 13.6 us: contract_rows(): lax.dot_general(left, right, (((0,), (0,)), ((), ())), preferred_element_...]
    dot_general x4 -> x1, matrix products: 21.2 us -> 4.45 us  [contract_cols(): lax.dot_general(left, right, (((1,), (1,)), ((), ())), preferred_element_...]
  transfers between devices with their start and end apart: 8 -> 4, of which waited for: 7 -> 3; matrix products, arithmetic and copies ran while one was open for 7% -> 2% of each run, Pallas kernels for 26% -> 28%
where the time goes in v5:
time: 688 us; the launch traced here: 681 us
  Pallas kernels  577 us (84%)
  local copies, waits for them, and re-layouts  23.3 us (3%)
  waiting for transfers between devices  21.8 us (3%)
  matrix products  21.8 us (3%)
  between operations  15 us (2%)
  other arithmetic  13.8 us (2%)
  starting transfers between devices  7.97 us (1%)
    pallas_call x1, Pallas kernels, attend_back(): pl.pallas_call(partial(attend_back_kernel, dims, groups), out_shape=(rows...  139 us
    pallas_call x1, Pallas kernels, feed_close(): pl.pallas_call(partial(feed_close_kernel, dims, lines, chunks), out_shape...  113 us
    pallas_call x1, Pallas kernels, feed_open(): pl.pallas_call(partial(feed_open_kernel, dims, lines, chunks), out_shape=...  102 us
    pallas_call x1, Pallas kernels, finish(): pl.pallas_call(partial(finish_kernel, dims, groups, lines), out_shape=(ja...  93.8 us
    pallas_call x1, Pallas kernels, open_rows(): pl.pallas_call(partial(open_kernel, dims, lines, chunks), out_shape=(jax....  79.7 us
    pallas_call x1, Pallas kernels, attend(): pl.pallas_call(partial(attend_kernel, dims), out_shape=(jax.ShapeDtypeStr...  49.7 us
  transfers between devices with their start and end apart: 4, of which 3 were waited for; matrix products, arithmetic and copies ran while one was open for 2% of the time, Pallas kernels for 28%

profile of v5, /device:TPU:0, one launch (start us, length us, event | category | flops | bytes accessed | tf_op | source)
XLA Modules:
  0.0 680.8 jit_solution(10602999329388606324)
XLA Ops:
  7.2 2.1 copy.52
  9.3 4.3 all-to-all-start
  17.9 7.2 %all-to-all-done = bf16[4,2,32,1536]{3,2,1,0:T(8,128)(2,1)S(1)} async-done(((bf16[4,2,32,1536]{3,2,1,0:T(8,128)(2,1)}), bf16[4,2,32,1536]{3,2,1,0:T(8,128)(2,1)S(1)}, u32[]{:S(2)}, u32[]{:S(2)}) %all-to-all-start) | async-done | bytes 786464 | tf_op jit(solution)/shard_map/all_to_all | solution.py:1185
  26.8 79.7 %open_rows.1 = (bf16[8,4,32,1536]{3,2,1,0:T(8,128)(2,1)}, bf16[8,128,384]{2,1,0:T(8,128)(2,1)}, bf16[4,8,2,128,384]{4,3,2,1,0:T(8,128)(2,1)}, bf16[4,2,32,1536]{3,2,1,0:T(8,128)(2,1)}) custom-call(bf16[8,32,1536]{2,1,0:T(8,128)(2,1)} %broadcast_select_fusion.3.x_ref.inputs_ref, f32[1,1536]{1,0:T(1,128)} %reshape.208.gain_ref, bf16[1536,384]{1,0:T(8,128)(2,1)} %wq_ref.3, ...), custom_call_target="tpu_custom_call" | custom-call | flops 4000000000 | bytes 16000000 | tf_op jit(solution)/shard_map/open_rows/pallas_call | solution.py:905
  106.6 1.8 gather_fusion.1
  110.7 1.2 multiply_sine_fusion
  112.0 49.7 %attend.1 = (bf16[8,128,384]{2,1,0:T(8,128)(2,1)S(1)}, f32[8,3,128,128]{3,2,1,0:T(8,128)S(1)}, f32[8,3,128,128]{3,2,1,0:T(8,128)S(1)}, f32[8,3,1,256]{3,2,1,0:T(1,128)S(1)}) custom-call(s32[1]{0:T(128)} %bitcast.part_ref, f32[3]{0:T(128)S(1)} %subtract_add_fusion.lam_ref, bf16[8,128,384]{2,1,0:T(8,128)(2,1)S(1)} %copy-done.3, ...), custom_call_target="tpu_custom_call" | custom-call | flops 20000000000 | bytes 12000000 | tf_op jit(solution)/shard_map/attend/pallas_call | solution.py:384
  165.6 6.6 all-gather.2.cloned.1.call-done.grad_ref
  172.3 102.3 %feed_open.1 = (f32[8,32,1536]{2,1,0:T(8,128)}, bf16[8,4,32,1536]{3,2,1,0:T(8,128)(2,1)}, f32[8,128,1024]{2,1,0:T(8,128)}) custom-call(bf16[8,128,384]{2,1,0:T(8,128)(2,1)} %copy-done.2, bf16[384,1536]{1,0:T(8,128)(2,1)} %wo_ref.1, bf16[8,32,1536]{2,1,0:T(8,128)(2,1)} %broadcast_select_fusion.3.x_ref.inputs_ref, f32[1,1536]{1,0:T(1,128)} %reshape.212.gain_ref, ...), custom_call_target="tpu_custom_call" | custom-call | flops 4000000000 | bytes 20000000 | tf_op jit(solution)/shard_map/feed_open/pallas_call | solution.py:1020
  274.6 5.4 fusion.10
  280.1 7.0 %multiply_convert_fusion = (bf16[1024,1024]{1,0:T(8,128)(2,1)S(1)}, bf16[1024,1024]{1,0:T(8,128)(2,1)}, bf16[1024,1024]{1,0:T(8,128)(2,1)}) fusion(f32[1024,1024]{1,0:T(8,128)S(1)} %fusion.10, f32[8,128,1024]{2,1,0:T(8,128)S(1)} %copy-done.25, bf16[1024,1536]{1,0:T(8,128)(2,1)S(1)} %bitcast.91, bf16[1536,1024]{1,0:T(8,128)(2,1)S(1)} %copy-done.20), kind=kOutput, calls=%fused_computation.10 | convolution fusion | flops 3236954112 | bytes 20971520 | tf_op jit(solution)/shard_map/dot_general | solution.py:1215
  287.2 4.8 convolution_convert_fusion
  292.0 112.5 %feed_close.1 = (f32[8,32,1536]{2,1,0:T(8,128)}, bf16[8,4,32,1536]{3,2,1,0:T(8,128)(2,1)}, bf16[3,1536,1024]{2,1,0:T(8,128)(2,1)}, f32[8,1536]{1,0:T(8,128)}) custom-call(bf16[8,128,1024]{2,1,0:T(8,128)(2,1)} %bitcast.93, bf16[8,128,1024]{2,1,0:T(8,128)(2,1)} %bitcast.94, bf16[1536,1024]{1,0:T(8,128)(2,1)} %wg_ref.1, bf16[1536,1024]{1,0:T(8,128)(2,1)} %wu_ref.1, ...), custom_call_target="tpu_custom_call" | custom-call | flops 16000000000 | bytes 40000000 | tf_op jit(solution)/shard_map/feed_close/pallas_call | solution.py:1107
  404.5 4.4 convolution_bitcast_fusion.gg_ref
  409.0 139.1 %attend_back.1 = (bf16[8,128,384]{2,1,0:T(8,128)(2,1)}, bf16[8,128,384]{2,1,0:T(8,128)(2,1)}, bf16[8,128,384]{2,1,0:T(8,128)(2,1)}, f32[384,128]{1,0:T(8,128)}, ...) custom-call(f32[3]{0:T(128)} %copy-done.1, bf16[8,128,384]{2,1,0:T(8,128)(2,1)} %get-tuple-element.50.q_ref, ...), custom_call_target="tpu_custom_call" | custom-call | flops 60000002048 | bytes 24000000 | tf_op jit(solution)/shard_map/attend_back/pallas_call | solution.py:413
  551.2 3.1 slice_bitcast_fusion
  554.2 1.4 add_convert_fusion
  557.2 93.8 %finish.1 = (bf16[8,32,1536]{2,1,0:T(8,128)(2,1)}, f32[4,192,384]{2,1,0:T(8,128)}, f32[8,1536]{1,0:T(8,128)}, bf16[2,4,32,1536]{3,2,1,0:T(8,128)(2,1)}) custom-call(bf16[8,128,384]{2,1,0:T(8,128)(2,1)} %get-tuple-element.67.gq_ref, bf16[8,128,384]{2,1,0:T(8,128)(2,1)} %get-tuple-element.68.gk_ref, bf16[8,128,384]{2,1,0:T(8,128)(2,1)} %get-tuple-element.69.gv_ref, ...), custom_call_target="tpu_custom_call" | custom-call | flops 8000000000 | bytes 24000000 | tf_op jit(solution)/shard_map/finish/pallas_call | solution.py:719
  651.0 1.6 slice_reduce_fusion
  653.2 1.7 gather_fusion.3
  656.0 3.5 all-to-all-start.1
  660.2 1.3 slice_reduce_fusion.2
  663.1 8.0 %all-to-all-done.1 = bf16[4,2,32,1536]{3,2,1,0:T(8,128)(2,1)S(1)} async-done(((bf16[4,2,32,1536]{3,2,1,0:T(8,128)(2,1)}), bf16[4,2,32,1536]{3,2,1,0:T(8,128)(2,1)S(1)}, u32[]{:S(2)}, u32[]{:S(2)}) %all-to-all-start.1) | async-done | bytes 786464 | tf_op jit(solution)/shard_map/all_to_all | solution.py:1190
  671.3 1.3 copy.60
  (103 shorter events, 21.9 us)
Async XLA Ops:
  7.2 6.4 copy-start.22
  7.2 9.3 %copy-start.11 = (f32[1536]{0:T(1024)S(1)}, f32[1536]{0:T(1024)}, u32[]{:S(2)}) copy-start(f32[1536]{0:T(1024)} %param.21) | copy-start | bytes 18436
  9.3 15.9 %all-to-all-start = ((bf16[4,2,32,1536]{3,2,1,0:T(8,128)(2,1)}), bf16[4,2,32,1536]{3,2,1,0:T(8,128)(2,1)S(1)}, u32[]{:S(2)}, u32[]{:S(2)}) async-start(bf16[4,2,32,1536]{3,2,1,0:T(8,128)(2,1)} %copy.52), calls=%async_computation | async-start | bytes 1572864 | tf_op jit(solution)/shard_map/all_to_all | solution.py:1185
  13.5 158.7 %all-gather.2.cloned.1.call-start = ((), (), s32[]{:S(2)}) async-start(), calls=%async_computation.3 | async-start | bytes 3932160 | tf_op jit(solution)/shard_map/all_gather | solution.py:1202
  106.6 3.9 copy-start.13
  106.6 3.9 copy-start.14
  106.6 3.9 copy-start.15
  106.6 3.9 copy-start.16
  106.6 5.4 copy-start.3
  109.5 444.8 %reduce-scatter.2.cloned.1.call-start = ((), (), s32[]{:S(2)}) async-start(), calls=%async_computation.4 | async-start | bytes 3932160 | tf_op jit(solution)/shard_map/reduce_scatter | solution.py:1234
  109.8 51.8 %copy-start = (f32[384,1]{1,0:T(8,128)}, f32[384,1]{1,0:T(8,128)S(1)}, u32[]{:S(2)}) copy-start(f32[384,1]{1,0:T(8,128)S(1)} %reshape.270.gain_ref) | copy-start | bytes 4612
  110.7 51.0 %copy-start.1 = (f32[3]{0:T(128)}, f32[3]{0:T(128)S(1)}, u32[]{:S(2)}) copy-start(f32[3]{0:T(128)S(1)} %subtract_add_fusion.lam_ref) | copy-start | bytes 40
  172.3 102.3 %copy-start.19 = (bf16[1536,1024]{1,0:T(8,128)(2,1)S(1)}, bf16[1536,1024]{1,0:T(8,128)(2,1)}, u32[]{:S(2)}) copy-start(bf16[1536,1024]{1,0:T(8,128)(2,1)} %wg_ref.1) | copy-start | bytes 9437188
  274.6 5.5 copy-start.20
  274.6 5.5 copy-start.23
  274.6 5.5 copy-start.25
  280.1 7.1 %copy-start.18 = (bf16[1024,1536]{1,0:T(8,128)(2,1)S(1)}, bf16[1024,1536]{1,0:T(8,128)(2,1)}, u32[]{:S(2)}) copy-start(bf16[1024,1536]{1,0:T(8,128)(2,1)} %down_ref.1) | copy-start | bytes 9437188
  287.2 4.9 copy-start.24
  292.0 112.5 %copy-start.21 = (bf16[384,1536]{1,0:T(8,128)(2,1)S(1)}, bf16[384,1536]{1,0:T(8,128)(2,1)}, u32[]{:S(2)}) copy-start(bf16[384,1536]{1,0:T(8,128)(2,1)} %wo_ref.1) | copy-start | bytes 3538948
  409.0 141.4 %copy-start.10 = (f32[8,1536]{1,0:T(8,128)S(1)}, f32[8,1536]{1,0:T(8,128)}, u32[]{:S(2)}) copy-start(f32[8,1536]{1,0:T(8,128)} %get-tuple-element.72) | copy-start | bytes 147460
  548.1 6.1 copy-start.7
  651.0 11.1 %copy-start.8 = (f32[4,192,384]{2,1,0:T(8,128)S(1)}, f32[4,192,384]{2,1,0:T(8,128)}, u32[]{:S(2)}) copy-start(f32[4,192,384]{2,1,0:T(8,128)} %get-tuple-element.79) | copy-start | bytes 3538948
  656.0 15.1 %all-to-all-start.1 = ((bf16[4,2,32,1536]{3,2,1,0:T(8,128)(2,1)}), bf16[4,2,32,1536]{3,2,1,0:T(8,128)(2,1)S(1)}, u32[]{:S(2)}, u32[]{:S(2)}) async-start(bf16[4,2,32,1536]{3,2,1,0:T(8,128)(2,1)} %bitcast.23), calls=%async_computation.2 | async-start | bytes 1572864 | tf_op jit(solution)/shard_map/all_to_all | solution.py:1190
  663.1 9.5 %copy-start.9 = (bf16[2,4,32,1536]{3,2,1,0:T(8,128)(2,1)S(1)}, bf16[2,4,32,1536]{3,2,1,0:T(8,128)(2,1)}, u32[]{:S(2)}) copy-start(bf16[2,4,32,1536]{3,2,1,0:T(8,128)(2,1)} %get-tuple-element.76) | copy-start | bytes 2359300
  (6 other events, 10.4 us)
Sparse Core Ops, SparseCore 0:
  109.6 62.6 all-gather.1
  409.1 58.5 reduce-scatter.1

commit v6 on v5

--- a/solution.py
+++ b/solution.py
@@ -169,8 +169,8 @@
                        gq_ref, gk_ref, gv_ref, gpart_ref, lpart_ref, wsum_ref,
                        kt_ref, qbdt_ref, qbd_ref, gt_ref, g_ref, delta_ref, dqt_ref,
                        dka_ref, dva_ref, sb_ref, r1_ref, s2_ref, r2_ref,
-                       wown_ref, wr1_ref, wr2_ref,
-                       s1_sem, r1_sem, s2_sem, r2_sem, w1_sem, w2s_sem, w2r_sem):
+                       wr2_ref,
+                       s1_sem, r1_sem, s2_sem, r2_sem, w2s_sem, w2r_sem):
     slots, parts, heads, tile, width, strip = dims
     half = width // 2
     scale = half ** -0.5
@@ -190,36 +190,19 @@
     others = [lax.rem(me + step, groups) for step in range(1, groups)]
     greet([sibling] + [group_device(index) for index in others])
 
-    weights_out = mesh_copy(
-        wg_ref.at[:, :, other_core], wr1_ref, w1_sem.at[0], w1_sem.at[1], sibling)
-    weights_out.start()
-    weights_own = pltpu.make_async_copy(wg_ref.at[:, :, core], wown_ref, w1_sem.at[2])
-    weights_own.start()
-
     def weights_send(step):
         index = others[step]
-        return mesh_copy(wown_ref.at[:, index], wr2_ref.at[step], w2s_sem.at[step],
+        return mesh_copy(wg_ref.at[:, index], wr2_ref.at[step], w2s_sem.at[step],
                          w2r_sem.at[step], group_device(index))
 
-    def weights_cross():
-        weights_out.wait()
-        weights_own.wait()
-
-        def add(index, carry):
-            for t in range(wown_ref.shape[0]):
-                wown_ref[t, index] = (
-                    wown_ref[t, index].astype(F32) + wr1_ref[t, index].astype(F32)).astype(BF16)
-            return carry
-
-        lax.fori_loop(0, groups, add, 0)
-        for step in range(groups - 1):
-            weights_send(step).start()
+    for step in range(groups - 1):
+        weights_send(step).start()
 
     def weights_finish():
         for step in range(groups - 1):
             weights_send(step).wait()
-        for t in range(wown_ref.shape[0]):
-            total = wown_ref[t, me].astype(F32)
+        for t in range(wg_ref.shape[0]):
+            total = wg_ref[t, me].astype(F32)
             for step in range(groups - 1):
                 total = total + wr2_ref[step, t].astype(F32)
             wsum_ref[t] = total
@@ -333,10 +316,6 @@
         def _():
             pass_on(j - 1)
 
-        @pl.when(j == 0)
-        def _():
-            weights_cross()
-
         @pl.when(j >= 2)
         def _():
             finish(j - 2)
@@ -420,7 +399,7 @@
             jax.ShapeDtypeStruct((heads, width, tile), F32),
             jax.ShapeDtypeStruct((kinds, rows, cols), F32),
         ),
-        in_specs=specs(12, 1) + [pl.BlockSpec(memory_space=pl.ANY)],
+        in_specs=specs(13, 1),
         out_specs=specs(6, 0),
         scratch_shapes=[
             pltpu.VMEM((heads, width, parts * tile), BF16),
@@ -436,14 +415,11 @@
             pltpu.VMEM((slots, 2, 2, tile, full), BF16),
             pltpu.VMEM((slots, 2, tile, full), BF16),
             pltpu.VMEM((slots, 2, tile, full), BF16),
-            pltpu.VMEM((kinds, groups, rows, cols), BF16),
-            pltpu.VMEM((kinds, groups, rows, cols), BF16),
             pltpu.VMEM((groups - 1, kinds, rows, cols), BF16),
             pltpu.SemaphoreType.DMA((slots,)),
             pltpu.SemaphoreType.DMA((slots,)),
             pltpu.SemaphoreType.DMA((slots,)),
             pltpu.SemaphoreType.DMA((slots,)),
-            pltpu.SemaphoreType.DMA((3,)),
             pltpu.SemaphoreType.DMA((groups - 1,)),
             pltpu.SemaphoreType.DMA((groups - 1,)),
         ],
@@ -601,32 +577,32 @@
     def share(index, which):
         return pl.ds(pl.multiple_of((index * 2 + which) * rows, 16), rows)
 
-    def weights_out(index):
-        return mesh_copy(wloc_ref.at[:, share(index, other_core)], wr1_ref.at[:, index],
-                         w1_sem.at[0, index], w1_sem.at[1, index], sibling)
-
-    def weights_send(step):
+    def weights_out(kind, index):
+        return mesh_copy(wloc_ref.at[kind, share(index, other_core)], wr1_ref.at[kind, index],
+                         w1_sem.at[0, kind, index], w1_sem.at[1, kind, index], sibling)
+
+    def weights_send(kind, step):
         index = others[step]
-        return mesh_copy(wloc_ref.at[:, share(index, core)], wr2_ref.at[step], w2_sem.at[0, step],
-                         w2_sem.at[1, step], group_device(index))
-
-    def weights_cross():
+        return mesh_copy(wloc_ref.at[kind, share(index, core)], wr2_ref.at[step, kind],
+                         w2_sem.at[0, kind, step], w2_sem.at[1, kind, step],
+                         group_device(index))
+
+    def weights_cross(kind):
         for index in range(groups):
-            weights_out(index).wait()
+            weights_out(kind, index).wait()
 
         def add(index, carry):
-            for k in range(4):
-                wloc_ref[k, share(index, core)] = (
-                    wloc_ref[k, share(index, core)].astype(F32) + wr1_ref[k, index].astype(F32)
-                ).astype(BF16)
+            wloc_ref[kind, share(index, core)] = (
+                wloc_ref[kind, share(index, core)].astype(F32)
+                + wr1_ref[kind, index].astype(F32)).astype(BF16)
             return carry
 
         lax.fori_loop(0, groups, add, 0)
 
     def weights_finish():
-        for step in range(groups - 1):
-            weights_send(step).wait()
         for k in range(4):
+            for step in range(groups - 1):
+                weights_send(k, step).wait()
             total = wloc_ref[k, share(me, core)].astype(F32)
             for step in range(groups - 1):
                 total = total + wr2_ref[step, k].astype(F32)
@@ -653,28 +629,22 @@
             for step in range(parts - 1):
                 out_copy(step).start()
             bout_ref[:, part] = bo_ref[part]
+        if 1 <= slot < 5:
+            weights_cross(slot - 1)
         if slot < 4:
             weight_term(slot)
-            if slot == 3:
-                for index in range(groups):
-                    weights_out(index).start()
-        if slot == 4:
-            weights_cross()
-        if slot == 5:
+            for index in range(groups):
+                weights_out(slot, index).start()
+        if 1 <= slot < 5:
             for step in range(groups - 1):
-                weights_send(step).start()
+                weights_send(slot - 1, step).start()
         if slot - lines + 1 >= 0:
             close(slot - lines + 1)
     first_row = lax.broadcasted_iota(jnp.int32, small_ref.shape, 0) == 0
     mixer = jnp.broadcast_to(jnp.sum(mixer_ref[...], axis=0, keepdims=True), small_ref.shape)
     va_ref[0] = jnp.where(first_row, mixer, small_ref[...])
-    for q in range(chunks):
-        line.drain(q)
-    for step in range(parts - 1):
-        out_copy(step).wait()
     swap = mesh_copy(va_ref.at[0], va_ref.at[1], va_sem.at[0], va_sem.at[1], sibling)
     swap.start()
-    weights_finish()
     swap.wait()
     vb_ref[me] = va_ref[0] + va_ref[1]
 
@@ -705,6 +675,11 @@
         total = total + vc_ref[index]
     row_index = lax.broadcasted_iota(jnp.int32, total.shape, 0)
     vec_ref[...] = jnp.where(row_index < 2, total, v2_ref[...])
+    weights_finish()
+    for q in range(chunks):
+        line.drain(q)
+    for step in range(parts - 1):
+        out_copy(step).wait()
     for step, index in enumerate(others):
         group_copy(me, index, step).wait_send()
     for step, index in enumerate(line_others):
@@ -735,8 +710,8 @@
             pltpu.VMEM((groups, 8, model), F32),
             pltpu.VMEM((lines, 8, model), F32),
             pltpu.VMEM((8, model), F32),
-            pltpu.SemaphoreType.DMA((2, groups)),
-            pltpu.SemaphoreType.DMA((2, groups - 1)),
+            pltpu.SemaphoreType.DMA((2, 4, groups)),
+            pltpu.SemaphoreType.DMA((2, 4, groups - 1)),
             pltpu.SemaphoreType.DMA((2,)),
             pltpu.SemaphoreType.DMA((2, groups)),
             pltpu.SemaphoreType.DMA((2, lines)),
@@ -940,7 +915,7 @@
                 terms[p * tile + z * strip:p * tile + (z + 1) * strip])
 
 
-def line_turn(lines, chunks, summed, gathered, before, between):
+def line_turn(lines, chunks, summed, gathered, before, between, after=None):
     for slot in range(chunks + 2 * (lines - 1)):
         if slot < chunks:
             before(slot)
@@ -953,6 +928,8 @@
         for t in range(lines):
             if 0 <= q - t < chunks:
                 gathered.step(q - t, t)
+        if after is not None:
+            after(slot)
     for q in range(chunks):
         summed.drain(q)
         gathered.drain(q)
@@ -1039,15 +1016,40 @@
 
 def feed_close_kernel(dims, lines, chunks, gg_ref, gu_ref, wg_ref, wu_ref, rows_ref, grad_ref,
                       act_ref, hidden_ref, cot_ref, gain_ref,
-                      gh_ref, branch_ref, terms_ref, part_ref,
-                      own_ref, left_ref, right_ref, acc_ref, line_sem, gather_sem):
+                      gh_ref, branch_ref, pair_ref, part_ref,
+                      own_ref, left_ref, right_ref, acc_ref, line_sem, gather_sem,
+                      terms_ref, landed_ref, pair_sem):
     slots, parts, heads, tile, width, strip = dims
     per = slots // chunks
     model = cot_ref.shape[-1]
     units = act_ref.shape[-1]
     block, narrow = 256, 128
     place = lax.axis_index("head")
-    greet_line("head", lines)
+    part_index = lax.axis_index("ctx")
+    core = part_index % 2
+    sibling = {"ctx": part_index + 1 - 2 * core}
+    greet([sibling] + [{"head": lax.rem(place + step, lines)} for step in range(1, lines)])
+    groups, rows = pair_ref.shape[1:3]
+
+    def share(index, which):
+        return pl.ds(pl.multiple_of((index * 2 + which) * rows, 16), rows)
+
+    def pair_copy(kind, index):
+        return mesh_copy(terms_ref.at[kind, share(index, 1 - core)], landed_ref.at[kind, index],
+                         pair_sem.at[0, kind, index], pair_sem.at[1, kind, index], sibling)
+
+    def pair_sum(kind):
+        for index in range(groups):
+            pair_copy(kind, index).wait()
+
+        def add(index, carry):
+            pair_ref[kind, index] = (
+                terms_ref[kind, share(index, core)].astype(F32)
+                + landed_ref[kind, index].astype(F32)).astype(BF16)
+            return carry
+
+        lax.fori_loop(0, groups, add, 0)
+
     summed = LineSum("head", lines, own_ref, left_ref, right_ref, line_sem)
     gathered = LineGather(
         "head", lines, lambda q, s: branch_ref.at[pl.ds(q * per, per), s], gather_sem)
@@ -1081,6 +1083,8 @@
         lax.fori_loop(0, model // block, columns, 0)
         if q > 0:
             weight_term(q - 1)
+            for index in range(groups):
+                pair_copy(q - 1, index).start()
 
     def between(q):
         summed.total(q, acc_ref)
@@ -1098,10 +1102,14 @@
         for p in range(per):
             branch_ref[q * per + p, place] = low[p]
 
-    line_turn(lines, chunks, summed, gathered, before, between)
-
-
-def feed_close(dims, lines, chunks, *operands):
+    def after(slot):
+        if lines <= slot < lines + 3:
+            pair_sum(slot - lines)
+
+    line_turn(lines, chunks, summed, gathered, before, between, after)
+
+
+def feed_close(dims, groups, lines, chunks, *operands):
     slots, parts, heads, tile, width, strip = dims
     model, units = operands[8].shape[-1], operands[6].shape[-1]
     return pl.pallas_call(
@@ -1109,13 +1117,16 @@
         out_shape=(
             jax.ShapeDtypeStruct((slots, strip, model), F32),
             jax.ShapeDtypeStruct((slots, lines, strip, model), BF16),
-            jax.ShapeDtypeStruct((3, model, units), BF16),
+            jax.ShapeDtypeStruct((3, groups, model // groups // 2, units), BF16),
             jax.ShapeDtypeStruct((8, model), F32),
         ),
         in_specs=specs(10, 0),
         out_specs=specs(4, 0),
         scratch_shapes=line_scratch(chunks, lines, slots // chunks * strip, model) + [
             pltpu.SemaphoreType.DMA((2, 2, chunks, lines)),
+            pltpu.VMEM((3, model, units), BF16),
+            pltpu.VMEM((3, groups, model // groups // 2, units), BF16),
+            pltpu.SemaphoreType.DMA((2, 3, groups)),
         ],
         compiler_params=pltpu.CompilerParams(
             vmem_limit_bytes=60 << 20, collective_id=5, has_side_effects=True),
@@ -1222,7 +1233,7 @@
     grad_up = (grad_activ * silu_gate).astype(jnp.bfloat16)
     unit_shape = (slots, tile, activation.shape[-1])
     grad_hidden, branch_rows, wgrads, feed_part = feed_close(
-        dims, head_total, 4, grad_gate.reshape(unit_shape), grad_up.reshape(unit_shape),
+        dims, groups, head_total, 4, grad_gate.reshape(unit_shape), grad_up.reshape(unit_shape),
         gate_weight, up_weight, feed_rows.reshape(slots, tile, model_width), grad_rows,
         activation.reshape(unit_shape), hidden, cotangent_here, feed_gain.reshape(1, model_width))
     feed_part = jnp.sum(feed_part, axis=0)
@@ -1234,7 +1245,6 @@
     feed_sum = lax.psum_scatter(feed_terms, "head", scatter_dimension=1, tiled=True)
     grad_grouped = contract_cols(output_weight, branch_rows)
     shares = lax.axis_size("dp") * parts
-    wgrads = wgrads.reshape(3, groups, 2, model_width // shares, wgrads.shape[-1])
     grad_query, grad_key, grad_value, group_part, lambda_part, feed_sums = attend_back(
         dims, groups, lambda_head, queries, kv_all,
         grad_grouped, gain_col, mixed, second, lse, tables, wgrads)

time: 688 us -> 650 us (0.945)
  Pallas kernels: 577 us -> 540 us
    pallas_call x1, Pallas kernels: 139 us -> 119 us  [attend_back(): pl.pallas_call(partial(attend_back_kernel, dims, groups), out_shape=(rows...]
    pallas_call x1, Pallas kernels: 93.8 us -> 75.8 us  [finish(): pl.pallas_call(partial(finish_kernel, dims, groups, lines), out_shape=(ja...]
  transfers between devices with their start and end apart: 4 -> 4, of which waited for: 3 -> 3; matrix products, arithmetic and copies ran while one was open for 2% -> 3% of each run, Pallas kernels for 28% -> 26%
where the time goes in v6:
time: 650 us; the launch traced here: 643 us
  Pallas kernels  540 us (83%)
  local copies, waits for them, and re-layouts  23.2 us (4%)
  waiting for transfers between devices  21.9 us (3%)
  matrix products  21.6 us (3%)
  between operations  15 us (2%)
  other arithmetic  13.8 us (2%)
  starting transfers between devices  7.97 us (1%)
    pallas_call x1, Pallas kernels, attend_back(): pl.pallas_call(partial(attend_back_kernel, dims, groups), out_shape=(rows...  119 us
    pallas_call x1, Pallas kernels, feed_close(): pl.pallas_call(partial(feed_close_kernel, dims, lines, chunks), out_shape...  113 us
    pallas_call x1, Pallas kernels, feed_open(): pl.pallas_call(partial(feed_open_kernel, dims, lines, chunks), out_shape=...  102 us
    pallas_call x1, Pallas kernels, open_rows(): pl.pallas_call(partial(open_kernel, dims, lines, chunks), out_shape=(jax....  79.6 us
    pallas_call x1, Pallas kernels, finish(): pl.pallas_call(partial(finish_kernel, dims, groups, lines), out_shape=(ja...  75.8 us
    pallas_call x1, Pallas kernels, attend(): pl.pallas_call(partial(attend_kernel, dims), out_shape=(jax.ShapeDtypeStr...  49.7 us
  transfers between devices with their start and end apart: 4, of which 3 were waited for; matrix products, arithmetic and copies ran while one was open for 3% of the time, Pallas kernels for 26%

profile of v6, /device:TPU:0, one launch (start us, length us, event | category | flops | bytes accessed | tf_op | source)
XLA Modules:
  0.0 643.3 jit_solution(9755227570713277466)
XLA Ops:
  7.2 2.1 copy.52
  9.3 4.3 all-to-all-start
  17.9 7.2 %all-to-all-done = bf16[4,2,32,1536]{3,2,1,0:T(8,128)(2,1)S(1)} async-done(((bf16[4,2,32,1536]{3,2,1,0:T(8,128)(2,1)}), bf16[4,2,32,1536]{3,2,1,0:T(8,128)(2,1)S(1)}, u32[]{:S(2)}, u32[]{:S(2)}) %all-to-all-start) | async-done | bytes 786464 | tf_op jit(solution)/shard_map/all_to_all | solution.py:1196
  26.8 79.6 %open_rows.1 = (bf16[8,4,32,1536]{3,2,1,0:T(8,128)(2,1)}, bf16[8,128,384]{2,1,0:T(8,128)(2,1)}, bf16[4,8,2,128,384]{4,3,2,1,0:T(8,128)(2,1)}, bf16[4,2,32,1536]{3,2,1,0:T(8,128)(2,1)}) custom-call(bf16[8,32,1536]{2,1,0:T(8,128)(2,1)} %broadcast_select_fusion.3.x_ref.inputs_ref, f32[1,1536]{1,0:T(1,128)} %reshape.205.gain_ref, bf16[1536,384]{1,0:T(8,128)(2,1)} %wq_ref.3, ...), custom_call_target="tpu_custom_call" | custom-call | flops 4000000000 | bytes 16000000 | tf_op jit(solution)/shard_map/open_rows/pallas_call | solution.py:880
  106.4 1.8 gather_fusion.1
  110.6 1.2 multiply_sine_fusion
  111.8 49.7 %attend.1 = (bf16[8,128,384]{2,1,0:T(8,128)(2,1)S(1)}, f32[8,3,128,128]{3,2,1,0:T(8,128)S(1)}, f32[8,3,128,128]{3,2,1,0:T(8,128)S(1)}, f32[8,3,1,256]{3,2,1,0:T(1,128)S(1)}) custom-call(s32[1]{0:T(128)} %bitcast.part_ref, f32[3]{0:T(128)S(1)} %subtract_add_fusion.lam_ref, bf16[8,128,384]{2,1,0:T(8,128)(2,1)S(1)} %copy-done.3, ...), custom_call_target="tpu_custom_call" | custom-call | flops 20000000000 | bytes 12000000 | tf_op jit(solution)/shard_map/attend/pallas_call | solution.py:363
  165.4 6.7 %all-gather.2.cloned.1.call-done.grad_ref = bf16[8,128,1536]{2,1,0:T(8,128)(2,1)} async-done(((bf16[8,32,1536]{2,1,0:T(8,128)(2,1)}), bf16[8,128,1536]{2,1,0:T(8,128)(2,1)}) %all-gather.2.cloned.1.call-update) | async-done | bytes 3145744 | tf_op jit(solution)/shard_map/all_gather | solution.py:1213
  172.1 102.4 %feed_open.1 = (f32[8,32,1536]{2,1,0:T(8,128)}, bf16[8,4,32,1536]{3,2,1,0:T(8,128)(2,1)}, f32[8,128,1024]{2,1,0:T(8,128)}) custom-call(bf16[8,128,384]{2,1,0:T(8,128)(2,1)} %copy-done.2, bf16[384,1536]{1,0:T(8,128)(2,1)} %wo_ref.1, bf16[8,32,1536]{2,1,0:T(8,128)(2,1)} %broadcast_select_fusion.3.x_ref.inputs_ref, f32[1,1536]{1,0:T(1,128)} %reshape.209.gain_ref, ...), custom_call_target="tpu_custom_call" | custom-call | flops 4000000000 | bytes 20000000 | tf_op jit(solution)/shard_map/feed_open/pallas_call | solution.py:997
  274.5 5.4 fusion.10
  280.0 7.0 %multiply_convert_fusion = (bf16[1024,1024]{1,0:T(8,128)(2,1)S(1)}, bf16[1024,1024]{1,0:T(8,128)(2,1)}, bf16[1024,1024]{1,0:T(8,128)(2,1)}) fusion(f32[1024,1024]{1,0:T(8,128)S(1)} %fusion.10, f32[8,128,1024]{2,1,0:T(8,128)S(1)} %copy-done.25, bf16[1024,1536]{1,0:T(8,128)(2,1)S(1)} %bitcast.89, bf16[1536,1024]{1,0:T(8,128)(2,1)S(1)} %copy-done.20), kind=kOutput, calls=%fused_computation.10 | convolution fusion | flops 3236954112 | bytes 20971520 | tf_op jit(solution)/shard_map/dot_general | solution.py:1226
  287.0 4.8 convolution_convert_fusion
  291.8 113.0 %feed_close.1 = (f32[8,32,1536]{2,1,0:T(8,128)}, bf16[8,4,32,1536]{3,2,1,0:T(8,128)(2,1)}, bf16[3,4,192,1024]{3,2,1,0:T(8,128)(2,1)}, f32[8,1536]{1,0:T(8,128)}) custom-call(bf16[8,128,1024]{2,1,0:T(8,128)(2,1)} %bitcast.91, bf16[8,128,1024]{2,1,0:T(8,128)(2,1)} %bitcast.92, bf16[1536,1024]{1,0:T(8,128)(2,1)} %wg_ref.1, bf16[1536,1024]{1,0:T(8,128)(2,1)} %wu_ref.1, ...), custom_call_target="tpu_custom_call" | custom-call | flops 16000000000 | bytes 40000000 | tf_op jit(solution)/shard_map/feed_close/pallas_call | solution.py:1115
  404.8 4.4 convolution_bitcast_fusion.gg_ref
  409.3 119.2 %attend_back.1 = (bf16[8,128,384]{2,1,0:T(8,128)(2,1)}, bf16[8,128,384]{2,1,0:T(8,128)(2,1)}, bf16[8,128,384]{2,1,0:T(8,128)(2,1)}, f32[384,128]{1,0:T(8,128)}, ...) custom-call(f32[3]{0:T(128)} %copy-done.1, bf16[8,128,384]{2,1,0:T(8,128)(2,1)} %get-tuple-element.50.q_ref, ...), custom_call_target="tpu_custom_call" | custom-call | flops 60000002048 | bytes 24000000 | tf_op jit(solution)/shard_map/attend_back/pallas_call | solution.py:392
  531.5 3.1 slice_bitcast_fusion
  534.6 1.4 add_convert_fusion
  537.6 75.8 %finish.1 = (bf16[8,32,1536]{2,1,0:T(8,128)(2,1)}, f32[4,192,384]{2,1,0:T(8,128)}, f32[8,1536]{1,0:T(8,128)}, bf16[2,4,32,1536]{3,2,1,0:T(8,128)(2,1)}) custom-call(bf16[8,128,384]{2,1,0:T(8,128)(2,1)} %get-tuple-element.67.gq_ref, bf16[8,128,384]{2,1,0:T(8,128)(2,1)} %get-tuple-element.68.gk_ref, bf16[8,128,384]{2,1,0:T(8,128)(2,1)} %get-tuple-element.69.gv_ref, ...), custom_call_target="tpu_custom_call" | custom-call | flops 8000000000 | bytes 24000000 | tf_op jit(solution)/shard_map/finish/pallas_call | solution.py:694
  613.5 1.6 slice_reduce_fusion
  615.7 1.7 gather_fusion.3
  618.5 3.5 all-to-all-start.1
  622.6 1.3 slice_reduce_fusion.2
  625.6 8.0 %all-to-all-done.1 = bf16[4,2,32,1536]{3,2,1,0:T(8,128)(2,1)S(1)} async-done(((bf16[4,2,32,1536]{3,2,1,0:T(8,128)(2,1)}), bf16[4,2,32,1536]{3,2,1,0:T(8,128)(2,1)S(1)}, u32[]{:S(2)}, u32[]{:S(2)}) %all-to-all-start.1) | async-done | bytes 786464 | tf_op jit(solution)/shard_map/all_to_all | solution.py:1201
  633.7 1.3 copy.60
  (103 shorter events, 21.8 us)
Async XLA Ops:
  7.2 6.4 copy-start.22
  7.2 9.3 %copy-start.11 = (f32[1536]{0:T(1024)S(1)}, f32[1536]{0:T(1024)}, u32[]{:S(2)}) copy-start(f32[1536]{0:T(1024)} %param.21) | copy-start | bytes 18436
  9.3 15.9 %all-to-all-start = ((bf16[4,2,32,1536]{3,2,1,0:T(8,128)(2,1)}), bf16[4,2,32,1536]{3,2,1,0:T(8,128)(2,1)S(1)}, u32[]{:S(2)}, u32[]{:S(2)}) async-start(bf16[4,2,32,1536]{3,2,1,0:T(8,128)(2,1)} %copy.52), calls=%async_computation | async-start | bytes 1572864 | tf_op jit(solution)/shard_map/all_to_all | solution.py:1196
  13.5 158.6 %all-gather.2.cloned.1.call-start = ((), (), s32[]{:S(2)}) async-start(), calls=%async_computation.3 | async-start | bytes 3932160 | tf_op jit(solution)/shard_map/all_gather | solution.py:1213
  106.4 3.9 copy-start.13
  106.4 3.9 copy-start.14
  106.4 3.9 copy-start.15
  106.4 3.9 copy-start.16
  106.4 5.4 copy-start.3
  109.3 425.3 %reduce-scatter.2.cloned.1.call-start = ((), (), s32[]{:S(2)}) async-start(), calls=%async_computation.4 | async-start | bytes 3932160 | tf_op jit(solution)/shard_map/reduce_scatter | solution.py:1245
  109.7 51.9 %copy-start = (f32[384,1]{1,0:T(8,128)}, f32[384,1]{1,0:T(8,128)S(1)}, u32[]{:S(2)}) copy-start(f32[384,1]{1,0:T(8,128)S(1)} %reshape.266.gain_ref) | copy-start | bytes 4612
  110.5 51.0 %copy-start.1 = (f32[3]{0:T(128)}, f32[3]{0:T(128)S(1)}, u32[]{:S(2)}) copy-start(f32[3]{0:T(128)S(1)} %subtract_add_fusion.lam_ref) | copy-start | bytes 40
  172.1 102.4 %copy-start.19 = (bf16[1536,1024]{1,0:T(8,128)(2,1)S(1)}, bf16[1536,1024]{1,0:T(8,128)(2,1)}, u32[]{:S(2)}) copy-start(bf16[1536,1024]{1,0:T(8,128)(2,1)} %wg_ref.1) | copy-start | bytes 9437188
  274.5 5.5 copy-start.20
  274.5 5.5 copy-start.23
  274.5 5.5 copy-start.25
  280.0 7.0 %copy-start.18 = (bf16[1024,1536]{1,0:T(8,128)(2,1)S(1)}, bf16[1024,1536]{1,0:T(8,128)(2,1)}, u32[]{:S(2)}) copy-start(bf16[1024,1536]{1,0:T(8,128)(2,1)} %down_ref.1) | copy-start | bytes 9437188
  287.0 4.8 copy-start.24
  291.8 113.0 %copy-start.21 = (bf16[384,1536]{1,0:T(8,128)(2,1)S(1)}, bf16[384,1536]{1,0:T(8,128)(2,1)}, u32[]{:S(2)}) copy-start(bf16[384,1536]{1,0:T(8,128)(2,1)} %wo_ref.1) | copy-start | bytes 3538948
  409.3 121.5 %copy-start.10 = (f32[8,1536]{1,0:T(8,128)S(1)}, f32[8,1536]{1,0:T(8,128)}, u32[]{:S(2)}) copy-start(f32[8,1536]{1,0:T(8,128)} %get-tuple-element.72) | copy-start | bytes 147460
  528.5 6.1 copy-start.7
  613.4 11.1 %copy-start.8 = (f32[4,192,384]{2,1,0:T(8,128)S(1)}, f32[4,192,384]{2,1,0:T(8,128)}, u32[]{:S(2)}) copy-start(f32[4,192,384]{2,1,0:T(8,128)} %get-tuple-element.79) | copy-start | bytes 3538948
  618.5 15.1 %all-to-all-start.1 = ((bf16[4,2,32,1536]{3,2,1,0:T(8,128)(2,1)}), bf16[4,2,32,1536]{3,2,1,0:T(8,128)(2,1)S(1)}, u32[]{:S(2)}, u32[]{:S(2)}) async-start(bf16[4,2,32,1536]{3,2,1,0:T(8,128)(2,1)} %bitcast.22), calls=%async_computation.2 | async-start | bytes 1572864 | tf_op jit(solution)/shard_map/all_to_all | solution.py:1201
  625.6 9.4 %copy-start.9 = (bf16[2,4,32,1536]{3,2,1,0:T(8,128)(2,1)S(1)}, bf16[2,4,32,1536]{3,2,1,0:T(8,128)(2,1)}, u32[]{:S(2)}) copy-start(bf16[2,4,32,1536]{3,2,1,0:T(8,128)(2,1)} %get-tuple-element.76) | copy-start | bytes 2359300
  (6 other events, 10.3 us)
Sparse Core Ops, SparseCore 0:
  109.4 62.6 all-gather.1
  409.4 58.7 reduce-scatter.1

commit v7 on v6

--- a/solution.py
+++ b/solution.py
@@ -234,6 +234,8 @@
     lpart_ref[...] = jnp.zeros_like(lpart_ref)
     query_off = offsets_of(part, parts, strip, 1, (1, tile))
     query_off = jnp.concatenate([query_off, query_off], axis=1)
+    key_off = jnp.concatenate(
+        [offsets_of(c, parts, strip, 0, (tile, 1)) for c in range(parts)], axis=0)
 
     def prepare(place, carry):
         for h in range(heads):
@@ -270,26 +272,23 @@
             lse = lse_ref[place, h]
             delta = delta_ref[place, h]
             lanes = slice(h * width, (h + 1) * width)
-            turned = []
-            for c in range(parts):
-                keys = kv_ref[c, slot, 0, :, lanes]
-                s = dot(keys, qbdt_ref[place, h])
-                if diag:
-                    key_off = offsets_of(c, parts, strip, 0, (tile, 1))
-                    s = jnp.where(key_off <= query_off, s, NEGATIVE)
-                weights = jnp.exp(s - lse)
-                probs = dot(kv_ref[c, slot, 1, :, lanes], gt_ref[place, h])
-                ds = (weights * (probs - delta)).astype(BF16)
-                dv = dot(weights.astype(BF16), g_ref[place, h])
-                dk = dot(ds, qbd_ref[place, h])
-                if diag:
-                    dva_ref[h, c] = dv
-                    dka_ref[h, c] = dk
-                else:
-                    dva_ref[h, c] += dv
-                    dka_ref[h, c] += dk
-                turned.append(ds)
-            dq = dot(kt_ref[h], jnp.concatenate(turned, axis=0))
+            keys = kv_ref[:, slot, 0, :, lanes].reshape(parts * tile, width)
+            values = kv_ref[:, slot, 1, :, lanes].reshape(parts * tile, width)
+            s = dot(keys, qbdt_ref[place, h])
+            if diag:
+                s = jnp.where(key_off <= query_off, s, NEGATIVE)
+            weights = jnp.exp(s - lse)
+            probs = dot(values, gt_ref[place, h])
+            ds = (weights * (probs - delta)).astype(BF16)
+            dv = dot(weights.astype(BF16), g_ref[place, h]).reshape(parts, tile, width)
+            dk = dot(ds, qbd_ref[place, h]).reshape(parts, tile, width)
+            if diag:
+                dva_ref[h] = dv
+                dka_ref[h] = dk
+            else:
+                dva_ref[h] += dv
+                dka_ref[h] += dk
+            dq = dot(kt_ref[h], ds)
             dqt_ref[place, h, :half] += dq[:half, :tile]
             dqt_ref[place, h, half:] += dq[half:, tile:]
 
@@ -981,14 +980,11 @@
 
         lax.fori_loop(0, units // block, columns, 0)
 
-    def before_all(q):
-        before(q)
-        if q > 0:
-            extra(q - 1)
-        if q == chunks - 1:
-            extra(q)
-
-    line_turn(lines, chunks, summed, gathered, before_all, between)
+    def after(slot):
+        if slot < chunks:
+            extra(slot)
+
+    line_turn(lines, chunks, summed, gathered, before, between, after)
 
 
 def feed_open(dims, lines, chunks, *operands):
@@ -1081,10 +1077,6 @@
             return carry
 
         lax.fori_loop(0, model // block, columns, 0)
-        if q > 0:
-            weight_term(q - 1)
-            for index in range(groups):
-                pair_copy(q - 1, index).start()
 
     def between(q):
         summed.total(q, acc_ref)
@@ -1103,6 +1095,10 @@
             branch_ref[q * per + p, place] = low[p]
 
     def after(slot):
+        if slot < 3:
+            weight_term(slot)
+            for index in range(groups):
+                pair_copy(slot, index).start()
         if lines <= slot < lines + 3:
             pair_sum(slot - lines)
 
@@ -1194,10 +1190,10 @@
     def spread(rows):
         cut = rows.reshape(pair_count, parts, strip, model_width).transpose(1, 0, 2, 3)
         cut = lax.all_to_all(cut, "ctx", 0, 0, tiled=True)
-        return jnp.take(cut.reshape(slots, strip, model_width), slot_of, axis=0)
+        return jnp.take(cut.reshape(slots, strip, model_width), slot_of, axis=0, mode="clip")
 
     def unspread(rows):
-        cut = jnp.take(rows, order, axis=0).reshape(parts, pair_count, strip, model_width)
+        cut = jnp.take(rows, order, axis=0, mode="clip").reshape(parts, pair_count, strip, model_width)
         cut = lax.all_to_all(cut, "ctx", 0, 0, tiled=True)
         return cut.transpose(1, 0, 2, 3).reshape(1, pair_count, short_rows, model_width)
 
@@ -1206,10 +1202,10 @@
     part_shape = (slots, tile, qwidth)
     cut_shape = (pair_count, parts, strip, model_width)
     normed_rows, queries, kv_all, cotangent_slots = open_rows(
-        dims, head_total, 4, inputs_here, mixer_gain.reshape(1, model_width), query_weight,
+        dims, head_total, 8, inputs_here, mixer_gain.reshape(1, model_width), query_weight,
         key_weight, value_weight, cos_rows, sin_rows, cotangent.reshape(cut_shape))
     cotangent_here = jnp.take(
-        cotangent_slots.reshape(slots, strip, model_width), slot_of, axis=0)
+        cotangent_slots.reshape(slots, strip, model_width), slot_of, axis=0, mode="clip")
     grad_rows = lax.all_gather(cotangent_here, "head", axis=1, tiled=True)
     part_arr = part.reshape(1).astype(jnp.int32)
     gain_col = group_gain.reshape(qwidth, 1)
@@ -1218,7 +1214,7 @@
         gain_col)
     grouped, grad_rows = lax.optimization_barrier((grouped, grad_rows))
     hidden, feed_rows, grad_activ = feed_open(
-        dims, head_total, 4, grouped, output_weight, inputs_here,
+        dims, head_total, 8, grouped, output_weight, inputs_here,
         feed_gain.reshape(1, model_width), grad_rows, down_weight)
     feed_rows = feed_rows.reshape(row_count, model_width)
     grad_activ = grad_activ.reshape(row_count, grad_activ.shape[-1])
@@ -1256,7 +1252,7 @@
         jnp.concatenate([group_part, lambda_part]), (0, model_width - qwidth - heads_here))
     small = jnp.pad(jnp.stack([jnp.zeros_like(feed_part), feed_part, third]), ((0, 5), (0, 0)))
     grad_rows_shape = (slots, tile, model_width)
-    block_slots = jnp.take(block_out, order, axis=0).reshape(
+    block_slots = jnp.take(block_out, order, axis=0, mode="clip").reshape(
         parts, pair_count, strip, model_width)
     input_grad, attn_sums, vectors, block_out = finish(
         dims, groups, head_total, 4, model_width // shares, grad_query, grad_key, grad_value,

time: 650 us -> 626 us (0.963)
  Pallas kernels: 540 us -> 516 us
    pallas_call x1, Pallas kernels: 119 us -> 105 us  [attend_back(): pl.pallas_call(partial(attend_back_kernel, dims, groups), out_shape=(rows...]
    pallas_call x1, Pallas kernels: 102 us -> 95.4 us  [feed_open(): pl.pallas_call(partial(feed_open_kernel, dims, lines, chunks), out_shape=...]
  transfers between devices with their start and end apart: 4 -> 4, of which waited for: 3 -> 3; matrix products, arithmetic and copies ran while one was open for 3% -> 3% of each run, Pallas kernels for 26% -> 25%
where the time goes in v7:
time: 626 us; the launch traced here: 618 us
  Pallas kernels  516 us (82%)
  local copies, waits for them, and re-layouts  27.7 us (4%)
  matrix products  21.6 us (3%)
  waiting for transfers between devices  20.2 us (3%)
  between operations  14.9 us (2%)
  other arithmetic  9.66 us (2%)
  starting transfers between devices  7.97 us (1%)
    pallas_call x1, Pallas kernels, feed_close(): pl.pallas_call(partial(feed_close_kernel, dims, lines, chunks), out_shape...  113 us
    pallas_call x1, Pallas kernels, attend_back(): pl.pallas_call(partial(attend_back_kernel, dims, groups), out_shape=(rows...  105 us
    pallas_call x1, Pallas kernels, feed_open(): pl.pallas_call(partial(feed_open_kernel, dims, lines, chunks), out_shape=...  95.4 us
    pallas_call x1, Pallas kernels, finish(): pl.pallas_call(partial(finish_kernel, dims, groups, lines), out_shape=(ja...  78.5 us
    pallas_call x1, Pallas kernels, open_rows(): pl.pallas_call(partial(open_kernel, dims, lines, chunks), out_shape=(jax....  74.4 us
    pallas_call x1, Pallas kernels, attend(): pl.pallas_call(partial(attend_kernel, dims), out_shape=(jax.ShapeDtypeStr...  50 us
  transfers between devices with their start and end apart: 4, of which 3 were waited for; matrix products, arithmetic and copies ran while one was open for 3% of the time, Pallas kernels for 25%

profile of v7, /device:TPU:0, one launch (start us, length us, event | category | flops | bytes accessed | tf_op | source)
XLA Modules:
  0.0 617.8 jit_solution(16228255777559196118)
XLA Ops:
  7.2 2.1 copy.52
  9.3 4.3 all-to-all-start
  17.9 7.2 %all-to-all-done = bf16[4,2,32,1536]{3,2,1,0:T(8,128)(2,1)S(1)} async-done(((bf16[4,2,32,1536]{3,2,1,0:T(8,128)(2,1)}), bf16[4,2,32,1536]{3,2,1,0:T(8,128)(2,1)S(1)}, u32[]{:S(2)}, u32[]{:S(2)}) %all-to-all-start) | async-done | bytes 786464 | tf_op jit(solution)/shard_map/all_to_all | solution.py:1192
  25.2 1.5 gather_fusion
  26.7 74.4 %open_rows.1 = (bf16[8,4,32,1536]{3,2,1,0:T(8,128)(2,1)}, bf16[8,128,384]{2,1,0:T(8,128)(2,1)}, bf16[4,8,2,128,384]{4,3,2,1,0:T(8,128)(2,1)}, bf16[4,2,32,1536]{3,2,1,0:T(8,128)(2,1)}) custom-call(bf16[8,32,1536]{2,1,0:T(8,128)(2,1)} %gather_fusion, f32[1,1536]{1,0:T(1,128)} %reshape.201.gain_ref, bf16[1536,384]{1,0:T(8,128)(2,1)} %wq_ref.3, ...), custom_call_target="tpu_custom_call" | custom-call | flops 4000000000 | bytes 16000000 | tf_op jit(solution)/shard_map/open_rows/pallas_call | solution.py:879
  101.1 2.6 gather_fusion.1
  107.3 50.0 %attend.1 = (bf16[8,128,384]{2,1,0:T(8,128)(2,1)S(1)}, f32[8,3,128,128]{3,2,1,0:T(8,128)S(1)}, f32[8,3,128,128]{3,2,1,0:T(8,128)S(1)}, f32[8,3,1,256]{3,2,1,0:T(1,128)S(1)}) custom-call(s32[1]{0:T(128)} %bitcast.part_ref, f32[3]{0:T(128)S(1)} %subtract_add_fusion.lam_ref, bf16[8,128,384]{2,1,0:T(8,128)(2,1)S(1)} %copy-done.3, ...), custom_call_target="tpu_custom_call" | custom-call | flops 20000000000 | bytes 12000000 | tf_op jit(solution)/shard_map/attend/pallas_call | solution.py:362
  161.2 4.9 all-gather.3.cloned.1.call-done.grad_ref
  166.1 95.4 %feed_open.1 = (f32[8,32,1536]{2,1,0:T(8,128)}, bf16[8,4,32,1536]{3,2,1,0:T(8,128)(2,1)}, f32[8,128,1024]{2,1,0:T(8,128)}) custom-call(bf16[8,128,384]{2,1,0:T(8,128)(2,1)} %copy-done.2, bf16[384,1536]{1,0:T(8,128)(2,1)} %wo_ref.1, bf16[8,32,1536]{2,1,0:T(8,128)(2,1)} %gather_fusion, f32[1,1536]{1,0:T(1,128)} %reshape.205.gain_ref, ...), custom_call_target="tpu_custom_call" | custom-call | flops 4000000000 | bytes 20000000 | tf_op jit(solution)/shard_map/feed_open/pallas_call | solution.py:993
  261.6 5.4 fusion.10
  267.1 7.0 %multiply_convert_fusion = (bf16[1024,1024]{1,0:T(8,128)(2,1)S(1)}, bf16[1024,1024]{1,0:T(8,128)(2,1)}, bf16[1024,1024]{1,0:T(8,128)(2,1)}) fusion(f32[1024,1024]{1,0:T(8,128)S(1)} %fusion.10, f32[8,128,1024]{2,1,0:T(8,128)S(1)} %copy-done.25, bf16[1024,1536]{1,0:T(8,128)(2,1)S(1)} %bitcast.87, bf16[1536,1024]{1,0:T(8,128)(2,1)S(1)} %copy-done.21), kind=kOutput, calls=%fused_computation.10 | convolution fusion | flops 3236954112 | bytes 20971520 | tf_op jit(solution)/shard_map/dot_general | solution.py:1222
  274.0 4.8 convolution_convert_fusion
  278.8 112.6 %feed_close.1 = (f32[8,32,1536]{2,1,0:T(8,128)}, bf16[8,4,32,1536]{3,2,1,0:T(8,128)(2,1)}, bf16[3,4,192,1024]{3,2,1,0:T(8,128)(2,1)}, f32[8,1536]{1,0:T(8,128)}) custom-call(bf16[8,128,1024]{2,1,0:T(8,128)(2,1)} %bitcast.89, bf16[8,128,1024]{2,1,0:T(8,128)(2,1)} %bitcast.90, bf16[1536,1024]{1,0:T(8,128)(2,1)} %wg_ref.1, bf16[1536,1024]{1,0:T(8,128)(2,1)} %wu_ref.1, ...), custom_call_target="tpu_custom_call" | custom-call | flops 16000000000 | bytes 40000000 | tf_op jit(solution)/shard_map/feed_close/pallas_call | solution.py:1111
  391.5 4.4 convolution_bitcast_fusion.gg_ref
  395.9 104.8 %attend_back.1 = (bf16[8,128,384]{2,1,0:T(8,128)(2,1)}, bf16[8,128,384]{2,1,0:T(8,128)(2,1)}, bf16[8,128,384]{2,1,0:T(8,128)(2,1)}, f32[384,128]{1,0:T(8,128)}, ...) custom-call(f32[3]{0:T(128)} %copy-done.1, bf16[8,128,384]{2,1,0:T(8,128)(2,1)} %get-tuple-element.49.q_ref, ...), custom_call_target="tpu_custom_call" | custom-call | flops 60000002048 | bytes 24000000 | tf_op jit(solution)/shard_map/attend_back/pallas_call | solution.py:391
  503.8 3.1 slice_bitcast_fusion
  506.9 1.3 add_convert_fusion
  508.2 1.5 gather_fusion.2
  509.7 78.5 %finish.1 = (bf16[8,32,1536]{2,1,0:T(8,128)(2,1)}, f32[4,192,384]{2,1,0:T(8,128)}, f32[8,1536]{1,0:T(8,128)}, bf16[2,4,32,1536]{3,2,1,0:T(8,128)(2,1)}) custom-call(bf16[8,128,384]{2,1,0:T(8,128)(2,1)} %get-tuple-element.66.gq_ref, bf16[8,128,384]{2,1,0:T(8,128)(2,1)} %get-tuple-element.67.gk_ref, bf16[8,128,384]{2,1,0:T(8,128)(2,1)} %get-tuple-element.68.gv_ref, ...), custom_call_target="tpu_custom_call" | custom-call | flops 8000000000 | bytes 24000000 | tf_op jit(solution)/shard_map/finish/pallas_call | solution.py:693
  588.2 1.6 slice_reduce_fusion
  590.5 2.6 gather_fusion.3
  593.1 3.5 all-to-all-start.1
  600.2 8.0 %all-to-all-done.1 = bf16[4,2,32,1536]{3,2,1,0:T(8,128)(2,1)S(1)} async-done(((bf16[4,2,32,1536]{3,2,1,0:T(8,128)(2,1)}), bf16[4,2,32,1536]{3,2,1,0:T(8,128)(2,1)S(1)}, u32[]{:S(2)}, u32[]{:S(2)}) %all-to-all-start.1) | async-done | bytes 786464 | tf_op jit(solution)/shard_map/all_to_all | solution.py:1197
  608.4 1.3 copy.60
  (95 shorter events, 20.1 us)
Async XLA Ops:
  7.2 8.3 %copy-start.11 = (f32[1536]{0:T(1024)S(1)}, f32[1536]{0:T(1024)}, u32[]{:S(2)}) copy-start(f32[1536]{0:T(1024)} %param.19) | copy-start | bytes 18436
  7.2 8.9 %copy-start.18 = (s32[1,8]{1,0:T(1,128)S(1)}, s32[1,8]{1,0:T(1,128)}, u32[]{:S(2)}) copy-start(s32[1,8]{1,0:T(1,128)} %param.18) | copy-start | bytes 100
  9.3 15.9 %all-to-all-start = ((bf16[4,2,32,1536]{3,2,1,0:T(8,128)(2,1)}), bf16[4,2,32,1536]{3,2,1,0:T(8,128)(2,1)S(1)}, u32[]{:S(2)}, u32[]{:S(2)}) async-start(bf16[4,2,32,1536]{3,2,1,0:T(8,128)(2,1)} %copy.52), calls=%async_computation | async-start | bytes 1572864 | tf_op jit(solution)/shard_map/all_to_all | solution.py:1192
  13.5 152.6 %all-gather.3.cloned.1.call-start = ((), (), s32[]{:S(2)}) async-start(), calls=%async_computation.4 | async-start | bytes 3932160 | tf_op jit(solution)/shard_map/all_gather | solution.py:1209
  26.6 77.3 %copy-start.17 = (f32[384]{0:T(512)S(1)}, f32[384]{0:T(512)}, u32[]{:S(2)}) copy-start(f32[384]{0:T(512)} %param.27) | copy-start | bytes 4612
  26.6 77.4 %copy-start.12 = (f32[1536]{0:T(1024)S(1)}, f32[1536]{0:T(1024)}, u32[]{:S(2)}) copy-start(f32[1536]{0:T(1024)} %param.29) | copy-start | bytes 18436
  26.6 78.1 %copy-start.13 = (f32[3,64]{1,0:T(4,128)S(1)}, f32[3,64]{1,0:T(4,128)}, u32[]{:S(2)}) copy-start(f32[3,64]{1,0:T(4,128)} %param.23) | copy-start | bytes 2308
  26.6 78.1 %copy-start.14 = (f32[3,64]{1,0:T(4,128)S(1)}, f32[3,64]{1,0:T(4,128)}, u32[]{:S(2)}) copy-start(f32[3,64]{1,0:T(4,128)} %param.24) | copy-start | bytes 2308
  26.6 78.1 %copy-start.15 = (f32[3,64]{1,0:T(4,128)S(1)}, f32[3,64]{1,0:T(4,128)}, u32[]{:S(2)}) copy-start(f32[3,64]{1,0:T(4,128)} %param.25) | copy-start | bytes 2308
  26.7 78.1 %copy-start.16 = (f32[3,64]{1,0:T(4,128)S(1)}, f32[3,64]{1,0:T(4,128)}, u32[]{:S(2)}) copy-start(f32[3,64]{1,0:T(4,128)} %param.26) | copy-start | bytes 2308
  103.7 403.2 %reduce-scatter.2.cloned.1.call-start = ((), (), s32[]{:S(2)}) async-start(), calls=%async_computation.3 | async-start | bytes 3932160 | tf_op jit(solution)/shard_map/reduce_scatter | solution.py:1241
  104.1 53.2 %copy-start = (f32[384,1]{1,0:T(8,128)}, f32[384,1]{1,0:T(8,128)S(1)}, u32[]{:S(2)}) copy-start(f32[384,1]{1,0:T(8,128)S(1)} %reshape.255.gain_ref) | copy-start | bytes 4612
  105.0 52.4 %copy-start.1 = (f32[3]{0:T(128)}, f32[3]{0:T(128)S(1)}, u32[]{:S(2)}) copy-start(f32[3]{0:T(128)S(1)} %subtract_add_fusion.lam_ref) | copy-start | bytes 40
  166.1 95.4 %copy-start.20 = (bf16[1536,1024]{1,0:T(8,128)(2,1)S(1)}, bf16[1536,1024]{1,0:T(8,128)(2,1)}, u32[]{:S(2)}) copy-start(bf16[1536,1024]{1,0:T(8,128)(2,1)} %wg_ref.1) | copy-start | bytes 9437188
  261.5 5.5 copy-start.21
  261.5 5.5 copy-start.23
  261.5 5.5 copy-start.25
  267.0 7.0 %copy-start.19 = (bf16[1024,1536]{1,0:T(8,128)(2,1)S(1)}, bf16[1024,1536]{1,0:T(8,128)(2,1)}, u32[]{:S(2)}) copy-start(bf16[1024,1536]{1,0:T(8,128)(2,1)} %down_ref.1) | copy-start | bytes 9437188
  278.8 112.6 %copy-start.22 = (bf16[384,1536]{1,0:T(8,128)(2,1)S(1)}, bf16[384,1536]{1,0:T(8,128)(2,1)}, u32[]{:S(2)}) copy-start(bf16[384,1536]{1,0:T(8,128)(2,1)} %wo_ref.1) | copy-start | bytes 3538948
  395.9 107.1 %copy-start.10 = (f32[8,1536]{1,0:T(8,128)S(1)}, f32[8,1536]{1,0:T(8,128)}, u32[]{:S(2)}) copy-start(f32[8,1536]{1,0:T(8,128)} %get-tuple-element.71) | copy-start | bytes 147460
  500.8 6.1 copy-start.7
  588.2 11.0 %copy-start.8 = (f32[4,192,384]{2,1,0:T(8,128)S(1)}, f32[4,192,384]{2,1,0:T(8,128)}, u32[]{:S(2)}) copy-start(f32[4,192,384]{2,1,0:T(8,128)} %get-tuple-element.78) | copy-start | bytes 3538948
  593.1 15.1 %all-to-all-start.1 = ((bf16[4,2,32,1536]{3,2,1,0:T(8,128)(2,1)}), bf16[4,2,32,1536]{3,2,1,0:T(8,128)(2,1)S(1)}, u32[]{:S(2)}, u32[]{:S(2)}) async-start(bf16[4,2,32,1536]{3,2,1,0:T(8,128)(2,1)} %bitcast.22), calls=%async_computation.2 | async-start | bytes 1572864 | tf_op jit(solution)/shard_map/all_to_all | solution.py:1197
  600.2 9.4 %copy-start.9 = (bf16[2,4,32,1536]{3,2,1,0:T(8,128)(2,1)S(1)}, bf16[2,4,32,1536]{3,2,1,0:T(8,128)(2,1)}, u32[]{:S(2)}) copy-start(bf16[2,4,32,1536]{3,2,1,0:T(8,128)(2,1)} %get-tuple-element.75) | copy-start | bytes 2359300
  (6 other events, 9.8 us)
Sparse Core Ops, SparseCore 0:
  103.9 62.1 all-gather.2
  396.1 59.4 reduce-scatter.1
